TPU v7x, 512 devices: a whole 4x8x8 slice. The times are simulated.
512 devices in a mesh: mode: 8 (over x, core), slab: 64 (over z, y).
Axes of the slice: x: 4, y: 8, z: 8, core: 2. Of those that a mesh axis runs over, the one named last changes fastest.
Arguments:
- log_cond: float32 [256, 128, 128], P('slab'), may hold values from -1 to 1
- head_slope: float32 [256, 128, 128], P('slab'), may hold values from -6 to 6
- modes: bfloat16 [64, 256, 128, 128], P('mode', 'slab'), may hold values from -6 to 6
- obs_cells: int32 [65536], P('slab'), may hold values from 0 to 65535
- obs_var: float32 [65536], P('slab'), may hold values from 0.2 to 2
- misfit: float32 [65536, 16], P('slab'), may hold values from -24 to 24
- base_fields: bfloat16 [16, 256, 128, 128], P(None, 'slab', 'mode'), may hold values from -6 to 6
Outputs:
- fields: float32 [16, 256, 128, 128], P(None, 'slab', 'mode')
Inputs may be any that keep to these rules, and one draw needn't show every extreme that they name: `obs_cells`: entry o names a cell of the planes (o // 1024) * 4 to (o // 1024 + 1) * 4 - 1, counted from the first of them: value c stands for plane (o // 1024) * 4 + c // 16384, first horizontal index (c // 128) % 128, second c % 128; cells may repeat.
All inputs are finite; a program needn't handle non-finite values.
Results may differ from a plain program's by a relative error of at most 0.0003.
Values may be sent and summed in bfloat16 or wider, within the bound.
No kernel may reach another device: no remote copies, remote signals or barrier semaphores. Data moves between devices by JAX's collectives and lax.ppermute only.
A program may use at most 128 MiB of HBM per device.

v0:
```python
import functools
import math

import jax
import jax.numpy as jnp
from jax import lax
from jax.sharding import Mesh
from jax.sharding import PartitionSpec as P

ITERS = 3
SLAB = ("slab_0", "slab_1")
MODE = ("mode_0", "mode_1")


STORAGE = 0.05


def padded_2(cells, sides, width):
    for axis, dim in sides:
        count = lax.axis_size(axis)
        ends = count - 1
        head = lax.slice_in_dim(cells, 0, width, axis=dim)
        tail = lax.slice_in_dim(cells, cells.shape[dim] - width, cells.shape[dim], axis=dim)
        cells = jnp.concatenate(
            [
                lax.ppermute(tail, axis, [(i, (i + 1) % count) for i in range(ends)]),
                cells,
                lax.ppermute(head, axis, [((i + 1) % count, i) for i in range(ends)]),
            ],
            axis=dim,
        )
    return cells


def in_order(pieces, dim):
    shape = list(pieces.shape[1:])
    shape[dim] *= pieces.shape[0]
    return jnp.moveaxis(pieces, 0, dim).reshape(shape)


def from_everyone(x, axis):
    copies = jnp.broadcast_to(x, (lax.axis_size(axis), *x.shape))
    return lax.all_to_all(copies, axis, split_axis=0, concat_axis=0, tiled=True)


def collect(x, axis, dim):
    return in_order(from_everyone(x, axis), dim)


def over_axes(x, axes):
    return functools.reduce(lax.psum, axes, x)


def in_one_piece(arrays, axis, dim, along):
    widths = [a.shape[along] for a in arrays]
    both = jnp.concatenate(arrays, axis=along)
    filled = lax.all_gather(both, axis, axis=dim, tiled=True)
    return tuple(jnp.split(filled, [sum(widths[:k]) for k in range(1, len(widths))], axis=along))


def cut_along(x, dim, devices):
    before, after = (x.shape[:dim], x.shape[dim + 1 :])
    return jnp.moveaxis(x.reshape(*before, devices, -1, *after), dim, 0)


def moved_by_axis(pieces, axes, turns):
    inside = pieces.shape[1:]
    filled = pieces.reshape(*(lax.axis_size(a) for a in axes), *inside)
    for k in turns:
        filled = lax.all_to_all(filled, axes[k], k, k, tiled=True)
    return filled.reshape(-1, *inside)


def exchange_by_chip(x, groups, turns, split_dim, concat_dim):
    devices = lax.axis_size(groups[0]) * lax.axis_size(groups[1])
    pieces = cut_along(x, split_dim, devices)
    return in_order(moved_by_axis(pieces, groups, turns), concat_dim)


def sweep_weights(count):
    order = []
    low, high = (0, count - 1)
    while low <= high:
        order.append(low)
        if high != low:
            order.append(high)
        low += 1
        high -= 1
    return [1.0 / (1.15 + 0.85 * math.cos((2 * i + 1) * math.pi / (2 * count))) for i in order]


def coefficients(cond_ext):
    padded = jnp.pad(cond_ext, ((0, 0), (1, 1), (1, 1)), mode="edge")
    centre = padded[1:-1, 1:-1, 1:-1]

    def harmonic(other):
        return 2.0 * centre * other / (centre + other)

    lower = harmonic(padded[:-2, 1:-1, 1:-1])
    upper = harmonic(padded[2:, 1:-1, 1:-1])
    west = harmonic(padded[1:-1, :-2, 1:-1])
    east = harmonic(padded[1:-1, 2:, 1:-1])
    south = harmonic(padded[1:-1, 1:-1, :-2])
    north = harmonic(padded[1:-1, 1:-1, 2:])
    diag = STORAGE + lower + upper + west + east + south + north
    return (lower, upper, west, east, south, north, diag)


def relax(u_ext, source, coeffs, weight):
    lower, upper, west, east, south, north, diag = coeffs
    core = u_ext[:, 1:-1]
    px = jnp.pad(core, ((0, 0), (0, 0), (1, 1), (0, 0)))
    py = jnp.pad(core, ((0, 0), (0, 0), (0, 0), (1, 1)))
    beside = (
        lower * u_ext[:, :-2]
        + upper * u_ext[:, 2:]
        + west * px[:, :, :-2]
        + east * px[:, :, 2:]
        + south * py[..., :-2]
        + north * py[..., 2:]
    )
    return core + weight * (source - (diag * core - beside)) / diag


def fix_ends(extended, width, first_plane, total_planes):
    levels = first_plane - width + jnp.arange(extended.shape[0], dtype=jnp.int32)
    levels = levels[:, None, None]
    extended = jnp.where(levels < 0, extended[width][None], extended)
    return jnp.where(
        levels >= total_planes, extended[extended.shape[0] - width - 1][None], extended
    )


def on_device(log_cond, head_slope, modes, obs_cells, obs_var, misfit, base_fields):
    planes, width_x, width_y = log_cond.shape
    local_modes = modes.shape[0]
    first_plane = lax.axis_index(SLAB) * planes
    total_planes = planes * lax.axis_size(SLAB)
    cond = jnp.exp(log_cond)
    source = head_slope[None] * cond[None] * modes.astype(jnp.float32)
    weights = sweep_weights(ITERS)
    stacked = jnp.concatenate([cond[None], source], axis=0)
    extended = padded_2(stacked, ((SLAB, 1),), ITERS)
    coeffs_full = coefficients(fix_ends(extended[0], ITERS, first_plane, total_planes))
    source_full = extended[1:, 1:-1]
    span = planes + 2 * (ITERS - 1)
    levels = first_plane - (ITERS - 1) + jnp.arange(span, dtype=jnp.int32)
    inside_grid = ((levels >= 0) & (levels < total_planes)).astype(jnp.float32)[:, None, None]
    head = jnp.zeros((local_modes, planes + 2 * ITERS, width_x, width_y), jnp.float32)
    for step, weight in enumerate(weights):
        lower_cut, upper_cut = (step, span - step)
        coeffs_now = tuple((item[lower_cut:upper_cut] for item in coeffs_full))
        head = (
            relax(head, source_full[:, lower_cut:upper_cut], coeffs_now, weight)
            * inside_grid[lower_cut:upper_cut]
        )
    cells_dev = planes * width_x * width_y
    flat = head.reshape(local_modes, cells_dev)
    picked = jnp.take(flat, obs_cells, axis=1)
    whole = collect(picked, MODE, 0)
    scaled = picked / obs_var[None, :]
    row_part = jnp.dot(scaled, whole.T, precision=lax.Precision.HIGHEST)
    rhs_rows = jnp.dot(scaled, misfit, precision=lax.Precision.HIGHEST)
    row_total, rhs_total = (over_axes(row_part, SLAB), over_axes(rhs_rows, SLAB))
    gram, rhs = in_one_piece((row_total, rhs_total), MODE, 0, 1)
    gram = gram + jnp.eye(gram.shape[0], dtype=jnp.float32)
    factor = jnp.linalg.cholesky(gram)
    coef = jax.scipy.linalg.cho_solve((factor, True), rhs)
    block = exchange_by_chip(modes, ("mode_0", "mode_1"), (1, 0), 2, 0)
    total_modes, count_planes, cols, rows = block.shape
    layer = block.reshape(total_modes, count_planes * cols * rows).astype(jnp.float32)
    update = jnp.dot(coef.T, layer, precision=lax.Precision.HIGHEST)
    update = update.reshape(coef.shape[1], count_planes, cols, rows)
    return base_fields.astype(jnp.float32) + update


def solution(mesh):
    torus = Mesh(mesh.devices.reshape(4, 2, 8, 8), ("mode_0", "mode_1", "slab_0", "slab_1"))
    in_specs = (
        P(SLAB, None, None),
        P(SLAB, None, None),
        P(MODE, SLAB, None, None),
        P(SLAB),
        P(SLAB),
        P(SLAB, None),
        P(None, SLAB, MODE, None),
    )
    out_specs = P(None, SLAB, MODE, None)
    return jax.shard_map(
        on_device, mesh=torus, in_specs=in_specs, out_specs=out_specs, check_vma=False
    )
```

profile of v0, /device:TPU:1, one launch (start us, length us, event | category | flops | bytes accessed | tf_op | source)
XLA Modules:
  0.0 186.9 jit_solution(12096614171080402182)
XLA Ops:
  0.0 1.1 exponential_bitcast_fusion
  1.1 0.7 copy-done.3
  1.8 1.5 convert_multiply_fusion
  3.3 2.2 %fusion.43 = (f32[9,3,128,128]{3,2,1,0:T(8,128)}, f32[9,3,128,128]{3,2,1,0:T(8,128)}) fusion(f32[1,4,128,128]{3,2,1,0:T(8,128)S(1)} %get-tuple-element.23, f32[8,4,128,128]{3,2,1,0:T(8,128)S(1)} %convert_multiply_fusion), kind=kLoop, calls=%fused_computation.64 | loop fusion | flops 884736 | bytes 5898240 | tf_op jit(solution)/shard_map/concatenate | solution.py:142
  5.5 5.2 %collective-permute-start = (f32[9,3,128,128]{3,2,1,0:T(8,128)}, f32[9,3,128,128]{3,2,1,0:T(8,128)}, u32[]{:S(2)}, u32[]{:S(2)}) collective-permute-start(f32[9,3,128,128]{3,2,1,0:T(8,128)} %get-tuple-element.17), channel_id=1, source_target_pairs={{0,1},{1,2},{2,3},{3,4},{4,5},{5,6},{6,7},{7,8},{8,9},{9,10},{10,1... | collective-permute-start | bytes 5308424 | tf_op jit(solution)/shard_map/ppermute | solution.py:26
  10.7 1.3 collective-permute-start.1
  12.0 0.3 copy.49
  12.3 8.3 %all_to_all.15 = bf16[4,2,8,4,16,128]{5,4,3,2,0,1:T(8,128)(2,1)S(1)} all-to-all(bf16[4,2,8,4,16,128]{5,4,3,2,0,1:T(8,128)(2,1)S(1)} %copy.49), channel_id=1, replica_groups=mesh['mode_0'=4,'mode_1'=2,'slab_0'=8,'slab_1'=8] {'mode_1'}, dimensions={1} | all-to-all | bytes 2097152 | tf_op jit(solution)/shard_map/all_to_all | solution.py:70
  20.7 1.4 copy.50
  22.0 4.2 %all-to-all-start.2 = ((bf16[4,2,8,4,16,128]{5,4,3,2,1,0:T(8,128)(2,1)}), bf16[4,2,8,4,16,128]{5,4,3,2,1,0:T(8,128)(2,1)}, u32[]{:S(2)}, u32[]{:S(2)}) async-start(bf16[4,2,8,4,16,128]{5,4,3,2,1,0:T(8,128)(2,1)} %copy.50), calls=%async_computation.2 | async-start | bytes 2097152 | tf_op jit(solution)/shard_map/all_to_all | solution.py:70
  26.3 0.7 slice.237
  26.9 0.6 slice.252
  27.5 0.5 fusion.56
  28.1 13.1 %all-to-all-done.2 = bf16[4,2,8,4,16,128]{5,4,3,2,1,0:T(8,128)(2,1)} async-done(((bf16[4,2,8,4,16,128]{5,4,3,2,1,0:T(8,128)(2,1)}), bf16[4,2,8,4,16,128]{5,4,3,2,1,0:T(8,128)(2,1)}, u32[]{:S(2)}, u32[]{:S(2)}) %all-to-all-start.2) | async-done | bytes 1048608 | tf_op jit(solution)/shard_map/all_to_all | solution.py:70
  41.1 2.3 %reshape_reshape_reshape.3 = bf16[64,8192]{1,0:T(8,128)(2,1)} reshape(bf16[4,2,8,4,16,128]{5,4,3,2,1,0:T(8,128)(2,1)} %all-to-all-done.2) | data formatting | bytes 2097152 | tf_op jit(solution)/shard_map/reshape;reshape;reshape | solution.py:171
  43.5 2.5 %copy.56 = bf16[8,8,64,128]{3,2,1,0:T(8,128)(2,1)} copy(bf16[8,8,64,128]{3,1,2,0:T(8,128)(2,1)} %bitcast.50) | data formatting | bytes 2097152
  46.0 3.0 %collective-permute-done.1 = f32[9,3,128,128]{3,2,1,0:T(8,128)} collective-permute-done((f32[9,3,128,128]{3,2,1,0:T(8,128)}, f32[9,3,128,128]{3,2,1,0:T(8,128)}, u32[]{:S(2)}, u32[]{:S(2)}) %collective-permute-start.1) | collective-permute-done | bytes 1769504 | tf_op jit(solution)/shard_map/ppermute | solution.py:28
  49.0 1.1 fusion.45
  50.1 0.1 broadcast_select_fusion
  50.3 0.2 fusion.58
  50.6 0.9 broadcast_multiply_fusion
  51.7 0.7 slice.280
  52.4 0.7 slice.282
  53.2 0.7 slice.284
  53.9 0.7 slice.285
  54.7 0.7 slice.286
  55.4 0.7 slice.287
  56.1 2.3 %pad_maximum_fusion = f32[9,10,128,128]{3,2,1,0:T(8,128)S(1)} fusion(f32[9,3,128,128]{3,2,1,0:T(8,128)} %collective-permute-done.1, f32[8,4,128,128]{3,2,1,0:T(8,128)S(1)} %convert_multiply_fusion, f32[1,4,128,128]{3,2,1,0:T(8,128)S(1)} %get-tuple-element.23, f32[9,3,128,128]{3,2,1,0:T(8,128)} %collective-permute-done), kind=kLoop, calls=%fused_computation.7 | loop fusion | flops 4423680 | bytes 11796480 | tf_op jit(solution)/shard_map/concatenate | solution.py:24
  58.5 0.5 broadcast.168
  59.0 3.4 %fusion.12 = f32[8,8,128,128]{3,2,1,0:T(8,128)S(1)} fusion(f32[8,8,128,128]{3,2,1,0:T(8,128)S(1)} %broadcast.168, f32[9,10,128,128]{3,2,1,0:T(8,128)S(1)} %pad_maximum_fusion, f32[8]{0:T(128)S(1)} %and_convert_fusion, f32[8,128,128]{2,1,0:T(8,128)S(1)} %get-tuple-element.10, f32[8,128,128]{2,1,0:T(8,128)S(1)} %get-tuple-element.16, ...), kind=kLoop, calls=%fused_computation.22 | loop fusion | flops 13631488 | bytes 16252960 | tf_op jit(solution)/shard_map/mul | solution.py:154
  62.4 0.3 slice.267
  62.8 0.3 copy-done.14
  63.1 3.1 %fusion.27 = f32[8,6,128,128]{3,2,1,0:T(8,128)S(1)} fusion(f32[8,6,128,128]{3,2,1,0:T(8,128)S(1)} %slice.267, f32[8,8,128,128]{3,2,1,0:T(8,128)S(1)} %fusion.12, f32[9,10,128,128]{3,2,1,0:T(8,128)S(1)} %pad_maximum_fusion, f32[6]{0:T(128)S(1)} %copy-done.14, f32[6,128,128]{2,1,0:T(8,128)S(1)} %slice.277, f32[6,128,128]{2,1,0:T(8,128)S(1)} %slice.276, ...), kind=kLoop, calls=%fused_computation.41 | loop fusion | flops 14155776 | bytes 18481176 | tf_op jit(solution)/shard_map/mul | solution.py:154
  66.3 0.2 slice.278
  66.5 0.6 copy-done.4
  67.1 0.1 copy-done.5
  67.2 0.1 copy-done.6
  67.3 0.1 copy-done.7
  67.4 0.1 copy-done.8
  67.5 0.1 copy-done.9
  67.6 0.1 copy-done.10
  67.6 2.2 %fusion.42 = f32[8,4,128,128]{3,2,1,0:T(8,128)S(1)} fusion(f32[8,4,128,128]{3,2,1,0:T(8,128)S(1)} %slice.278, f32[8,6,128,128]{3,2,1,0:T(8,128)S(1)} %fusion.27, f32[4]{0:T(128)S(1)} %copy-done.13, f32[4,128,128]{2,1,0:T(8,128)S(1)} %copy-done.10, f32[4,128,128]{2,1,0:T(8,128)S(1)} %copy-done.9, f32[4,128,128]{2,1,0:T(8,128)S(1)} %copy-done.8, ...), kind=kLoop, calls=%fused_computation.63 | loop fusion | flops 10485760 | bytes 11534352 | tf_op jit(solution)/shard_map/mul | solution.py:154
  69.8 16.5 %copy.45 = f32[8,4,128,128]{0,3,2,1:T(8,128)} copy(f32[8,4,128,128]{3,2,1,0:T(8,128)S(1)} %fusion.42) | data formatting | bytes 4194304 | tf_op jit(solution)/shard_map/mul | solution.py:154
  86.3 13.3 %gather_fusion = f32[1024,8]{1,0:T(8,128)S(1)} fusion(f32[8,65536]{0,1:T(8,128)} %bitcast.47, s32[1024]{0:T(1024)S(1)} %fusion.55), kind=kCustom, calls=%fused_computation | custom fusion | bytes 69632 | tf_op jit(solution)/shard_map/jit(_take)/gather | solution.py:159
  99.7 0.2 select_bitcast_fusion
  99.9 0.2 copy.46
  100.1 0.7 broadcast_in_dim.91
  100.8 9.3 %all-to-all-start = ((f32[8,8,1024]{2,1,0:T(8,128)}), f32[8,8,1024]{2,1,0:T(8,128)S(1)}, u32[]{:S(2)}, u32[]{:S(2)}) async-start(f32[8,8,1024]{2,1,0:T(8,128)} %broadcast_in_dim.91), calls=%async_computation | async-start | bytes 524288 | tf_op jit(solution)/shard_map/all_to_all | solution.py:43
  110.1 1.1 fusion.48
  111.2 5.3 %all-to-all-done = f32[8,8,1024]{2,1,0:T(8,128)S(1)} async-done(((f32[8,8,1024]{2,1,0:T(8,128)}), f32[8,8,1024]{2,1,0:T(8,128)S(1)}, u32[]{:S(2)}, u32[]{:S(2)}) %all-to-all-start) | async-done | bytes 262176 | tf_op jit(solution)/shard_map/all_to_all | solution.py:43
  116.5 1.1 fusion.46
  117.6 18.6 %all-reduce.7 = (f32[8,16]{1,0:T(8,128)S(1)}, f32[8,64]{1,0:T(8,128)S(1)}) all-reduce(f32[8,16]{1,0:T(8,128)S(1)} %fusion.48, f32[8,64]{1,0:T(8,128)S(1)} %fusion.46), channel_id=1, replica_groups=mesh['mode_0'=4,'mode_1'=2,'slab_0'=8,'slab_1'=8] {'slab_0'}, use_global_device_ids=true, to_apply=%region_2.3 | all-reduce | flops 640 | bytes 5120 | tf_op jit(solution)/shard_map/psum | solution.py:51
  136.3 15.0 %all-reduce.6 = (f32[8,16]{1,0:T(8,128)S(1)}, f32[8,64]{1,0:T(8,128)S(1)}) all-reduce(f32[8,16]{1,0:T(8,128)S(1)} %get-tuple-element.7, f32[8,64]{1,0:T(8,128)S(1)} %get-tuple-element.8), channel_id=1, replica_groups=mesh['mode_0'=4,'mode_1'=2,'slab_0'=8,'slab_1'=8] {'slab_1'}, use_global_device_ids=true, to_apply=%region_3.4 | all-reduce | flops 640 | bytes 5120 | tf_op jit(solution)/shard_map/psum | solution.py:51
  151.3 0.1 pad_maximum_fusion.11
  151.4 20.8 %all_gather.3 = f32[64,80]{1,0:T(8,128)S(1)} all-gather(f32[8,80]{1,0:T(8,128)S(1)} %pad_maximum_fusion.11), channel_id=1, replica_groups=mesh['mode_0'=4,'mode_1'=2,'slab_0'=8,'slab_1'=8] {'mode_0','mode_1'}, dimensions={0}, use_global_device_ids=true | all-gather | bytes 23040 | tf_op jit(solution)/shard_map/all_gather | solution.py:57
  172.2 0.1 copy.47
  172.3 5.8 %cholesky.17 = f32[64,64]{1,0:T(8,128)S(1)} custom-call(f32[64,64]{1,0:T(8,128)S(1)} %fusion.54), custom_call_target="Cholesky" | custom-call | tf_op jit(solution)/shard_map/jit(cholesky)/cholesky | solution.py:167
  178.2 0.6 compare_reduce_fusion
  178.8 0.7 fusion.49
  179.5 4.9 %custom-call.10 = f32[1,64,64]{1,2,0:T(8,128)S(1)} custom-call(f32[1,64,64]{2,1,0:T(8,128)S(1)} %fusion.49), custom_call_target="InvertDiagBlocksLowerTriangular" | custom-call | tf_op jit(solution)/shard_map/jit(_cho_solve)/triangular_solve | solution.py:168
  184.4 0.3 fusion.50
  184.7 0.2 convolution_bitcast_fusion
  184.9 1.0 convolution_add_fusion
  185.9 1.0 copy.52
  (43 shorter events, 0.5 us)
Async XLA Ops:
  0.0 110.1 %copy-start = (f32[1024,16]{0,1:T(8,128)S(1)}, f32[1024,16]{0,1:T(8,128)}, u32[]{:S(2)}) copy-start(f32[1024,16]{0,1:T(8,128)} %param.12) | copy-start | bytes 196612
  1.1 0.7 copy-start.3
  3.3 8.7 %copy-start.1 = (bf16[8,4,128,128]{3,2,1,0:T(8,128)(2,1)S(1)}, bf16[8,4,128,128]{3,2,1,0:T(8,128)(2,1)}, u32[]{:S(2)}) copy-start(bf16[8,4,128,128]{3,2,1,0:T(8,128)(2,1)} %param.9) | copy-start | bytes 3145732
  5.5 40.5 %collective-permute-start = (f32[9,3,128,128]{3,2,1,0:T(8,128)}, f32[9,3,128,128]{3,2,1,0:T(8,128)}, u32[]{:S(2)}, u32[]{:S(2)}) collective-permute-start(f32[9,3,128,128]{3,2,1,0:T(8,128)} %get-tuple-element.17), channel_id=1, source_target_pairs={{0,1},{1,2},{2,3},{3,4},{4,5},{5,6},{6,7},{7,8},{8,9},{9,10},{10,1... | collective-permute-start | bytes 5308424 | tf_op jit(solution)/shard_map/ppermute | solution.py:26
  10.7 38.3 %collective-permute-start.1 = (f32[9,3,128,128]{3,2,1,0:T(8,128)}, f32[9,3,128,128]{3,2,1,0:T(8,128)}, u32[]{:S(2)}, u32[]{:S(2)}) collective-permute-start(f32[9,3,128,128]{3,2,1,0:T(8,128)} %get-tuple-element.18), channel_id=1, source_target_pairs={{1,0},{2,1},{3,2},{4,3},{5,4},{6,5},{7,6},{8,7},{9,8},{10,9},{11,1... | collective-permute-start | bytes 5308424 | tf_op jit(solution)/shard_map/ppermute | solution.py:28
  12.3 15.7 %copy-start.12 = (s32[1024]{0:T(1024)S(1)}, s32[1024]{0:T(1024)}, u32[]{:S(2)}) copy-start(s32[1024]{0:T(1024)} %param.10) | copy-start | bytes 12292
  22.0 19.1 %all-to-all-start.2 = ((bf16[4,2,8,4,16,128]{5,4,3,2,1,0:T(8,128)(2,1)}), bf16[4,2,8,4,16,128]{5,4,3,2,1,0:T(8,128)(2,1)}, u32[]{:S(2)}, u32[]{:S(2)}) async-start(bf16[4,2,8,4,16,128]{5,4,3,2,1,0:T(8,128)(2,1)} %copy.50), calls=%async_computation.2 | async-start | bytes 2097152 | tf_op jit(solution)/shard_map/all_to_all | solution.py:70
  62.4 0.7 copy-start.14
  66.2 1.0 copy-start.4
  66.2 1.0 copy-start.5
  66.2 1.1 copy-start.6
  66.2 1.2 copy-start.7
  66.2 1.2 copy-start.8
  66.2 1.3 copy-start.9
  66.3 1.4 copy-start.10
  66.3 1.4 copy-start.13
  69.8 40.2 %copy-start.15 = (f32[1024]{0:T(1024)S(1)}, f32[1024]{0:T(1024)}, u32[]{:S(2)}) copy-start(f32[1024]{0:T(1024)} %param.11) | copy-start | bytes 12292
  99.7 85.2 %copy-start.2 = (bf16[8,8,64,128]{3,2,1,0:T(8,128)(2,1)S(1)}, bf16[8,8,64,128]{3,2,1,0:T(8,128)(2,1)}, u32[]{:S(2)}) copy-start(bf16[8,8,64,128]{3,2,1,0:T(8,128)(2,1)} %copy.56) | copy-start | bytes 3145732
  99.7 85.2 %copy-start.11 = (bf16[16,4,16,128]{3,2,1,0:T(8,128)(2,1)S(1)}, bf16[16,4,16,128]{3,2,1,0:T(8,128)(2,1)}, u32[]{:S(2)}) copy-start(bf16[16,4,16,128]{3,2,1,0:T(8,128)(2,1)} %param.13) | copy-start | bytes 786436
  100.8 15.7 %all-to-all-start = ((f32[8,8,1024]{2,1,0:T(8,128)}), f32[8,8,1024]{2,1,0:T(8,128)S(1)}, u32[]{:S(2)}, u32[]{:S(2)}) async-start(f32[8,8,1024]{2,1,0:T(8,128)} %broadcast_in_dim.91), calls=%async_computation | async-start | bytes 524288 | tf_op jit(solution)/shard_map/all_to_all | solution.py:43
where the time goes:
time: 188 us; the launch traced here: 187 us
  blocking collectives  62.8 us (33%)
  local copies, waits for them, and re-layouts  47.6 us (25%)
  other arithmetic  31 us (16%)
  waiting for transfers between devices  21.4 us (11%)
  starting transfers between devices  20 us (11%)
  matrix products  3.69 us (2%)
    psum x2, blocking collectives, over_axes(): return functools.reduce(lax.psum, axes, x)  33.7 us
    all_gather x1, blocking collectives, in_one_piece(): filled = lax.all_gather(both, axis, axis=dim, tiled=True)  20.8 us
    mul x1, local copies, waits for them, and re-layouts, on_device(): relax(head, source_full[:, lower_cut:upper_cut], coeffs_now, weight)  16.5 us
    gather x1, local copies, waits for them, and re-layouts, on_device(): picked = jnp.take(flat, obs_cells, axis=1)  13.3 us
    all_to_all x1, waiting for transfers between devices, moved_by_axis(): filled = lax.all_to_all(filled, axes[k], k, k, tiled=True)  13.1 us
    all_to_all x1, starting transfers between devices, from_everyone(): return lax.all_to_all(copies, axis, split_axis=0, concat_axis=0, tiled=True)  9.27 us
    mul x3, other arithmetic, on_device(): relax(head, source_full[:, lower_cut:upper_cut], coeffs_now, weight)  8.7 us
    all_to_all x1, blocking collectives, moved_by_axis(): filled = lax.all_to_all(filled, axes[k], k, k, tiled=True)  8.31 us
  transfers between devices with their start and end apart: 4, of which 3 were waited for; matrix products, arithmetic and copies ran while one was open for 5% of the time, Pallas kernels for 0%

commit v1 on v0

v1 whole, which is shorter than its diff:
```python
import math

import jax
import jax.numpy as jnp
from jax import lax
from jax.experimental import pallas as pl
from jax.experimental.pallas import tpu as pltpu
from jax.sharding import Mesh
from jax.sharding import PartitionSpec as P

ITERS = 3
SLAB = ("slab_0", "slab_1")
MODE = ("mode_0", "mode_1")
STORAGE = 0.05
CZ = 4
NX = 128
NY = 128
LM = 8
OBS = 1024
MODES = 64
FIELDS = 16
ROWS = NX + 2
HI = lax.Precision.HIGHEST


def sweep_weights(count):
    order = []
    low, high = (0, count - 1)
    while low <= high:
        order.append(low)
        if high != low:
            order.append(high)
        low += 1
        high -= 1
    return [1.0 / (1.15 + 0.85 * math.cos((2 * i + 1) * math.pi / (2 * count))) for i in order]


W1, W2, W3 = sweep_weights(ITERS)


def harmonic(a, b):
    return 2.0 * a * b / (a + b)


def respond_kernel(edge, pick, lc, hs, before, after, modes, mbefore, mafter, out, coef, u1, u2, u3):
    first = edge[0] == 0
    last = edge[1] == 0
    rows = lax.broadcasted_iota(jnp.int32, (NX, NY), 0)
    cols = lax.broadcasted_iota(jnp.int32, (NX, NY), 1)

    own = [jnp.exp(lc[z]) for z in range(CZ)]
    cond = [jnp.where(first, own[0], jnp.exp(before[z])) for z in range(3)]
    cond += own
    cond += [jnp.where(last, own[CZ - 1], jnp.exp(after[z])) for z in range(3)]
    slope = [before[3], before[4]] + [hs[z] for z in range(CZ)] + [after[3], after[4]]
    faces = [harmonic(cond[z], cond[z + 1]) for z in range(9)]
    zero = jnp.zeros((LM, NY), jnp.float32)

    for e in range(8):
        c = cond[e + 1]
        lower = faces[e]
        upper = faces[e + 1]
        toward_e = jnp.where(rows == NX - 1, c, pltpu.roll(c, NX - 1, 0))
        east = harmonic(c, toward_e)
        west = jnp.where(rows == 0, harmonic(c, c), pltpu.roll(east, 1, 0))
        toward_n = jnp.where(cols == NY - 1, c, pltpu.roll(c, NY - 1, 1))
        north = harmonic(c, toward_n)
        south = jnp.where(cols == 0, harmonic(c, c), pltpu.roll(north, 1, 1))
        diag = STORAGE + lower + upper + west + east + south + north
        inv = 1.0 / diag
        if 1 <= e <= 6:
            keep = 1.0
            if e == 1:
                keep = jnp.where(first, 0.0, 1.0)
            if e == 6:
                keep = jnp.where(last, 0.0, 1.0)
            scale = inv * (W2 * keep)
            coef[0, e] = lower * scale
            coef[1, e] = upper * scale
            coef[2, e] = jnp.where(rows == 0, 0.0, west * scale)
            coef[3, e] = jnp.where(rows == NX - 1, 0.0, east * scale)
            coef[4, e] = jnp.where(cols == 0, 0.0, south * scale)
            coef[5, e] = jnp.where(cols == NY - 1, 0.0, north * scale)
        lead = slope[e] * c * inv * W1
        base = e * ROWS * LM
        u1[pl.ds(base, LM), :] = zero
        u1[pl.ds(base + (ROWS - 1) * LM, LM), :] = zero
        for k in range(LM):
            if e < 2:
                m = mbefore[k, e]
            elif e < 2 + CZ:
                m = modes[k, e - 2]
            else:
                m = mafter[k, e - 2 - CZ]
            u1[pl.ds(base + LM + k, NX, stride=LM), :] = m.astype(jnp.float32) * lead

    def at(ref, e, x):
        return ref[pl.ds(pl.multiple_of((e * ROWS + x) * LM, LM), LM), :]

    def sweep(ref, e, x):
        def c(i):
            return coef[i, e, pl.ds(x - 1, 1), :]

        u = at(ref, e, x)
        total = c(0) * at(ref, e - 1, x) + c(1) * at(ref, e + 1, x)
        total = total + (c(2) * at(ref, e, x - 1) + c(3) * at(ref, e, x + 1))
        total = total + (c(4) * pltpu.roll(u, 1, 1) + c(5) * pltpu.roll(u, NY - 1, 1))
        return u, total

    UN = 8
    for e in range(1, 7):
        base = e * ROWS * LM
        u2[pl.ds(base, LM), :] = zero
        u2[pl.ds(base + (ROWS - 1) * LM, LM), :] = zero
        own_weight = 1.0 - W2 + W2 / W1
        if e == 1:
            own_weight = jnp.where(first, 0.0, own_weight)
        if e == 6:
            own_weight = jnp.where(last, 0.0, own_weight)

        def second(i, _, e=e, own_weight=own_weight):
            for j in range(UN):
                x = i * UN + j + 1
                u, total = sweep(u1, e, x)
                u2[pl.ds(pl.multiple_of((e * ROWS + x) * LM, LM), LM), :] = own_weight * u + total
            return 0

        lax.fori_loop(0, NX // UN, second, 0)

    for e in range(2, 6):

        def third(i, _, e=e):
            for j in range(UN):
                x = i * UN + j + 1
                u, total = sweep(u2, e, x)
                value = (1.0 - W3) * u + (W3 / W1) * at(u1, e, x) + (W3 / W2) * total
                u3[(e - 2) * NX + x - 1] = value
            return 0

        lax.fori_loop(0, NX // UN, third, 0)

    lanes = lax.broadcasted_iota(jnp.int32, (LM, NY), 1)
    PU = 16

    def block(b, _):
        def group(g, acc):
            for j in range(PU):
                p = pick[b * NY + g * PU + j]
                row = u3[lax.shift_right_logical(p, 7)]
                acc = jnp.where(lanes == g * PU + j, pltpu.roll(row, p & 127, 1), acc)
            return acc

        got = lax.fori_loop(0, NY // PU, group, zero)
        for d in range(8):
            out[d, b] = got
        return 0

    lax.fori_loop(0, OBS // NY, block, 0)


def gram_kernel(resp, var, misfit, out):
    r = resp[...]
    scaled = r / var[...]
    mis = misfit[...]
    half = MODES // 2
    none = jnp.zeros((half, OBS), jnp.float32)
    none_f = jnp.zeros((FIELDS, OBS), jnp.float32)
    right_a = jnp.concatenate([r, none, mis, none_f], axis=0)
    right_b = jnp.concatenate([none, none, r[half:], none_f, mis], axis=0)
    dims = (((1,), (1,)), ((), ()))
    got = lax.dot_general(scaled[:half], right_a, dims, precision=HI, preferred_element_type=jnp.float32)
    got = got + lax.dot_general(
        scaled[half:], right_b, dims, precision=HI, preferred_element_type=jnp.float32
    )
    for d in range(8):
        out[d] = got


def total_kernel(parts, out):
    got = parts[0]
    for d in range(1, 8):
        got = got + parts[d]
    for d in range(8):
        out[d] = got


def solve_kernel(parts, out):
    p = parts[0]
    for d in range(1, 8):
        p = p + parts[d]
    half = MODES // 2
    lane = lax.broadcasted_iota(jnp.int32, (half, 128), 1)
    square = jnp.concatenate([p, jnp.zeros((128 - half, 128), jnp.float32)], axis=0)
    turned = square.T[half : 2 * half]
    near = pltpu.roll(p, 128 - 32, 1)
    far = pltpu.roll(p, 128 - 48, 1)
    top = jnp.where(lane < 64, p, near)
    low = jnp.where(lane < 32, turned, jnp.where(lane < 64, near, far))
    a = jnp.concatenate([top, low], axis=0)
    row = lax.broadcasted_iota(jnp.int32, (MODES, 128), 0)
    col = lax.broadcasted_iota(jnp.int32, (MODES, 128), 1)
    a = jnp.where(row == col, a + 1.0, a)
    a = [a[8 * i : 8 * i + 8] for i in range(8)]
    sub = lax.broadcasted_iota(jnp.int32, (8, 128), 0)

    def wide(v):
        return jnp.broadcast_to(v, (8, 128))

    for q in range(8):
        cs = [[wide(a[i][:, 8 * q + t : 8 * q + t + 1]) for i in range(8)] for t in range(8)]
        for t in range(8):
            c = cs[t]
            inv = 1.0 / wide(c[q][t : t + 1])
            norm = wide(a[q][t : t + 1]) * inv
            for i in range(8):
                new = a[i] - c[i] * norm
                a[i] = jnp.where(sub == t, norm, new) if i == q else new
            for s in range(t + 1, 8):
                f = wide(c[q][s : s + 1]) * inv
                for i in range(8):
                    new = cs[s][i] - c[i] * f
                    cs[s][i] = jnp.where(sub == t, f, new) if i == q else new
    for i in range(8):
        out[8 * i : 8 * i + 8, :] = a[i]


def vmem(n):
    return [pl.BlockSpec(memory_space=pltpu.VMEM)] * n


def smem(n):
    return [pl.BlockSpec(memory_space=pltpu.SMEM)] * n


def on_device(log_cond, head_slope, modes, obs_cells, obs_var, misfit, base_fields):
    slabs = lax.axis_size(SLAB)
    slab = lax.axis_index(SLAB)
    ahead = [(i, i + 1) for i in range(slabs - 1)]
    back = [(i + 1, i) for i in range(slabs - 1)]

    mbefore = lax.ppermute(modes[:, 2:4], SLAB, ahead)
    mafter = lax.ppermute(modes[:, 0:2], SLAB, back)
    before = lax.ppermute(jnp.concatenate([log_cond[1:4], head_slope[2:4]]), SLAB, ahead)
    after = lax.ppermute(jnp.concatenate([log_cond[0:3], head_slope[0:2]]), SLAB, back)

    pieces = jnp.moveaxis(modes.reshape(LM, CZ, 8, NX // 8, NY), 2, 0)
    block = lax.all_to_all(pieces, MODE, 0, 0, tiled=True)
    block, mbefore, mafter = lax.optimization_barrier((block, mbefore, mafter))

    edge = jnp.stack([slab, slabs - 1 - slab]).astype(jnp.int32)
    place = jnp.arange(OBS, dtype=jnp.int32)
    pick = (obs_cells & ~127) | ((place - obs_cells) & 127)
    copies = pl.pallas_call(
        respond_kernel,
        out_shape=jax.ShapeDtypeStruct((8, 8, LM, NY), jnp.float32),
        in_specs=smem(2) + vmem(7),
        out_specs=pl.BlockSpec(memory_space=pltpu.VMEM),
        scratch_shapes=[
            pltpu.VMEM((6, 8, NX, NY), jnp.float32),
            pltpu.VMEM((8 * ROWS * LM, NY), jnp.float32),
            pltpu.VMEM((8 * ROWS * LM, NY), jnp.float32),
            pltpu.VMEM((CZ * NX, LM, NY), jnp.float32),
        ],
        name="respond",
    )(edge, pick, log_cond, head_slope, before, after, modes, mbefore, mafter)
    whole = lax.all_to_all(copies, MODE, 0, 0, tiled=True)
    whole = jnp.moveaxis(whole, 1, 2).reshape(MODES, OBS)

    shared = jax.ShapeDtypeStruct((8, 32, 128), jnp.float32)
    part = pl.pallas_call(gram_kernel, out_shape=shared, in_specs=vmem(3), out_specs=vmem(1)[0], name="gram")(
        whole, obs_var.reshape(1, OBS), misfit.T
    )
    part = lax.all_to_all(part, "slab_1", 0, 0, tiled=True)
    part = pl.pallas_call(total_kernel, out_shape=shared, in_specs=vmem(1), out_specs=vmem(1)[0], name="total")(part)
    part = lax.all_to_all(part, "slab_0", 0, 0, tiled=True)
    solved = pl.pallas_call(
        solve_kernel,
        out_shape=jax.ShapeDtypeStruct((MODES, 128), jnp.float32),
        in_specs=vmem(1),
        out_specs=vmem(1)[0],
        name="solve",
    )(part)
    coef = solved[:, MODES : MODES + FIELDS]

    layer = block.reshape(MODES, CZ, NX // 8, NY).astype(jnp.float32)
    update = lax.dot_general(coef, layer, (((0,), (0,)), ((), ())), precision=HI)
    return base_fields.astype(jnp.float32) + update


def solution(mesh):
    torus = Mesh(mesh.devices.reshape(4, 2, 8, 8), ("mode_0", "mode_1", "slab_0", "slab_1"))
    in_specs = (
        P(SLAB, None, None),
        P(SLAB, None, None),
        P(MODE, SLAB, None, None),
        P(SLAB),
        P(SLAB),
        P(SLAB, None),
        P(None, SLAB, MODE, None),
    )
    out_specs = P(None, SLAB, MODE, None)
    return jax.shard_map(
        on_device, mesh=torus, in_specs=in_specs, out_specs=out_specs, check_vma=False
    )
```

time: 188 us -> 116 us (0.62)
  the two profiles are of different devices: /device:TPU:1 before, /device:TPU:2 now
where the time goes in v1:
time: 116 us; the launch traced here: 115 us
  blocking collectives  44.4 us (38%)
  Pallas kernels  31.4 us (27%)
  starting transfers between devices  18.1 us (16%)
  waiting for transfers between devices  13 us (11%)
  local copies, waits for them, and re-layouts  3.77 us (3%)
  other arithmetic  2.63 us (2%)
  matrix products  1.82 us (2%)
    pallas_call x1, Pallas kernels, on_device(): pl.pallas_call(respond_kernel, out_shape=jax.ShapeDtypeStruct((8, 8, LM,...  24 us
    all_to_all x1, blocking collectives, on_device(): part = lax.all_to_all(part, 'slab_0', 0, 0, tiled=True)  19.6 us
    all_to_all x1, blocking collectives, on_device(): part = lax.all_to_all(part, 'slab_1', 0, 0, tiled=True)  13.8 us
    all_to_all x1, blocking collectives, on_device(): whole = lax.all_to_all(copies, MODE, 0, 0, tiled=True)  11 us
    all_to_all x1, starting transfers between devices, on_device(): block = lax.all_to_all(pieces, MODE, 0, 0, tiled=True)  9.48 us
    ppermute x1, waiting for transfers between devices, on_device(): mafter = lax.ppermute(modes[:, 0:2], SLAB, back)  4.57 us
    ppermute x1, starting transfers between devices, on_device(): lax.ppermute(jnp.concatenate([log_cond[1:4], head_slope[2:4]]), SLAB, ahead)  4.55 us
    ppermute x1, waiting for transfers between devices, on_device(): lax.ppermute(jnp.concatenate([log_cond[0:3], head_slope[0:2]]), SLAB, back)  4.29 us
  transfers between devices with their start and end apart: 5, of which 4 were waited for; matrix products, arithmetic and copies ran while one was open for 2% of the time, Pallas kernels for 0%

profile of v1, /device:TPU:2, one launch (start us, length us, event | category | flops | bytes accessed | tf_op | source)
XLA Modules:
  0.0 115.2 jit_solution(15209059701392016583)
XLA Ops:
  0.0 2.5 %copy.17 = bf16[8,8,4,16,128]{4,3,2,1,0:T(8,128)(2,1)} copy(bf16[8,8,4,16,128]{4,3,0,2,1:T(8,128)(2,1)} %bitcast.14) | data formatting | bytes 2097152 | tf_op jit(solution)/shard_map/transpose | solution.py:246
  2.5 0.0 copy-start
  2.5 9.5 %all-to-all-start = ((bf16[8,8,4,16,128]{4,3,2,1,0:T(8,128)(2,1)}), bf16[8,8,4,16,128]{4,3,2,1,0:T(8,128)(2,1)S(1)}, u32[]{:S(2)}, u32[]{:S(2)}) async-start(bf16[8,8,4,16,128]{4,3,2,1,0:T(8,128)(2,1)} %copy.17), calls=%async_computation | async-start | bytes 2097152 | tf_op jit(solution)/shard_map/all_to_all | solution.py:247
  12.0 0.0 copy-done
  12.0 0.0 copy-start.2
  12.0 0.1 fusion.1
  12.1 1.3 %collective-permute-start.2 = (bf16[8,2,128,128]{3,2,1,0:T(8,128)(2,1)S(1)}, bf16[8,2,128,128]{3,2,1,0:T(8,128)(2,1)S(1)}, u32[]{:S(2)}, u32[]{:S(2)}) collective-permute-start(bf16[8,2,128,128]{3,2,1,0:T(8,128)(2,1)S(1)} %get-tuple-element.12), channel_id=1, source_target_pairs={{0,1},{1,2},{2,3},{3,4},{4,5},{5,6},{6,7},{7,8},{8,9},{9,10},{10,1... | collective-permute-start | bytes 1572872 | tf_op jit(solution)/shard_map/ppermute | solution.py:241
  13.4 0.0 copy-start.1
  13.4 1.4 %collective-permute-start.3 = (bf16[8,2,128,128]{3,2,1,0:T(8,128)(2,1)S(1)}, bf16[8,2,128,128]{3,2,1,0:T(8,128)(2,1)S(1)}, u32[]{:S(2)}, u32[]{:S(2)}) collective-permute-start(bf16[8,2,128,128]{3,2,1,0:T(8,128)(2,1)S(1)} %get-tuple-element.11), channel_id=1, source_target_pairs={{1,0},{2,1},{3,2},{4,3},{5,4},{6,5},{7,6},{8,7},{9,8},{10,9},{11,1... | collective-permute-start | bytes 1572872 | tf_op jit(solution)/shard_map/ppermute | solution.py:242
  14.9 0.0 copy-done.2
  14.9 0.0 copy-done.1
  15.0 0.7 pad_maximum_fusion
  15.7 4.6 %collective-permute-start = (f32[5,128,128]{2,1,0:T(8,128)}, f32[5,128,128]{2,1,0:T(8,128)S(1)}, u32[]{:S(2)}, u32[]{:S(2)}) collective-permute-start(f32[5,128,128]{2,1,0:T(8,128)} %pad_maximum_fusion), channel_id=1, source_target_pairs={{0,1},{1,2},{2,3},{3,4},{4,5},{5,6},{6,7},{7,8},{8,9},{9,10},{10,1... | collective-permute-start | bytes 983048 | tf_op jit(solution)/shard_map/ppermute | solution.py:243
  20.3 0.7 pad_maximum_fusion.1
  21.0 1.3 %collective-permute-start.1 = (f32[5,128,128]{2,1,0:T(8,128)}, f32[5,128,128]{2,1,0:T(8,128)}, u32[]{:S(2)}, u32[]{:S(2)}) collective-permute-start(f32[5,128,128]{2,1,0:T(8,128)} %pad_maximum_fusion.1), channel_id=1, source_target_pairs={{1,0},{2,1},{3,2},{4,3},{5,4},{6,5},{7,6},{8,7},{9,8},{10,9},{11,1... | collective-permute-start | bytes 983048 | tf_op jit(solution)/shard_map/ppermute | solution.py:244
  22.3 0.0 copy-start.7
  22.3 0.6 pad_add_fusion.edge
  22.9 0.1 copy-done.7
  23.0 0.6 and_or_fusion.pick
  23.6 2.1 %collective-permute-done.2.mbefore = bf16[8,2,128,128]{3,2,1,0:T(8,128)(2,1)S(1)} collective-permute-done((bf16[8,2,128,128]{3,2,1,0:T(8,128)(2,1)S(1)}, bf16[8,2,128,128]{3,2,1,0:T(8,128)(2,1)S(1)}, u32[]{:S(2)}, u32[]{:S(2)}) %collective-permute-start.2) | collective-permute-done | bytes 524320 | tf_op jit(solution)/shard_map/ppermute | solution.py:241
  25.7 0.0 copy-start.3
  25.7 4.6 %collective-permute-done.3.mafter = bf16[8,2,128,128]{3,2,1,0:T(8,128)(2,1)S(1)} collective-permute-done((bf16[8,2,128,128]{3,2,1,0:T(8,128)(2,1)S(1)}, bf16[8,2,128,128]{3,2,1,0:T(8,128)(2,1)S(1)}, u32[]{:S(2)}, u32[]{:S(2)}) %collective-permute-start.3) | collective-permute-done | bytes 524320 | tf_op jit(solution)/shard_map/ppermute | solution.py:242
  30.3 0.0 copy-start.4
  30.3 0.0 all-to-all-done
  30.3 2.0 %collective-permute-done.before = f32[5,128,128]{2,1,0:T(8,128)S(1)} collective-permute-done((f32[5,128,128]{2,1,0:T(8,128)}, f32[5,128,128]{2,1,0:T(8,128)S(1)}, u32[]{:S(2)}, u32[]{:S(2)}) %collective-permute-start) | collective-permute-done | bytes 327712 | tf_op jit(solution)/shard_map/ppermute | solution.py:243
  32.3 0.0 copy-start.5
  32.3 4.3 %collective-permute-done.1.after = f32[5,128,128]{2,1,0:T(8,128)} collective-permute-done((f32[5,128,128]{2,1,0:T(8,128)}, f32[5,128,128]{2,1,0:T(8,128)}, u32[]{:S(2)}, u32[]{:S(2)}) %collective-permute-start.1) | collective-permute-done | bytes 327712 | tf_op jit(solution)/shard_map/ppermute | solution.py:244
  36.5 0.0 copy-done.3
  36.5 0.0 copy-done.4
  36.6 0.0 copy-done.5
  36.6 24.0 %respond.1 = f32[8,8,8,128]{3,2,1,0:T(8,128)} custom-call(s32[2]{0:T(128)} %pad_add_fusion.edge, s32[1024]{0:T(1024)} %and_or_fusion.pick, f32[4,128,128]{2,1,0:T(8,128)} %lc.1, f32[4,128,128]{2,1,0:T(8,128)} %hs.1, f32[5,128,128]{2,1,0:T(8,128)} %copy-done.5, f32[5,128,128]{2,1,0:T(8,128)} %collective-permute-done.1.after, bf16[8,4,128,128]{3,2,1,0:T(8,128)(2,1)} %modes.1, ...), custom_call_target="tpu_custom_call" | custom-call | tf_op jit(solution)/shard_map/respond/pallas_call | solution.py:253
  60.6 11.0 %all_to_all.20 = f32[8,8,8,128]{3,2,1,0:T(8,128)} all-to-all(f32[8,8,8,128]{3,2,1,0:T(8,128)} %respond.1), channel_id=1, replica_groups=mesh['mode_0'=4,'mode_1'=2,'slab_0'=8,'slab_1'=8] {'mode_0','mode_1'}, dimensions={0} | all-to-all | bytes 524288 | tf_op jit(solution)/shard_map/all_to_all | solution.py:266
  71.5 2.6 %gram.1 = f32[8,32,128]{2,1,0:T(8,128)} custom-call(f32[64,1024]{1,0:T(8,128)} %bitcast.16, f32[1,1024]{1,0:T(1,128)} %bitcast.18, f32[16,1024]{1,0:T(8,128)} %bitcast.17), custom_call_target="tpu_custom_call" | custom-call | tf_op jit(solution)/shard_map/gram/pallas_call | solution.py:270
  74.1 13.8 %all_to_all.21.parts = f32[8,32,128]{2,1,0:T(8,128)} all-to-all(f32[8,32,128]{2,1,0:T(8,128)} %gram.1), channel_id=1, replica_groups=mesh['mode_0'=4,'mode_1'=2,'slab_0'=8,'slab_1'=8] {'slab_1'}, dimensions={0} | all-to-all | bytes 262144 | tf_op jit(solution)/shard_map/all_to_all | solution.py:273
  87.9 1.6 %total.1 = f32[8,32,128]{2,1,0:T(8,128)} custom-call(f32[8,32,128]{2,1,0:T(8,128)} %all_to_all.21.parts), custom_call_target="tpu_custom_call" | custom-call | tf_op jit(solution)/shard_map/total/pallas_call | solution.py:274
  89.5 0.0 copy-start.6
  89.5 19.6 %all_to_all.22.parts = f32[8,32,128]{2,1,0:T(8,128)} all-to-all(f32[8,32,128]{2,1,0:T(8,128)} %total.1), channel_id=1, replica_groups=mesh['mode_0'=4,'mode_1'=2,'slab_0'=8,'slab_1'=8] {'slab_0'}, dimensions={0} | all-to-all | bytes 262144 | tf_op jit(solution)/shard_map/all_to_all | solution.py:275
  109.1 3.3 %solve.1 = f32[64,128]{1,0:T(8,128)} custom-call(f32[8,32,128]{2,1,0:T(8,128)} %all_to_all.22.parts), custom_call_target="tpu_custom_call" | custom-call | tf_op jit(solution)/shard_map/solve/pallas_call | solution.py:276
  112.4 0.0 copy-done.6
  112.4 1.8 %convolution_add_fusion = f32[16,4,16,128]{3,0,2,1:T(8,128)S(1)} fusion(bf16[64,4,16,128]{3,2,1,0:T(8,128)(2,1)S(1)} %bitcast.15, bf16[16,4,16,128]{3,2,1,0:T(8,128)(2,1)S(1)} %copy-done.6, f32[64,128]{1,0:T(8,128)} %solve.1), kind=kOutput, calls=%fused_computation | convolution fusion | flops 100925440 | bytes 1867776 | tf_op jit(solution)/shard_map/dot_general | solution.py:286
  114.2 1.0 copy.20
  (2 shorter events, 0.0 us)
Async XLA Ops:
  2.5 9.5 %copy-start = (bf16[8,4,128,128]{3,2,1,0:T(8,128)(2,1)S(1)}, bf16[8,4,128,128]{3,2,1,0:T(8,128)(2,1)}, u32[]{:S(2)}) copy-start(bf16[8,4,128,128]{3,2,1,0:T(8,128)(2,1)} %modes.1) | copy-start | bytes 3145732
  2.5 27.8 %all-to-all-start = ((bf16[8,8,4,16,128]{4,3,2,1,0:T(8,128)(2,1)}), bf16[8,8,4,16,128]{4,3,2,1,0:T(8,128)(2,1)S(1)}, u32[]{:S(2)}, u32[]{:S(2)}) async-start(bf16[8,8,4,16,128]{4,3,2,1,0:T(8,128)(2,1)} %copy.17), calls=%async_computation | async-start | bytes 2097152 | tf_op jit(solution)/shard_map/all_to_all | solution.py:247
  12.0 2.9 %copy-start.2 = (f32[4,128,128]{2,1,0:T(8,128)S(1)}, f32[4,128,128]{2,1,0:T(8,128)}, u32[]{:S(2)}) copy-start(f32[4,128,128]{2,1,0:T(8,128)} %hs.1) | copy-start | bytes 786436
  12.1 13.6 %collective-permute-start.2 = (bf16[8,2,128,128]{3,2,1,0:T(8,128)(2,1)S(1)}, bf16[8,2,128,128]{3,2,1,0:T(8,128)(2,1)S(1)}, u32[]{:S(2)}, u32[]{:S(2)}) collective-permute-start(bf16[8,2,128,128]{3,2,1,0:T(8,128)(2,1)S(1)} %get-tuple-element.12), channel_id=1, source_target_pairs={{0,1},{1,2},{2,3},{3,4},{4,5},{5,6},{6,7},{7,8},{8,9},{9,10},{10,1... | collective-permute-start | bytes 1572872 | tf_op jit(solution)/shard_map/ppermute | solution.py:241
  13.4 1.5 %copy-start.1 = (f32[4,128,128]{2,1,0:T(8,128)S(1)}, f32[4,128,128]{2,1,0:T(8,128)}, u32[]{:S(2)}) copy-start(f32[4,128,128]{2,1,0:T(8,128)} %lc.1) | copy-start | bytes 786436
  13.4 16.8 %collective-permute-start.3 = (bf16[8,2,128,128]{3,2,1,0:T(8,128)(2,1)S(1)}, bf16[8,2,128,128]{3,2,1,0:T(8,128)(2,1)S(1)}, u32[]{:S(2)}, u32[]{:S(2)}) collective-permute-start(bf16[8,2,128,128]{3,2,1,0:T(8,128)(2,1)S(1)} %get-tuple-element.11), channel_id=1, source_target_pairs={{1,0},{2,1},{3,2},{4,3},{5,4},{6,5},{7,6},{8,7},{9,8},{10,9},{11,1... | collective-permute-start | bytes 1572872 | tf_op jit(solution)/shard_map/ppermute | solution.py:242
  15.7 16.6 %collective-permute-start = (f32[5,128,128]{2,1,0:T(8,128)}, f32[5,128,128]{2,1,0:T(8,128)S(1)}, u32[]{:S(2)}, u32[]{:S(2)}) collective-permute-start(f32[5,128,128]{2,1,0:T(8,128)} %pad_maximum_fusion), channel_id=1, source_target_pairs={{0,1},{1,2},{2,3},{3,4},{4,5},{5,6},{6,7},{7,8},{8,9},{9,10},{10,1... | collective-permute-start | bytes 983048 | tf_op jit(solution)/shard_map/ppermute | solution.py:243
  21.0 15.5 %collective-permute-start.1 = (f32[5,128,128]{2,1,0:T(8,128)}, f32[5,128,128]{2,1,0:T(8,128)}, u32[]{:S(2)}, u32[]{:S(2)}) collective-permute-start(f32[5,128,128]{2,1,0:T(8,128)} %pad_maximum_fusion.1), channel_id=1, source_target_pairs={{1,0},{2,1},{3,2},{4,3},{5,4},{6,5},{7,6},{8,7},{9,8},{10,9},{11,1... | collective-permute-start | bytes 983048 | tf_op jit(solution)/shard_map/ppermute | solution.py:244
  22.3 0.7 copy-start.7
  25.7 10.9 %copy-start.3 = (bf16[8,2,128,128]{3,2,1,0:T(8,128)(2,1)}, bf16[8,2,128,128]{3,2,1,0:T(8,128)(2,1)S(1)}, u32[]{:S(2)}) copy-start(bf16[8,2,128,128]{3,2,1,0:T(8,128)(2,1)S(1)} %collective-permute-done.2.mbefore) | copy-start | bytes 1572868
  30.3 6.3 %copy-start.4 = (bf16[8,2,128,128]{3,2,1,0:T(8,128)(2,1)}, bf16[8,2,128,128]{3,2,1,0:T(8,128)(2,1)S(1)}, u32[]{:S(2)}) copy-start(bf16[8,2,128,128]{3,2,1,0:T(8,128)(2,1)S(1)} %collective-permute-done.3.mafter) | copy-start | bytes 1572868
  32.3 4.3 %copy-start.5 = (f32[5,128,128]{2,1,0:T(8,128)}, f32[5,128,128]{2,1,0:T(8,128)S(1)}, u32[]{:S(2)}) copy-start(f32[5,128,128]{2,1,0:T(8,128)S(1)} %collective-permute-done.before) | copy-start | bytes 983044
  89.5 22.9 %copy-start.6 = (bf16[16,4,16,128]{3,2,1,0:T(8,128)(2,1)S(1)}, bf16[16,4,16,128]{3,2,1,0:T(8,128)(2,1)}, u32[]{:S(2)}) copy-start(bf16[16,4,16,128]{3,2,1,0:T(8,128)(2,1)} %param.13) | copy-start | bytes 786436

commit v2 on v1

v2 whole, which is shorter than its diff:
```python
import functools
import math

import jax
import jax.numpy as jnp
from jax import lax
from jax.experimental import pallas as pl
from jax.experimental.pallas import tpu as pltpu
from jax.sharding import Mesh
from jax.sharding import PartitionSpec as P

ITERS = 3
SLAB = ("slab_0", "slab_1")
MODE = ("mode_0", "mode_1")
STORAGE = 0.05
CZ = 4
NX = 128
NY = 128
LM = 8
OBS = 1024
MODES = 64
FIELDS = 16
ROWS = NX + 2
HI = lax.Precision.HIGHEST


def sweep_weights(count):
    order = []
    low, high = (0, count - 1)
    while low <= high:
        order.append(low)
        if high != low:
            order.append(high)
        low += 1
        high -= 1
    return [1.0 / (1.15 + 0.85 * math.cos((2 * i + 1) * math.pi / (2 * count))) for i in order]


W1, W2, W3 = sweep_weights(ITERS)
OWN2 = 1.0 - W2 + W2 / W1


def harmonic(a, b):
    return 2.0 * a * b / (a + b)


def at(ref, e, x):
    return ref[pl.ds(pl.multiple_of((e * ROWS + x) * LM, LM), LM), :]


def put(ref, e, x, value):
    ref[pl.ds(pl.multiple_of((e * ROWS + x) * LM, LM), LM), :] = value


def sweep(coef, ref, e, x):
    def c(i):
        return coef[i, e, pl.ds(x - 1, 1), :]

    u = at(ref, e, x)
    total = c(0) * at(ref, e - 1, x) + c(1) * at(ref, e + 1, x)
    total = total + (c(2) * at(ref, e, x - 1) + c(3) * at(ref, e, x + 1))
    total = total + (c(4) * pltpu.roll(u, 1, 1) + c(5) * pltpu.roll(u, NY - 1, 1))
    return u, total


def over_rows(planes, unroll, fn):
    first, step, count = planes
    pieces = NX // unroll

    def body(i, _):
        e = first + step * (i // pieces)
        start = (i % pieces) * unroll + 1
        for j in range(unroll):
            fn(e, start + j)
        return 0

    lax.fori_loop(0, count * pieces, body, 0)


def second_row(coef, u1, u2, e, x):
    u, total = sweep(coef, u1, e, x)
    put(u2, e, x, OWN2 * u + total)


def pick_block(pick, u3, first, out, slot):
    lanes = lax.broadcasted_iota(jnp.int32, (LM, NY), 1)
    acc = jnp.zeros((LM, NY), jnp.float32)
    for j in range(NY):
        p = pick[first + j]
        row = u3[lax.shift_right_logical(p, 7)]
        acc = jnp.where(lanes == j, pltpu.roll(row, p & 127, 1), acc)
    out[slot] = acc


def clear_edges(ref, e):
    zero = jnp.zeros((LM, NY), jnp.float32)
    put(ref, e, 0, zero)
    put(ref, e, ROWS - 1, zero)


def outer_kernel(edge, pick, lc, hs, before, after, modes, share, coef, u1, u2, u3):
    first = edge[0] == 0
    last = edge[1] == 0
    rows = lax.broadcasted_iota(jnp.int32, (NX, NY), 0)
    cols = lax.broadcasted_iota(jnp.int32, (NX, NY), 1)
    zero = jnp.zeros((LM, NY), jnp.float32)

    own = [jnp.exp(lc[z]) for z in range(CZ)]
    cond = [jnp.where(first, own[0], jnp.exp(before[NX * z : NX * z + NX])) for z in range(3)]
    cond += own
    cond += [jnp.where(last, own[CZ - 1], jnp.exp(after[NX * z : NX * z + NX])) for z in range(3)]
    faces = [harmonic(cond[z], cond[z + 1]) for z in range(9)]

    for e in range(8):
        c = cond[e + 1]
        lower = faces[e]
        upper = faces[e + 1]
        toward_e = jnp.where(rows == NX - 1, c, pltpu.roll(c, NX - 1, 0))
        east = harmonic(c, toward_e)
        west = jnp.where(rows == 0, harmonic(c, c), pltpu.roll(east, 1, 0))
        toward_n = jnp.where(cols == NY - 1, c, pltpu.roll(c, NY - 1, 1))
        north = harmonic(c, toward_n)
        south = jnp.where(cols == 0, harmonic(c, c), pltpu.roll(north, 1, 1))
        diag = STORAGE + lower + upper + west + east + south + north
        inv = 1.0 / diag
        scale = inv * W2
        if e == 1:
            scale = jnp.where(first, 0.0, scale)
        if e == 6:
            scale = jnp.where(last, 0.0, scale)
        coef[0, e] = lower * scale
        coef[1, e] = upper * scale
        if 1 <= e <= 6:
            coef[2, e] = jnp.where(rows == 0, 0.0, west * scale)
            coef[3, e] = jnp.where(rows == NX - 1, 0.0, east * scale)
            coef[4, e] = jnp.where(cols == 0, 0.0, south * scale)
            coef[5, e] = jnp.where(cols == NY - 1, 0.0, north * scale)
            clear_edges(u2, e)
        if 2 <= e <= 5:
            clear_edges(u1, e)
            lead = hs[e - 2] * c * inv * W1
            for k in range(LM):
                m = modes[k, e - 2].astype(jnp.float32)
                u1[pl.ds((e * ROWS + 1) * LM + k, NX, stride=LM), :] = m * lead

    def clear(i, _):
        for j in range(13):
            x = i * 13 + j
            put(u1, 1, x, zero)
            put(u1, 6, x, zero)
            put(u2, 0, x, zero)
            put(u2, 7, x, zero)
        return 0

    lax.fori_loop(0, ROWS // 13, clear, 0)
    for j in range(8):
        u3[8 * NX + j] = zero

    def c(i, e, x):
        return coef[i, e, pl.ds(x - 1, 1), :]

    def end_two(e, x):
        put(u2, 1, x, c(1, 1, x) * at(u1, 2, x))
        put(u2, 6, x, c(0, 6, x) * at(u1, 5, x))

    over_rows((0, 0, 1), 16, end_two)
    over_rows((2, 3, 2), 64, functools.partial(second_row, coef, u1, u2))

    def end_three(e, x):
        u3[x - 1] = (W3 / W2) * (c(1, 0, x) * at(u2, 1, x))
        u3[7 * NX + x - 1] = (W3 / W2) * (c(0, 7, x) * at(u2, 6, x))

    over_rows((0, 0, 1), 16, end_three)

    def third(e, x):
        u, total = sweep(coef, u2, e, x)
        u3[e * NX + x - 1] = (1.0 - W3) * u + (W3 / W2) * total

    over_rows((1, 5, 2), 64, third)

    def block(b, _):
        pick_block(pick, u3, b * NY, share, b)
        return 0

    lax.fori_loop(0, 16, block, 0)


def inner_kernel(pick, coef, u1, u2, out, w2, u3):
    def second(e, x):
        u, total = sweep(coef, u1, e, x)
        put(w2, e - 2, x, OWN2 * u + total)

    clear_edges(w2, 1)
    clear_edges(w2, 2)
    over_rows((3, 1, 2), 64, second)

    def third(e, x, here, below, above):
        def c(i):
            return coef[i, e, pl.ds(x - 1, 1), :]

        u = here(x)
        total = c(0) * below(x) + c(1) * above(x)
        total = total + (c(2) * here(x - 1) + c(3) * here(x + 1))
        total = total + (c(4) * pltpu.roll(u, 1, 1) + c(5) * pltpu.roll(u, NY - 1, 1))
        value = (1.0 - W3) * u + (W3 / W1) * at(u1, e, x) + (W3 / W2) * total
        u3[(e - 2) * NX + x - 1] = value

    def plane(ref, e):
        return lambda x: at(ref, e, x)

    lines = {e: plane(u2, e) for e in (1, 2, 5, 6)}
    lines.update({e: plane(w2, e - 2) for e in (3, 4)})
    for q in range(4):
        over_rows(
            (q + 2, 0, 1),
            64,
            lambda e, x, q=q: third(q + 2, x, lines[q + 2], lines[q + 1], lines[q + 3]),
        )

    def block(b, _):
        pick_block(pick, u3, b * NY, out, b)
        return 0

    lax.fori_loop(0, 8, block, 0)


def gram_kernel(resp, var, misfit, out):
    r = resp[...]
    scaled = r / var[...]
    mis = misfit[...]
    half = MODES // 2
    none = jnp.zeros((half, OBS), jnp.float32)
    none_f = jnp.zeros((FIELDS, OBS), jnp.float32)
    right_a = jnp.concatenate([r, none, mis, none_f], axis=0)
    right_b = jnp.concatenate([none, none, r[half:], none_f, mis], axis=0)
    dims = (((1,), (1,)), ((), ()))
    got = lax.dot_general(scaled[:half], right_a, dims, precision=HI, preferred_element_type=jnp.float32)
    got = got + lax.dot_general(
        scaled[half:], right_b, dims, precision=HI, preferred_element_type=jnp.float32
    )
    for d in range(8):
        out[d] = got


def total_kernel(parts, out):
    got = parts[0]
    for d in range(1, 8):
        got = got + parts[d]
    for d in range(8):
        out[d] = got


def solve_kernel(parts, out):
    p = parts[0]
    for d in range(1, 8):
        p = p + parts[d]
    half = MODES // 2
    lane = lax.broadcasted_iota(jnp.int32, (half, 128), 1)
    square = jnp.concatenate([p, jnp.zeros((128 - half, 128), jnp.float32)], axis=0)
    turned = square.T[half : 2 * half]
    near = pltpu.roll(p, 128 - 32, 1)
    far = pltpu.roll(p, 128 - 48, 1)
    top = jnp.where(lane < 64, p, near)
    low = jnp.where(lane < 32, turned, jnp.where(lane < 64, near, far))
    a = jnp.concatenate([top, low], axis=0)
    row = lax.broadcasted_iota(jnp.int32, (MODES, 128), 0)
    col = lax.broadcasted_iota(jnp.int32, (MODES, 128), 1)
    a = jnp.where(row == col, a + 1.0, a)
    a = [a[8 * i : 8 * i + 8] for i in range(8)]
    sub = lax.broadcasted_iota(jnp.int32, (8, 128), 0)

    def wide(v):
        return jnp.broadcast_to(v, (8, 128))

    for q in range(8):
        cs = [[wide(a[i][:, 8 * q + t : 8 * q + t + 1]) for i in range(8)] for t in range(8)]
        for t in range(8):
            c = cs[t]
            inv = 1.0 / wide(c[q][t : t + 1])
            norm = wide(a[q][t : t + 1]) * inv
            for i in range(8):
                new = a[i] - c[i] * norm
                a[i] = jnp.where(sub == t, norm, new) if i == q else new
            for s in range(t + 1, 8):
                f = wide(c[q][s : s + 1]) * inv
                for i in range(8):
                    new = cs[s][i] - c[i] * f
                    cs[s][i] = jnp.where(sub == t, f, new) if i == q else new
    for i in range(8):
        out[8 * i : 8 * i + 8, :] = a[i]


def vmem(n):
    return [pl.BlockSpec(memory_space=pltpu.VMEM)] * n


def smem(n):
    return [pl.BlockSpec(memory_space=pltpu.SMEM)] * n


def limit(mib):
    return pltpu.CompilerParams(vmem_limit_bytes=mib * 1024 * 1024)


def on_device(log_cond, head_slope, modes, obs_cells, obs_var, misfit, base_fields):
    slabs = lax.axis_size(SLAB)
    slab = lax.axis_index(SLAB)
    ahead = [(i, i + 1) for i in range(slabs - 1)]
    back = [(i + 1, i) for i in range(slabs - 1)]

    cells = obs_cells.astype(jnp.float32).reshape(8, NY)
    upward = jnp.concatenate([log_cond[1:4].reshape(3 * NX, NY), cells])
    downward = jnp.concatenate([log_cond[0:3].reshape(3 * NX, NY), cells])
    before = lax.ppermute(upward, SLAB, ahead)
    after = lax.ppermute(downward, SLAB, back)

    pieces = jnp.moveaxis(modes.reshape(LM, CZ, 8, NX // 8, NY), 2, 0)
    block = lax.all_to_all(pieces, MODE, 0, 0, tiled=True)

    edge = jnp.stack([slab, slabs - 1 - slab]).astype(jnp.int32)
    place = jnp.arange(OBS, dtype=jnp.int32)

    def address(where, shift, low, high):
        plane = where >> 14
        row = jnp.where((plane >= low) & (plane <= high), (where >> 7) + shift * NX, 8 * NX)
        return (row << 7) | ((place - where) & 127)

    def arrived(x):
        return x[3 * NX :].astype(jnp.int32).reshape(OBS)

    far_pick = jnp.concatenate([address(arrived(before), -2, 2, 3), address(arrived(after), 6, 0, 1)])
    near_pick = address(obs_cells, 0, 0, 3)
    plane_rows = jax.ShapeDtypeStruct((8 * ROWS * LM, NY), jnp.float32)
    share, coefs, u1, u2 = pl.pallas_call(
        outer_kernel,
        out_shape=(
            jax.ShapeDtypeStruct((16, LM, NY), jnp.float32),
            jax.ShapeDtypeStruct((6, 8, NX, NY), jnp.float32),
            plane_rows,
            plane_rows,
        ),
        in_specs=smem(2) + vmem(5),
        out_specs=vmem(4),
        scratch_shapes=[pltpu.VMEM((8 * NX + 8, LM, NY), jnp.float32)],
        compiler_params=limit(24),
        name="outer",
    )(edge, far_pick, log_cond, head_slope, before, after, modes)
    from_above = lax.ppermute(share[:8], SLAB, back)
    from_below = lax.ppermute(share[8:], SLAB, ahead)
    picked = pl.pallas_call(
        inner_kernel,
        out_shape=jax.ShapeDtypeStruct((8, LM, NY), jnp.float32),
        in_specs=smem(1) + vmem(3),
        out_specs=vmem(1)[0],
        scratch_shapes=[
            pltpu.VMEM((4 * ROWS * LM, NY), jnp.float32),
            pltpu.VMEM((4 * NX + 8, LM, NY), jnp.float32),
        ],
        compiler_params=limit(24),
        name="inner",
    )(near_pick, coefs, u1, u2)
    block, from_above, from_below = lax.optimization_barrier((block, from_above, from_below))
    picked = picked + from_above + from_below
    copies = jnp.broadcast_to(picked, (8, 8, LM, NY))
    whole = lax.all_to_all(copies, MODE, 0, 0, tiled=True)
    whole = jnp.moveaxis(whole, 1, 2).reshape(MODES, OBS)

    shared = jax.ShapeDtypeStruct((8, 32, 128), jnp.float32)
    part = pl.pallas_call(gram_kernel, out_shape=shared, in_specs=vmem(3), out_specs=vmem(1)[0], compiler_params=limit(6), name="gram")(
        whole, obs_var.reshape(1, OBS), misfit.T
    )
    part = lax.all_to_all(part, "slab_1", 0, 0, tiled=True)
    part = pl.pallas_call(total_kernel, out_shape=shared, in_specs=vmem(1), out_specs=vmem(1)[0], compiler_params=limit(4), name="total")(part)
    part = lax.all_to_all(part, "slab_0", 0, 0, tiled=True)
    solved = pl.pallas_call(
        solve_kernel,
        out_shape=jax.ShapeDtypeStruct((MODES, 128), jnp.float32),
        in_specs=vmem(1),
        out_specs=vmem(1)[0],
        compiler_params=limit(4),
        name="solve",
    )(part)
    coef = solved[:, MODES : MODES + FIELDS]

    layer = block.reshape(MODES, CZ, NX // 8, NY).astype(jnp.float32)
    update = lax.dot_general(coef, layer, (((0,), (0,)), ((), ())), precision=HI)
    return base_fields.astype(jnp.float32) + update


def solution(mesh):
    torus = Mesh(mesh.devices.reshape(4, 2, 8, 8), ("mode_0", "mode_1", "slab_0", "slab_1"))
    in_specs = (
        P(SLAB, None, None),
        P(SLAB, None, None),
        P(MODE, SLAB, None, None),
        P(SLAB),
        P(SLAB),
        P(SLAB, None),
        P(None, SLAB, MODE, None),
    )
    out_specs = P(None, SLAB, MODE, None)
    return jax.shard_map(
        on_device, mesh=torus, in_specs=in_specs, out_specs=out_specs, check_vma=False
    )
```

time: 116 us -> 88 us (0.76)
  Pallas kernels: 31.4 us -> 16.5 us
  waiting for transfers between devices: 13 us -> 0.01 us
  starting transfers between devices: 18.1 us -> 21 us
  other arithmetic: 2.63 us -> 0.9 us
  blocking collectives: 44.4 us -> 43.2 us
    ppermute x4, waiting for transfers between devices: 13 us -> 0.01 us  [the longest x1 0.01 us: on_device(): from_above = lax.ppermute(share[:8], SLAB, back)]
    pallas_call x1 -> x2, Pallas kernels: 24 us -> 13.8 us  [the longest x1 8.41 us: on_device(): pl.pallas_call(outer_kernel, out_shape=(jax.ShapeDtypeStruct((16, LM, NY)...]
    ppermute x4, starting transfers between devices: 8.58 us -> 11.7 us  [the longest x1 4.56 us: on_device(): before = lax.ppermute(upward, SLAB, ahead)]
    pallas_call x1, Pallas kernels: 2.56 us -> 0.91 us  [on_device(): pl.pallas_call(gram_kernel, out_shape=shared, in_specs=vmem(3), out_specs...]
    pallas_call x1, Pallas kernels: 1.58 us -> 0.02 us  [on_device(): pl.pallas_call(total_kernel, out_shape=shared, in_specs=vmem(1), out_spec...]
    pallas_call x1, Pallas kernels: 3.3 us -> 1.75 us  [on_device(): pl.pallas_call(solve_kernel, out_shape=jax.ShapeDtypeStruct((MODES, 128),...]
    concatenate x2, other arithmetic: 1.49 us -> 0.03 us  [the longest x1 0.03 us: on_device(): upward = jnp.concatenate([log_cond[1:4].reshape(3 * NX, NY), cells])]
  transfers between devices with their start and end apart: 5 -> 5, of which waited for: 4 -> 0; matrix products, arithmetic and copies ran while one was open for 2% -> 3% of each run, Pallas kernels for 0% -> 16%
where the time goes in v2:
time: 88 us; the launch traced here: 87.6 us
  blocking collectives  43.2 us (49%)
  starting transfers between devices  21 us (24%)
  Pallas kernels  16.5 us (19%)
  local copies, waits for them, and re-layouts  4.68 us (5%)
  matrix products  1.07 us (1%)
  other arithmetic  0.9 us (1%)
    all_to_all x1, blocking collectives, on_device(): part = lax.all_to_all(part, 'slab_0', 0, 0, tiled=True)  19.2 us
    all_to_all x1, blocking collectives, on_device(): part = lax.all_to_all(part, 'slab_1', 0, 0, tiled=True)  13.3 us
    all_to_all x1, blocking collectives, on_device(): whole = lax.all_to_all(copies, MODE, 0, 0, tiled=True)  10.7 us
    all_to_all x1, starting transfers between devices, on_device(): block = lax.all_to_all(pieces, MODE, 0, 0, tiled=True)  9.34 us
    pallas_call x1, Pallas kernels, on_device(): pl.pallas_call(outer_kernel, out_shape=(jax.ShapeDtypeStruct((16, LM, NY)...  8.41 us
    pallas_call x1, Pallas kernels, on_device(): pl.pallas_call(inner_kernel, out_shape=jax.ShapeDtypeStruct((8, LM, NY),...  5.43 us
    ppermute x1, starting transfers between devices, on_device(): before = lax.ppermute(upward, SLAB, ahead)  4.56 us
    ppermute x1, starting transfers between devices, on_device(): from_below = lax.ppermute(share[8:], SLAB, ahead)  4.55 us
  transfers between devices with their start and end apart: 5, of which 0 were waited for; matrix products, arithmetic and copies ran while one was open for 3% of the time, Pallas kernels for 16%

profile of v2, /device:TPU:2, one launch (start us, length us, event | category | flops | bytes accessed | tf_op | source)
XLA Modules:
  0.0 87.6 jit_solution(9549017592114373667)
XLA Ops:
  0.0 0.0 copy-start.1
  0.0 0.0 copy-start
  0.0 0.0 copy-start.2
  0.0 1.2 %fusion.3 = (f32[3,128,128]{2,1,0:T(8,128)S(1)}, f32[3,128,128]{2,1,0:T(8,128)S(1)}) fusion(f32[4,128,128]{2,1,0:T(8,128)} %lc.1), kind=kLoop, calls=%fused_computation.16 | loop fusion | bytes 786432 | tf_op jit(solution)/shard_map/slice | solution.py:312
  1.2 0.8 and_or_fusion.2
  2.0 1.3 %collective-permute-start.1 = (f32[392,128]{1,0:T(8,128)S(1)}, f32[392,128]{1,0:T(8,128)S(1)}, u32[]{:S(2)}, u32[]{:S(2)}) collective-permute-start(f32[392,128]{1,0:T(8,128)S(1)} %get-tuple-element.26), channel_id=1, source_target_pairs={{1,0},{2,1},{3,2},{4,3},{5,4},{6,5},{7,6},{8,7},{9,8},{10,9},{11,1... | collective-permute-start | bytes 602120 | tf_op jit(solution)/shard_map/ppermute | solution.py:315
  3.3 4.6 %collective-permute-start = (f32[392,128]{1,0:T(8,128)S(1)}, f32[392,128]{1,0:T(8,128)S(1)}, u32[]{:S(2)}, u32[]{:S(2)}) collective-permute-start(f32[392,128]{1,0:T(8,128)S(1)} %get-tuple-element.25), channel_id=1, source_target_pairs={{0,1},{1,2},{2,3},{3,4},{4,5},{5,6},{6,7},{7,8},{8,9},{9,10},{10,1... | collective-permute-start | bytes 602120 | tf_op jit(solution)/shard_map/ppermute | solution.py:314
  7.8 2.5 %copy.17 = bf16[8,8,4,16,128]{4,3,2,1,0:T(8,128)(2,1)} copy(bf16[8,8,4,16,128]{4,3,0,2,1:T(8,128)(2,1)} %bitcast.26) | data formatting | bytes 2097152 | tf_op jit(solution)/shard_map/transpose | solution.py:317
  10.4 9.3 %all-to-all-start = ((bf16[8,8,4,16,128]{4,3,2,1,0:T(8,128)(2,1)}), bf16[8,8,4,16,128]{4,3,2,1,0:T(8,128)(2,1)S(1)}, u32[]{:S(2)}, u32[]{:S(2)}) async-start(bf16[8,8,4,16,128]{4,3,2,1,0:T(8,128)(2,1)} %copy.17), calls=%async_computation | async-start | bytes 2097152 | tf_op jit(solution)/shard_map/all_to_all | solution.py:318
  19.7 0.1 pad_add_fusion.1.edge
  19.8 0.0 collective-permute-done.1.after
  19.8 0.0 collective-permute-done.before
  19.8 0.0 copy-done.1
  19.8 0.0 copy-done
  19.8 0.0 copy-done.2
  19.9 8.4 %outer.1 = (f32[16,8,128]{2,1,0:T(8,128)S(1)}, f32[6,8,128,128]{3,2,1,0:T(8,128)S(1)}, f32[8320,128]{1,0:T(8,128)S(1)}, f32[8320,128]{1,0:T(8,128)S(1)}) custom-call(s32[2]{0:T(128)S(1)} %pad_add_fusion.1.edge, s32[2048]{0:T(1024)S(1)} %pad_add_fusion.pick, f32[4,128,128]{2,1,0:T(8,128)S(1)} %copy-done.1, f32[4,128,128]{2,1,0:T(8,128)S(1)} %copy-done.2, ...), custom_call_target="tpu_custom_call" | custom-call | tf_op jit(solution)/shard_map/outer/pallas_call | solution.py:334
  28.3 1.3 %collective-permute-start.2 = (f32[8,8,128]{2,1,0:T(8,128)S(1)}, f32[8,8,128]{2,1,0:T(8,128)S(1)}, u32[]{:S(2)}, u32[]{:S(2)}) collective-permute-start(f32[8,8,128]{2,1,0:T(8,128)S(1)} %get-tuple-element.22), channel_id=1, source_target_pairs={{1,0},{2,1},{3,2},{4,3},{5,4},{6,5},{7,6},{8,7},{9,8},{10,9},{11,1... | collective-permute-start | bytes 98312 | tf_op jit(solution)/shard_map/ppermute | solution.py:348
  29.6 4.5 %collective-permute-start.3 = (f32[8,8,128]{2,1,0:T(8,128)S(1)}, f32[8,8,128]{2,1,0:T(8,128)S(1)}, u32[]{:S(2)}, u32[]{:S(2)}) collective-permute-start(f32[8,8,128]{2,1,0:T(8,128)S(1)} %get-tuple-element.21), channel_id=1, source_target_pairs={{0,1},{1,2},{2,3},{3,4},{4,5},{5,6},{6,7},{7,8},{8,9},{9,10},{10,1... | collective-permute-start | bytes 98312 | tf_op jit(solution)/shard_map/ppermute | solution.py:349
  34.1 0.0 copy-start.3
  34.1 0.0 copy-start.4
  34.1 0.0 copy-start.5
  34.2 5.4 %inner.1 = f32[8,8,128]{2,1,0:T(8,128)S(1)} custom-call(s32[1024]{0:T(1024)S(1)} %get-tuple-element.23.pick, f32[6,8,128,128]{3,2,1,0:T(8,128)S(1)} %get-tuple-element.12.coef, f32[8320,128]{1,0:T(8,128)S(1)} %get-tuple-element.13.u1, f32[8320,128]{1,0:T(8,128)S(1)} %get-tuple-element.14.u2), custom_call_target="tpu_custom_call" | custom-call | tf_op jit(solution)/shard_map/inner/pallas_call | solution.py:350
  39.6 0.0 collective-permute-done.2
  39.6 0.0 collective-permute-done.3
  39.6 0.0 all-to-all-done
  39.7 10.7 %all_to_all.20 = f32[8,8,8,128]{3,2,1,0:T(8,128)S(1)} all-to-all(f32[8,8,8,128]{3,2,1,0:T(8,128)S(1)} %broadcast_in_dim.10), channel_id=1, replica_groups=mesh['mode_0'=4,'mode_1'=2,'slab_0'=8,'slab_1'=8] {'mode_0','mode_1'}, dimensions={0} | all-to-all | bytes 524288 | tf_op jit(solution)/shard_map/all_to_all | solution.py:365
  50.3 0.0 copy-done.3
  50.3 0.0 copy-done.4
  50.3 0.9 %gram.1 = f32[8,32,128]{2,1,0:T(8,128)S(1)} custom-call(f32[64,1024]{1,0:T(8,128)S(1)} %bitcast.27, f32[1,1024]{1,0:T(1,128)S(1)} %bitcast.29, f32[16,1024]{1,0:T(8,128)S(1)} %bitcast.28), custom_call_target="tpu_custom_call" | custom-call | tf_op jit(solution)/shard_map/gram/pallas_call | solution.py:369
  51.3 13.3 %all_to_all.21.parts = f32[8,32,128]{2,1,0:T(8,128)S(1)} all-to-all(f32[8,32,128]{2,1,0:T(8,128)S(1)} %gram.1), channel_id=1, replica_groups=mesh['mode_0'=4,'mode_1'=2,'slab_0'=8,'slab_1'=8] {'slab_1'}, dimensions={0} | all-to-all | bytes 262144 | tf_op jit(solution)/shard_map/all_to_all | solution.py:372
  64.6 19.2 %all_to_all.22.parts = f32[8,32,128]{2,1,0:T(8,128)S(1)} all-to-all(f32[8,32,128]{2,1,0:T(8,128)S(1)} %total.1), channel_id=1, replica_groups=mesh['mode_0'=4,'mode_1'=2,'slab_0'=8,'slab_1'=8] {'slab_0'}, dimensions={0} | all-to-all | bytes 262144 | tf_op jit(solution)/shard_map/all_to_all | solution.py:374
  83.8 1.8 %solve.1 = f32[64,128]{1,0:T(8,128)S(1)} custom-call(f32[8,32,128]{2,1,0:T(8,128)S(1)} %all_to_all.22.parts), custom_call_target="tpu_custom_call" | custom-call | tf_op jit(solution)/shard_map/solve/pallas_call | solution.py:375
  85.5 0.0 copy-done.5
  85.5 1.1 %convolution_add_fusion = f32[16,4,16,128]{3,0,2,1:T(8,128)S(1)} fusion(bf16[64,4,16,128]{3,2,1,0:T(8,128)(2,1)S(1)} %bitcast.30, bf16[16,4,16,128]{3,2,1,0:T(8,128)(2,1)S(1)} %copy-done.5, f32[64,128]{1,0:T(8,128)S(1)} %solve.1), kind=kOutput, calls=%fused_computation | convolution fusion | flops 100925440 | bytes 1867776 | tf_op jit(solution)/shard_map/dot_general | solution.py:386
  86.6 1.0 %copy.20 = f32[16,4,16,128]{3,2,1,0:T(8,128)} copy(f32[16,4,16,128]{3,0,2,1:T(8,128)S(1)} %convolution_add_fusion) | data formatting | bytes 1048576 | tf_op jit(solution)/shard_map/add | solution.py:387
  (8 shorter events, 0.1 us)
Async XLA Ops:
  0.0 19.8 %copy-start.1 = (f32[4,128,128]{2,1,0:T(8,128)S(1)}, f32[4,128,128]{2,1,0:T(8,128)}, u32[]{:S(2)}) copy-start(f32[4,128,128]{2,1,0:T(8,128)} %lc.1) | copy-start | bytes 786436
  0.0 19.8 %copy-start = (bf16[8,4,128,128]{3,2,1,0:T(8,128)(2,1)S(1)}, bf16[8,4,128,128]{3,2,1,0:T(8,128)(2,1)}, u32[]{:S(2)}) copy-start(bf16[8,4,128,128]{3,2,1,0:T(8,128)(2,1)} %modes.1) | copy-start | bytes 3145732
  0.0 19.8 %copy-start.2 = (f32[4,128,128]{2,1,0:T(8,128)S(1)}, f32[4,128,128]{2,1,0:T(8,128)}, u32[]{:S(2)}) copy-start(f32[4,128,128]{2,1,0:T(8,128)} %hs.1) | copy-start | bytes 786436
  2.0 17.8 %collective-permute-start.1 = (f32[392,128]{1,0:T(8,128)S(1)}, f32[392,128]{1,0:T(8,128)S(1)}, u32[]{:S(2)}, u32[]{:S(2)}) collective-permute-start(f32[392,128]{1,0:T(8,128)S(1)} %get-tuple-element.26), channel_id=1, source_target_pairs={{1,0},{2,1},{3,2},{4,3},{5,4},{6,5},{7,6},{8,7},{9,8},{10,9},{11,1... | collective-permute-start | bytes 602120 | tf_op jit(solution)/shard_map/ppermute | solution.py:315
  3.3 16.5 %collective-permute-start = (f32[392,128]{1,0:T(8,128)S(1)}, f32[392,128]{1,0:T(8,128)S(1)}, u32[]{:S(2)}, u32[]{:S(2)}) collective-permute-start(f32[392,128]{1,0:T(8,128)S(1)} %get-tuple-element.25), channel_id=1, source_target_pairs={{0,1},{1,2},{2,3},{3,4},{4,5},{5,6},{6,7},{7,8},{8,9},{9,10},{10,1... | collective-permute-start | bytes 602120 | tf_op jit(solution)/shard_map/ppermute | solution.py:314
  10.4 29.3 %all-to-all-start = ((bf16[8,8,4,16,128]{4,3,2,1,0:T(8,128)(2,1)}), bf16[8,8,4,16,128]{4,3,2,1,0:T(8,128)(2,1)S(1)}, u32[]{:S(2)}, u32[]{:S(2)}) async-start(bf16[8,8,4,16,128]{4,3,2,1,0:T(8,128)(2,1)} %copy.17), calls=%async_computation | async-start | bytes 2097152 | tf_op jit(solution)/shard_map/all_to_all | solution.py:318
  28.3 11.3 %collective-permute-start.2 = (f32[8,8,128]{2,1,0:T(8,128)S(1)}, f32[8,8,128]{2,1,0:T(8,128)S(1)}, u32[]{:S(2)}, u32[]{:S(2)}) collective-permute-start(f32[8,8,128]{2,1,0:T(8,128)S(1)} %get-tuple-element.22), channel_id=1, source_target_pairs={{1,0},{2,1},{3,2},{4,3},{5,4},{6,5},{7,6},{8,7},{9,8},{10,9},{11,1... | collective-permute-start | bytes 98312 | tf_op jit(solution)/shard_map/ppermute | solution.py:348
  29.6 10.0 %collective-permute-start.3 = (f32[8,8,128]{2,1,0:T(8,128)S(1)}, f32[8,8,128]{2,1,0:T(8,128)S(1)}, u32[]{:S(2)}, u32[]{:S(2)}) collective-permute-start(f32[8,8,128]{2,1,0:T(8,128)S(1)} %get-tuple-element.21), channel_id=1, source_target_pairs={{0,1},{1,2},{2,3},{3,4},{4,5},{5,6},{6,7},{7,8},{8,9},{9,10},{10,1... | collective-permute-start | bytes 98312 | tf_op jit(solution)/shard_map/ppermute | solution.py:349
  34.1 16.2 %copy-start.3 = (f32[1024,16]{0,1:T(8,128)S(1)}, f32[1024,16]{0,1:T(8,128)}, u32[]{:S(2)}) copy-start(f32[1024,16]{0,1:T(8,128)} %param.12) | copy-start | bytes 196612
  34.1 16.2 %copy-start.4 = (f32[1024]{0:T(1024)S(1)}, f32[1024]{0:T(1024)}, u32[]{:S(2)}) copy-start(f32[1024]{0:T(1024)} %param.11) | copy-start | bytes 12292
  34.1 51.4 %copy-start.5 = (bf16[16,4,16,128]{3,2,1,0:T(8,128)(2,1)S(1)}, bf16[16,4,16,128]{3,2,1,0:T(8,128)(2,1)}, u32[]{:S(2)}) copy-start(bf16[16,4,16,128]{3,2,1,0:T(8,128)(2,1)} %param.13) | copy-start | bytes 786436

commit v3 on v2

--- a/solution.py
+++ b/solution.py
@@ -82,20 +82,41 @@
     put(u2, e, x, OWN2 * u + total)
 
 
-def pick_block(pick, u3, first, out, slot):
+def pick_block(pick, u3, b, out):
     lanes = lax.broadcasted_iota(jnp.int32, (LM, NY), 1)
     acc = jnp.zeros((LM, NY), jnp.float32)
     for j in range(NY):
-        p = pick[first + j]
-        row = u3[lax.shift_right_logical(p, 7)]
+        p = pick[b, j]
+        row = u3[pl.ds(pl.multiple_of(lax.shift_right_logical(p, 7), LM), LM), :]
         acc = jnp.where(lanes == j, pltpu.roll(row, p & 127, 1), acc)
-    out[slot] = acc
+    out[b] = acc
+
+
+def put_row(ref, row, value):
+    ref[pl.ds(pl.multiple_of(row * LM, LM), LM), :] = value
 
 
 def clear_edges(ref, e):
     zero = jnp.zeros((LM, NY), jnp.float32)
     put(ref, e, 0, zero)
     put(ref, e, ROWS - 1, zero)
+
+
+def address(where, place, shift, low, high):
+    plane = where >> 14
+    row = jnp.where((plane >= low) & (plane <= high), (where >> 7) + shift * NX, 8 * NX)
+    return (row << 10) | ((place - where) & 127)
+
+
+def pack_kernel(lc, cells, upward, downward, near):
+    for z in range(3):
+        upward[NX * z : NX * z + NX] = lc[z + 1]
+        downward[NX * z : NX * z + NX] = lc[z]
+    where = cells[...]
+    upward[3 * NX :] = where.astype(jnp.float32)
+    downward[3 * NX :] = where.astype(jnp.float32)
+    place = lax.broadcasted_iota(jnp.int32, (8, NY), 1)
+    near[...] = address(where, place, 0, 0, 3)
 
 
 def outer_kernel(edge, pick, lc, hs, before, after, modes, share, coef, u1, u2, u3):
@@ -117,10 +138,10 @@
         upper = faces[e + 1]
         toward_e = jnp.where(rows == NX - 1, c, pltpu.roll(c, NX - 1, 0))
         east = harmonic(c, toward_e)
-        west = jnp.where(rows == 0, harmonic(c, c), pltpu.roll(east, 1, 0))
+        west = jnp.where(rows == 0, c, pltpu.roll(east, 1, 0))
         toward_n = jnp.where(cols == NY - 1, c, pltpu.roll(c, NY - 1, 1))
         north = harmonic(c, toward_n)
-        south = jnp.where(cols == 0, harmonic(c, c), pltpu.roll(north, 1, 1))
+        south = jnp.where(cols == 0, c, pltpu.roll(north, 1, 1))
         diag = STORAGE + lower + upper + west + east + south + north
         inv = 1.0 / diag
         scale = inv * W2
@@ -154,7 +175,7 @@
 
     lax.fori_loop(0, ROWS // 13, clear, 0)
     for j in range(8):
-        u3[8 * NX + j] = zero
+        put_row(u3, 8 * NX + j, zero)
 
     def c(i, e, x):
         return coef[i, e, pl.ds(x - 1, 1), :]
@@ -167,19 +188,19 @@
     over_rows((2, 3, 2), 64, functools.partial(second_row, coef, u1, u2))
 
     def end_three(e, x):
-        u3[x - 1] = (W3 / W2) * (c(1, 0, x) * at(u2, 1, x))
-        u3[7 * NX + x - 1] = (W3 / W2) * (c(0, 7, x) * at(u2, 6, x))
+        put_row(u3, x - 1, (W3 / W2) * (c(1, 0, x) * at(u2, 1, x)))
+        put_row(u3, 7 * NX + x - 1, (W3 / W2) * (c(0, 7, x) * at(u2, 6, x)))
 
     over_rows((0, 0, 1), 16, end_three)
 
     def third(e, x):
         u, total = sweep(coef, u2, e, x)
-        u3[e * NX + x - 1] = (1.0 - W3) * u + (W3 / W2) * total
+        put_row(u3, e * NX + x - 1, (1.0 - W3) * u + (W3 / W2) * total)
 
     over_rows((1, 5, 2), 64, third)
 
     def block(b, _):
-        pick_block(pick, u3, b * NY, share, b)
+        pick_block(pick, u3, b, share)
         return 0
 
     lax.fori_loop(0, 16, block, 0)
@@ -203,7 +224,7 @@
         total = total + (c(2) * here(x - 1) + c(3) * here(x + 1))
         total = total + (c(4) * pltpu.roll(u, 1, 1) + c(5) * pltpu.roll(u, NY - 1, 1))
         value = (1.0 - W3) * u + (W3 / W1) * at(u1, e, x) + (W3 / W2) * total
-        u3[(e - 2) * NX + x - 1] = value
+        put_row(u3, (e - 2) * NX + x - 1, value)
 
     def plane(ref, e):
         return lambda x: at(ref, e, x)
@@ -218,7 +239,7 @@
         )
 
     def block(b, _):
-        pick_block(pick, u3, b * NY, out, b)
+        pick_block(pick, u3, b, out)
         return 0
 
     lax.fori_loop(0, 8, block, 0)
@@ -308,9 +329,15 @@
     ahead = [(i, i + 1) for i in range(slabs - 1)]
     back = [(i + 1, i) for i in range(slabs - 1)]
 
-    cells = obs_cells.astype(jnp.float32).reshape(8, NY)
-    upward = jnp.concatenate([log_cond[1:4].reshape(3 * NX, NY), cells])
-    downward = jnp.concatenate([log_cond[0:3].reshape(3 * NX, NY), cells])
+    message = jax.ShapeDtypeStruct((3 * NX + 8, NY), jnp.float32)
+    upward, downward, near_pick = pl.pallas_call(
+        pack_kernel,
+        out_shape=(message, message, jax.ShapeDtypeStruct((8, NY), jnp.int32)),
+        in_specs=vmem(2),
+        out_specs=vmem(3),
+        compiler_params=limit(4),
+        name="pack",
+    )(log_cond, obs_cells.reshape(8, NY))
     before = lax.ppermute(upward, SLAB, ahead)
     after = lax.ppermute(downward, SLAB, back)
 
@@ -318,18 +345,14 @@
     block = lax.all_to_all(pieces, MODE, 0, 0, tiled=True)
 
     edge = jnp.stack([slab, slabs - 1 - slab]).astype(jnp.int32)
-    place = jnp.arange(OBS, dtype=jnp.int32)
-
-    def address(where, shift, low, high):
-        plane = where >> 14
-        row = jnp.where((plane >= low) & (plane <= high), (where >> 7) + shift * NX, 8 * NX)
-        return (row << 7) | ((place - where) & 127)
+    place = lax.broadcasted_iota(jnp.int32, (8, NY), 1)
 
     def arrived(x):
-        return x[3 * NX :].astype(jnp.int32).reshape(OBS)
-
-    far_pick = jnp.concatenate([address(arrived(before), -2, 2, 3), address(arrived(after), 6, 0, 1)])
-    near_pick = address(obs_cells, 0, 0, 3)
+        return x[3 * NX :].astype(jnp.int32)
+
+    far_pick = jnp.concatenate(
+        [address(arrived(before), place, -2, 2, 3), address(arrived(after), place, 6, 0, 1)]
+    )
     plane_rows = jax.ShapeDtypeStruct((8 * ROWS * LM, NY), jnp.float32)
     share, coefs, u1, u2 = pl.pallas_call(
         outer_kernel,
@@ -341,7 +364,7 @@
         ),
         in_specs=smem(2) + vmem(5),
         out_specs=vmem(4),
-        scratch_shapes=[pltpu.VMEM((8 * NX + 8, LM, NY), jnp.float32)],
+        scratch_shapes=[pltpu.VMEM(((8 * NX + 8) * LM, NY), jnp.float32)],
         compiler_params=limit(24),
         name="outer",
     )(edge, far_pick, log_cond, head_slope, before, after, modes)
@@ -354,7 +377,7 @@
         out_specs=vmem(1)[0],
         scratch_shapes=[
             pltpu.VMEM((4 * ROWS * LM, NY), jnp.float32),
-            pltpu.VMEM((4 * NX + 8, LM, NY), jnp.float32),
+            pltpu.VMEM((4 * NX * LM, NY), jnp.float32),
         ],
         compiler_params=limit(24),
         name="inner",

time: 88 us -> 87.3 us (level)
    unnamed x12 -> x16, local copies, waits for them, and re-layouts: 0.03 us -> 1.75 us
    slice x1 -> x0, local copies, waits for them, and re-layouts: 1.17 us -> none  [on_device(): upward = jnp.concatenate([log_cond[1:4].reshape(3 * NX, NY), cells])]
  transfers between devices with their start and end apart: 5 -> 5, of which waited for: 0 -> 0; matrix products, arithmetic and copies ran while one was open for 3% -> 3% of each run, Pallas kernels for 16% -> 15%
where the time goes in v3:
time: 87.3 us; the launch traced here: 86.9 us
  blocking collectives  43.2 us (49%)
  starting transfers between devices  21.2 us (24%)
  Pallas kernels  15.9 us (18%)
  local copies, waits for them, and re-layouts  5.24 us (6%)
  matrix products  1.06 us (1%)
    all_to_all x1, blocking collectives, on_device(): part = lax.all_to_all(part, 'slab_0', 0, 0, tiled=True)  19.2 us
    all_to_all x1, blocking collectives, on_device(): part = lax.all_to_all(part, 'slab_1', 0, 0, tiled=True)  13.3 us
    all_to_all x1, blocking collectives, on_device(): whole = lax.all_to_all(copies, MODE, 0, 0, tiled=True)  10.7 us
    all_to_all x1, starting transfers between devices, on_device(): block = lax.all_to_all(pieces, MODE, 0, 0, tiled=True)  9.34 us
    pallas_call x1, Pallas kernels, on_device(): pl.pallas_call(outer_kernel, out_shape=(jax.ShapeDtypeStruct((16, LM, NY)...  7.89 us
    pallas_call x1, Pallas kernels, on_device(): pl.pallas_call(inner_kernel, out_shape=jax.ShapeDtypeStruct((8, LM, NY),...  5.34 us
    ppermute x1, starting transfers between devices, on_device(): before = lax.ppermute(upward, SLAB, ahead)  4.56 us
    ppermute x1, starting transfers between devices, on_device(): from_below = lax.ppermute(share[8:], SLAB, ahead)  4.55 us
  transfers between devices with their start and end apart: 5, of which 0 were waited for; matrix products, arithmetic and copies ran while one was open for 3% of the time, Pallas kernels for 15%

profile of v3, /device:TPU:2, one launch (start us, length us, event | category | flops | bytes accessed | tf_op | source)
XLA Modules:
  0.0 86.9 jit_solution(237493960720025134)
XLA Ops:
  0.0 0.0 copy-start
  0.0 0.0 copy-start.1
  0.0 1.0 %copy-done.1 = f32[4,128,128]{2,1,0:T(8,128)S(1)} copy-done((f32[4,128,128]{2,1,0:T(8,128)S(1)}, f32[4,128,128]{2,1,0:T(8,128)}, u32[]{:S(2)}) %copy-start.1) | copy-done | bytes 262168
  1.0 0.0 copy-start.5
  1.0 0.7 copy-done.5
  1.7 0.0 copy-start.2
  1.7 0.0 copy-start.3
  1.8 1.4 %collective-permute-start.1 = (f32[392,128]{1,0:T(8,128)S(1)}, f32[392,128]{1,0:T(8,128)S(1)}, u32[]{:S(2)}, u32[]{:S(2)}) collective-permute-start(f32[392,128]{1,0:T(8,128)S(1)} %get-tuple-element.17), channel_id=1, source_target_pairs={{1,0},{2,1},{3,2},{4,3},{5,4},{6,5},{7,6},{8,7},{9,8},{10,9},{11,1... | collective-permute-start | bytes 602120 | tf_op jit(solution)/shard_map/ppermute | solution.py:342
  3.2 4.6 %collective-permute-start = (f32[392,128]{1,0:T(8,128)S(1)}, f32[392,128]{1,0:T(8,128)S(1)}, u32[]{:S(2)}, u32[]{:S(2)}) collective-permute-start(f32[392,128]{1,0:T(8,128)S(1)} %get-tuple-element.16), channel_id=1, source_target_pairs={{0,1},{1,2},{2,3},{3,4},{4,5},{5,6},{6,7},{7,8},{8,9},{9,10},{10,1... | collective-permute-start | bytes 602120 | tf_op jit(solution)/shard_map/ppermute | solution.py:341
  7.8 2.5 %copy.17 = bf16[8,8,4,16,128]{4,3,2,1,0:T(8,128)(2,1)} copy(bf16[8,8,4,16,128]{4,3,0,2,1:T(8,128)(2,1)} %bitcast.15) | data formatting | bytes 2097152 | tf_op jit(solution)/shard_map/transpose | solution.py:344
  10.3 9.3 %all-to-all-start = ((bf16[8,8,4,16,128]{4,3,2,1,0:T(8,128)(2,1)}), bf16[8,8,4,16,128]{4,3,2,1,0:T(8,128)(2,1)S(1)}, u32[]{:S(2)}, u32[]{:S(2)}) async-start(bf16[8,8,4,16,128]{4,3,2,1,0:T(8,128)(2,1)} %copy.17), calls=%async_computation | async-start | bytes 2097152 | tf_op jit(solution)/shard_map/all_to_all | solution.py:345
  19.6 0.1 pad_add_fusion.1.edge
  19.7 0.0 collective-permute-done.1.after
  19.7 0.0 collective-permute-done.before
  19.7 0.0 copy-done
  19.8 0.0 copy-done.2
  19.8 0.0 copy-done.3
  19.8 7.9 %outer.1 = (f32[16,8,128]{2,1,0:T(8,128)S(1)}, f32[6,8,128,128]{3,2,1,0:T(8,128)S(1)}, f32[8320,128]{1,0:T(8,128)S(1)}, f32[8320,128]{1,0:T(8,128)S(1)}) custom-call(s32[2]{0:T(128)S(1)} %pad_add_fusion.1.edge, s32[16,128]{1,0:T(8,128)S(1)} %pad_add_fusion.pick, f32[4,128,128]{2,1,0:T(8,128)S(1)} %copy-done.2, f32[4,128,128]{2,1,0:T(8,128)S(1)} %copy-done.3, ...), custom_call_target="tpu_custom_call" | custom-call | tf_op jit(solution)/shard_map/outer/pallas_call | solution.py:357
  27.7 1.3 %collective-permute-start.2 = (f32[8,8,128]{2,1,0:T(8,128)S(1)}, f32[8,8,128]{2,1,0:T(8,128)S(1)}, u32[]{:S(2)}, u32[]{:S(2)}) collective-permute-start(f32[8,8,128]{2,1,0:T(8,128)S(1)} %get-tuple-element.26), channel_id=1, source_target_pairs={{1,0},{2,1},{3,2},{4,3},{5,4},{6,5},{7,6},{8,7},{9,8},{10,9},{11,1... | collective-permute-start | bytes 98312 | tf_op jit(solution)/shard_map/ppermute | solution.py:371
  29.0 4.5 %collective-permute-start.3 = (f32[8,8,128]{2,1,0:T(8,128)S(1)}, f32[8,8,128]{2,1,0:T(8,128)S(1)}, u32[]{:S(2)}, u32[]{:S(2)}) collective-permute-start(f32[8,8,128]{2,1,0:T(8,128)S(1)} %get-tuple-element.25), channel_id=1, source_target_pairs={{0,1},{1,2},{2,3},{3,4},{4,5},{5,6},{6,7},{7,8},{8,9},{9,10},{10,1... | collective-permute-start | bytes 98312 | tf_op jit(solution)/shard_map/ppermute | solution.py:372
  33.5 0.0 copy-start.4
  33.5 0.0 copy-start.6
  33.6 0.0 copy-start.7
  33.6 5.3 %inner.1 = f32[8,8,128]{2,1,0:T(8,128)S(1)} custom-call(s32[8,128]{1,0:T(8,128)S(1)} %get-tuple-element.15.pick, f32[6,8,128,128]{3,2,1,0:T(8,128)S(1)} %get-tuple-element.18.coef, f32[8320,128]{1,0:T(8,128)S(1)} %get-tuple-element.19.u1, f32[8320,128]{1,0:T(8,128)S(1)} %get-tuple-element.20.u2), custom_call_target="tpu_custom_call" | custom-call | tf_op jit(solution)/shard_map/inner/pallas_call | solution.py:373
  38.9 0.0 collective-permute-done.2
  38.9 0.0 collective-permute-done.3
  38.9 0.0 all-to-all-done
  39.0 10.7 %all_to_all.20 = f32[8,8,8,128]{3,2,1,0:T(8,128)S(1)} all-to-all(f32[8,8,8,128]{3,2,1,0:T(8,128)S(1)} %broadcast_in_dim.9), channel_id=1, replica_groups=mesh['mode_0'=4,'mode_1'=2,'slab_0'=8,'slab_1'=8] {'mode_0','mode_1'}, dimensions={0} | all-to-all | bytes 524288 | tf_op jit(solution)/shard_map/all_to_all | solution.py:388
  49.6 0.0 copy-done.4
  49.6 0.0 copy-done.6
  49.6 0.9 %gram.1 = f32[8,32,128]{2,1,0:T(8,128)S(1)} custom-call(f32[64,1024]{1,0:T(8,128)S(1)} %bitcast.16, f32[1,1024]{1,0:T(1,128)S(1)} %bitcast.19, f32[16,1024]{1,0:T(8,128)S(1)} %bitcast.17), custom_call_target="tpu_custom_call" | custom-call | tf_op jit(solution)/shard_map/gram/pallas_call | solution.py:392
  50.6 13.3 %all_to_all.21.parts = f32[8,32,128]{2,1,0:T(8,128)S(1)} all-to-all(f32[8,32,128]{2,1,0:T(8,128)S(1)} %gram.1), channel_id=1, replica_groups=mesh['mode_0'=4,'mode_1'=2,'slab_0'=8,'slab_1'=8] {'slab_1'}, dimensions={0} | all-to-all | bytes 262144 | tf_op jit(solution)/shard_map/all_to_all | solution.py:395
  63.9 19.2 %all_to_all.22.parts = f32[8,32,128]{2,1,0:T(8,128)S(1)} all-to-all(f32[8,32,128]{2,1,0:T(8,128)S(1)} %total.1), channel_id=1, replica_groups=mesh['mode_0'=4,'mode_1'=2,'slab_0'=8,'slab_1'=8] {'slab_0'}, dimensions={0} | all-to-all | bytes 262144 | tf_op jit(solution)/shard_map/all_to_all | solution.py:397
  83.1 1.8 %solve.1 = f32[64,128]{1,0:T(8,128)S(1)} custom-call(f32[8,32,128]{2,1,0:T(8,128)S(1)} %all_to_all.22.parts), custom_call_target="tpu_custom_call" | custom-call | tf_op jit(solution)/shard_map/solve/pallas_call | solution.py:398
  84.8 0.0 copy-done.7
  84.9 1.1 %convolution_add_fusion = f32[16,4,16,128]{3,0,2,1:T(8,128)S(1)} fusion(bf16[64,4,16,128]{3,2,1,0:T(8,128)(2,1)S(1)} %bitcast.20, bf16[16,4,16,128]{3,2,1,0:T(8,128)(2,1)S(1)} %copy-done.7, f32[64,128]{1,0:T(8,128)S(1)} %solve.1), kind=kOutput, calls=%fused_computation | convolution fusion | flops 100925440 | bytes 1867776 | tf_op jit(solution)/shard_map/dot_general | solution.py:409
  85.9 1.0 %copy.20 = f32[16,4,16,128]{3,2,1,0:T(8,128)} copy(f32[16,4,16,128]{3,0,2,1:T(8,128)S(1)} %convolution_add_fusion) | data formatting | bytes 1048576 | tf_op jit(solution)/shard_map/add | solution.py:410
  (8 shorter events, 0.1 us)
Async XLA Ops:
  0.0 19.7 %copy-start = (bf16[8,4,128,128]{3,2,1,0:T(8,128)(2,1)S(1)}, bf16[8,4,128,128]{3,2,1,0:T(8,128)(2,1)}, u32[]{:S(2)}) copy-start(bf16[8,4,128,128]{3,2,1,0:T(8,128)(2,1)} %modes.1) | copy-start | bytes 3145732
  0.0 1.0 %copy-start.1 = (f32[4,128,128]{2,1,0:T(8,128)S(1)}, f32[4,128,128]{2,1,0:T(8,128)}, u32[]{:S(2)}) copy-start(f32[4,128,128]{2,1,0:T(8,128)} %lc.3) | copy-start | bytes 786436
  1.0 0.7 copy-start.5
  1.7 18.0 %copy-start.2 = (f32[4,128,128]{2,1,0:T(8,128)S(1)}, f32[4,128,128]{2,1,0:T(8,128)}, u32[]{:S(2)}) copy-start(f32[4,128,128]{2,1,0:T(8,128)} %lc.3) | copy-start | bytes 786436
  1.7 18.0 %copy-start.3 = (f32[4,128,128]{2,1,0:T(8,128)S(1)}, f32[4,128,128]{2,1,0:T(8,128)}, u32[]{:S(2)}) copy-start(f32[4,128,128]{2,1,0:T(8,128)} %hs.1) | copy-start | bytes 786436
  1.8 17.9 %collective-permute-start.1 = (f32[392,128]{1,0:T(8,128)S(1)}, f32[392,128]{1,0:T(8,128)S(1)}, u32[]{:S(2)}, u32[]{:S(2)}) collective-permute-start(f32[392,128]{1,0:T(8,128)S(1)} %get-tuple-element.17), channel_id=1, source_target_pairs={{1,0},{2,1},{3,2},{4,3},{5,4},{6,5},{7,6},{8,7},{9,8},{10,9},{11,1... | collective-permute-start | bytes 602120 | tf_op jit(solution)/shard_map/ppermute | solution.py:342
  3.2 16.5 %collective-permute-start = (f32[392,128]{1,0:T(8,128)S(1)}, f32[392,128]{1,0:T(8,128)S(1)}, u32[]{:S(2)}, u32[]{:S(2)}) collective-permute-start(f32[392,128]{1,0:T(8,128)S(1)} %get-tuple-element.16), channel_id=1, source_target_pairs={{0,1},{1,2},{2,3},{3,4},{4,5},{5,6},{6,7},{7,8},{8,9},{9,10},{10,1... | collective-permute-start | bytes 602120 | tf_op jit(solution)/shard_map/ppermute | solution.py:341
  10.3 28.7 %all-to-all-start = ((bf16[8,8,4,16,128]{4,3,2,1,0:T(8,128)(2,1)}), bf16[8,8,4,16,128]{4,3,2,1,0:T(8,128)(2,1)S(1)}, u32[]{:S(2)}, u32[]{:S(2)}) async-start(bf16[8,8,4,16,128]{4,3,2,1,0:T(8,128)(2,1)} %copy.17), calls=%async_computation | async-start | bytes 2097152 | tf_op jit(solution)/shard_map/all_to_all | solution.py:345
  27.7 11.2 %collective-permute-start.2 = (f32[8,8,128]{2,1,0:T(8,128)S(1)}, f32[8,8,128]{2,1,0:T(8,128)S(1)}, u32[]{:S(2)}, u32[]{:S(2)}) collective-permute-start(f32[8,8,128]{2,1,0:T(8,128)S(1)} %get-tuple-element.26), channel_id=1, source_target_pairs={{1,0},{2,1},{3,2},{4,3},{5,4},{6,5},{7,6},{8,7},{9,8},{10,9},{11,1... | collective-permute-start | bytes 98312 | tf_op jit(solution)/shard_map/ppermute | solution.py:371
  29.0 9.9 %collective-permute-start.3 = (f32[8,8,128]{2,1,0:T(8,128)S(1)}, f32[8,8,128]{2,1,0:T(8,128)S(1)}, u32[]{:S(2)}, u32[]{:S(2)}) collective-permute-start(f32[8,8,128]{2,1,0:T(8,128)S(1)} %get-tuple-element.25), channel_id=1, source_target_pairs={{0,1},{1,2},{2,3},{3,4},{4,5},{5,6},{6,7},{7,8},{8,9},{9,10},{10,1... | collective-permute-start | bytes 98312 | tf_op jit(solution)/shard_map/ppermute | solution.py:372
  33.5 16.1 %copy-start.4 = (f32[1024,16]{0,1:T(8,128)S(1)}, f32[1024,16]{0,1:T(8,128)}, u32[]{:S(2)}) copy-start(f32[1024,16]{0,1:T(8,128)} %param.12) | copy-start | bytes 196612
  33.5 16.1 %copy-start.6 = (f32[1024]{0:T(1024)S(1)}, f32[1024]{0:T(1024)}, u32[]{:S(2)}) copy-start(f32[1024]{0:T(1024)} %param.11) | copy-start | bytes 12292
  33.6 51.3 %copy-start.7 = (bf16[16,4,16,128]{3,2,1,0:T(8,128)(2,1)S(1)}, bf16[16,4,16,128]{3,2,1,0:T(8,128)(2,1)}, u32[]{:S(2)}) copy-start(bf16[16,4,16,128]{3,2,1,0:T(8,128)(2,1)} %param.13) | copy-start | bytes 786436

commit v4 on v3

--- a/solution.py
+++ b/solution.py
@@ -108,20 +108,30 @@
     return (row << 10) | ((place - where) & 127)
 
 
-def pack_kernel(lc, cells, upward, downward, near):
+def pack_kernel(lc, cells, upward, downward, near, held, sems):
+    copies = [pltpu.make_async_copy(cells, held, sems.at[0])]
     for z in range(3):
-        upward[NX * z : NX * z + NX] = lc[z + 1]
-        downward[NX * z : NX * z + NX] = lc[z]
-    where = cells[...]
+        part = pl.ds(NX * z, NX)
+        copies.append(pltpu.make_async_copy(lc.at[z + 1], upward.at[part], sems.at[1 + z]))
+        copies.append(pltpu.make_async_copy(lc.at[z], downward.at[part], sems.at[4 + z]))
+    for copy in copies:
+        copy.start()
+    copies[0].wait()
+    where = held[...]
     upward[3 * NX :] = where.astype(jnp.float32)
     downward[3 * NX :] = where.astype(jnp.float32)
     place = lax.broadcasted_iota(jnp.int32, (8, NY), 1)
     near[...] = address(where, place, 0, 0, 3)
-
-
-def outer_kernel(edge, pick, lc, hs, before, after, modes, share, coef, u1, u2, u3):
-    first = edge[0] == 0
-    last = edge[1] == 0
+    for copy in copies[1:]:
+        copy.wait()
+
+
+def outer_kernel(far, lc, hs, before, after, modes, share, coef, u1, u2, u3, pick, sem):
+    fetch = pltpu.make_async_copy(far, pick, sem)
+    fetch.start()
+    slab = lax.axis_index("slab_0") * 8 + lax.axis_index("slab_1")
+    first = slab == 0
+    last = slab == 63
     rows = lax.broadcasted_iota(jnp.int32, (NX, NY), 0)
     cols = lax.broadcasted_iota(jnp.int32, (NX, NY), 1)
     zero = jnp.zeros((LM, NY), jnp.float32)
@@ -198,6 +208,7 @@
         put_row(u3, e * NX + x - 1, (1.0 - W3) * u + (W3 / W2) * total)
 
     over_rows((1, 5, 2), 64, third)
+    fetch.wait()
 
     def block(b, _):
         pick_block(pick, u3, b, share)
@@ -206,7 +217,10 @@
     lax.fori_loop(0, 16, block, 0)
 
 
-def inner_kernel(pick, coef, u1, u2, out, w2, u3):
+def inner_kernel(near, coef, u1, u2, out, w2, u3, pick, sem):
+    fetch = pltpu.make_async_copy(near, pick, sem)
+    fetch.start()
+
     def second(e, x):
         u, total = sweep(coef, u1, e, x)
         put(w2, e - 2, x, OWN2 * u + total)
@@ -237,6 +251,8 @@
             64,
             lambda e, x, q=q: third(q + 2, x, lines[q + 2], lines[q + 1], lines[q + 3]),
         )
+
+    fetch.wait()
 
     def block(b, _):
         pick_block(pick, u3, b, out)
@@ -319,13 +335,16 @@
     return [pl.BlockSpec(memory_space=pltpu.SMEM)] * n
 
 
+def stay(x):
+    return pltpu.with_memory_space_constraint(x, pltpu.HBM)
+
+
 def limit(mib):
     return pltpu.CompilerParams(vmem_limit_bytes=mib * 1024 * 1024)
 
 
 def on_device(log_cond, head_slope, modes, obs_cells, obs_var, misfit, base_fields):
     slabs = lax.axis_size(SLAB)
-    slab = lax.axis_index(SLAB)
     ahead = [(i, i + 1) for i in range(slabs - 1)]
     back = [(i + 1, i) for i in range(slabs - 1)]
 
@@ -333,18 +352,18 @@
     upward, downward, near_pick = pl.pallas_call(
         pack_kernel,
         out_shape=(message, message, jax.ShapeDtypeStruct((8, NY), jnp.int32)),
-        in_specs=vmem(2),
+        in_specs=[pl.BlockSpec(memory_space=pltpu.HBM)] * 2,
         out_specs=vmem(3),
+        scratch_shapes=[pltpu.VMEM((8, NY), jnp.int32), pltpu.SemaphoreType.DMA((7,))],
         compiler_params=limit(4),
         name="pack",
-    )(log_cond, obs_cells.reshape(8, NY))
+    )(stay(log_cond), stay(obs_cells.reshape(8, NY)))
     before = lax.ppermute(upward, SLAB, ahead)
     after = lax.ppermute(downward, SLAB, back)
 
     pieces = jnp.moveaxis(modes.reshape(LM, CZ, 8, NX // 8, NY), 2, 0)
     block = lax.all_to_all(pieces, MODE, 0, 0, tiled=True)
 
-    edge = jnp.stack([slab, slabs - 1 - slab]).astype(jnp.int32)
     place = lax.broadcasted_iota(jnp.int32, (8, NY), 1)
 
     def arrived(x):
@@ -362,22 +381,28 @@
             plane_rows,
             plane_rows,
         ),
-        in_specs=smem(2) + vmem(5),
+        in_specs=vmem(6),
         out_specs=vmem(4),
-        scratch_shapes=[pltpu.VMEM(((8 * NX + 8) * LM, NY), jnp.float32)],
+        scratch_shapes=[
+            pltpu.VMEM(((8 * NX + 8) * LM, NY), jnp.float32),
+            pltpu.SMEM((16, NY), jnp.int32),
+            pltpu.SemaphoreType.DMA,
+        ],
         compiler_params=limit(24),
         name="outer",
-    )(edge, far_pick, log_cond, head_slope, before, after, modes)
+    )(far_pick, log_cond, head_slope, before, after, modes)
     from_above = lax.ppermute(share[:8], SLAB, back)
     from_below = lax.ppermute(share[8:], SLAB, ahead)
     picked = pl.pallas_call(
         inner_kernel,
         out_shape=jax.ShapeDtypeStruct((8, LM, NY), jnp.float32),
-        in_specs=smem(1) + vmem(3),
+        in_specs=vmem(4),
         out_specs=vmem(1)[0],
         scratch_shapes=[
             pltpu.VMEM((4 * ROWS * LM, NY), jnp.float32),
             pltpu.VMEM((4 * NX * LM, NY), jnp.float32),
+            pltpu.SMEM((8, NY), jnp.int32),
+            pltpu.SemaphoreType.DMA,
         ],
         compiler_params=limit(24),
         name="inner",

time: 87.3 us -> 90.1 us (1.032)
  waiting for transfers between devices: 0.01 us -> 4.49 us
  local copies, waits for them, and re-layouts: 5.24 us -> 3.53 us
    ppermute x1, waiting for transfers between devices: 0.01 us -> 4.48 us  [on_device(): before = lax.ppermute(upward, SLAB, ahead)]
    unnamed x16 -> x12, local copies, waits for them, and re-layouts: 1.75 us -> 0.03 us
    pallas_call x1, Pallas kernels: 0.03 us -> 1.19 us  [on_device(): pl.pallas_call(pack_kernel, out_shape=(message, message, jax.ShapeDtypeSt...]
  transfers between devices with their start and end apart: 5 -> 5, of which waited for: 0 -> 1; matrix products, arithmetic and copies ran while one was open for 3% -> 3% of each run, Pallas kernels for 15% -> 13%
where the time goes in v4:
time: 90.1 us; the launch traced here: 89.7 us
  blocking collectives  43.2 us (48%)
  starting transfers between devices  21.5 us (24%)
  Pallas kernels  15.8 us (18%)
  waiting for transfers between devices  4.49 us (5%)
  local copies, waits for them, and re-layouts  3.53 us (4%)
  matrix products  1.07 us (1%)
    all_to_all x1, blocking collectives, on_device(): part = lax.all_to_all(part, 'slab_0', 0, 0, tiled=True)  19.2 us
    all_to_all x1, blocking collectives, on_device(): part = lax.all_to_all(part, 'slab_1', 0, 0, tiled=True)  13.3 us
    all_to_all x1, blocking collectives, on_device(): whole = lax.all_to_all(copies, MODE, 0, 0, tiled=True)  10.7 us
    all_to_all x1, starting transfers between devices, on_device(): block = lax.all_to_all(pieces, MODE, 0, 0, tiled=True)  9.34 us
    pallas_call x1, Pallas kernels, on_device(): pl.pallas_call(outer_kernel, out_shape=(jax.ShapeDtypeStruct((16, LM, NY)...  7.25 us
    ppermute x1, starting transfers between devices, on_device(): from_below = lax.ppermute(share[8:], SLAB, ahead)  5.02 us
    pallas_call x1, Pallas kernels, on_device(): pl.pallas_call(inner_kernel, out_shape=jax.ShapeDtypeStruct((8, LM, NY),...  4.64 us
    ppermute x1, starting transfers between devices, on_device(): before = lax.ppermute(upward, SLAB, ahead)  4.55 us
  transfers between devices with their start and end apart: 5, of which 1 were waited for; matrix products, arithmetic and copies ran while one was open for 3% of the time, Pallas kernels for 13%

profile of v4, /device:TPU:2, one launch (start us, length us, event | category | flops | bytes accessed | tf_op | source)
XLA Modules:
  0.0 89.7 jit_solution(9135883777707803340)
XLA Ops:
  0.0 0.0 copy-start.1
  0.0 0.0 copy-start
  0.0 0.0 copy-start.2
  0.0 1.2 %pack.1 = (f32[392,128]{1,0:T(8,128)S(1)}, f32[392,128]{1,0:T(8,128)S(1)}, s32[8,128]{1,0:T(8,128)S(1)}) custom-call(f32[4,128,128]{2,1,0:T(8,128)} %lc.3, s32[8,128]{1,0:T(8,128)} %bitcast.18), custom_call_target="tpu_custom_call" | custom-call | tf_op jit(solution)/shard_map/pack/pallas_call | solution.py:352
  1.2 1.3 %collective-permute-start.1 = (f32[392,128]{1,0:T(8,128)S(1)}, f32[392,128]{1,0:T(8,128)S(1)}, u32[]{:S(2)}, u32[]{:S(2)}) collective-permute-start(f32[392,128]{1,0:T(8,128)S(1)} %get-tuple-element.17), channel_id=1, source_target_pairs={{1,0},{2,1},{3,2},{4,3},{5,4},{6,5},{7,6},{8,7},{9,8},{10,9},{11,1... | collective-permute-start | bytes 602120 | tf_op jit(solution)/shard_map/ppermute | solution.py:362
  2.5 2.5 %copy.17 = bf16[8,8,4,16,128]{4,3,2,1,0:T(8,128)(2,1)} copy(bf16[8,8,4,16,128]{4,3,0,2,1:T(8,128)(2,1)} %bitcast.13) | data formatting | bytes 2097152 | tf_op jit(solution)/shard_map/transpose | solution.py:364
  5.0 9.3 %all-to-all-start = ((bf16[8,8,4,16,128]{4,3,2,1,0:T(8,128)(2,1)}), bf16[8,8,4,16,128]{4,3,2,1,0:T(8,128)(2,1)S(1)}, u32[]{:S(2)}, u32[]{:S(2)}) async-start(bf16[8,8,4,16,128]{4,3,2,1,0:T(8,128)(2,1)} %copy.17), calls=%async_computation | async-start | bytes 2097152 | tf_op jit(solution)/shard_map/all_to_all | solution.py:365
  14.4 4.5 %collective-permute-start = (f32[392,128]{1,0:T(8,128)S(1)}, f32[392,128]{1,0:T(8,128)S(1)}, u32[]{:S(2)}, u32[]{:S(2)}) collective-permute-start(f32[392,128]{1,0:T(8,128)S(1)} %get-tuple-element.16), channel_id=1, source_target_pairs={{0,1},{1,2},{2,3},{3,4},{4,5},{5,6},{6,7},{7,8},{8,9},{9,10},{10,1... | collective-permute-start | bytes 602120 | tf_op jit(solution)/shard_map/ppermute | solution.py:361
  18.9 0.0 collective-permute-done.1.after
  18.9 4.5 %collective-permute-done.before = f32[392,128]{1,0:T(8,128)S(1)} collective-permute-done((f32[392,128]{1,0:T(8,128)S(1)}, f32[392,128]{1,0:T(8,128)S(1)}, u32[]{:S(2)}, u32[]{:S(2)}) %collective-permute-start) | collective-permute-done | bytes 200736 | tf_op jit(solution)/shard_map/ppermute | solution.py:361
  23.4 0.0 copy-done.1
  23.4 0.0 copy-done
  23.5 0.0 copy-done.2
  23.5 7.2 %outer.1 = (f32[16,8,128]{2,1,0:T(8,128)S(1)}, f32[6,8,128,128]{3,2,1,0:T(8,128)S(1)}, f32[8320,128]{1,0:T(8,128)S(1)}, f32[8320,128]{1,0:T(8,128)S(1)}) custom-call(s32[16,128]{1,0:T(8,128)S(1)} %pad_add_fusion.far, f32[4,128,128]{2,1,0:T(8,128)S(1)} %copy-done.1, f32[4,128,128]{2,1,0:T(8,128)S(1)} %copy-done.2, ...), custom_call_target="tpu_custom_call" | custom-call | tf_op jit(solution)/shard_map/outer/pallas_call | solution.py:376
  30.7 1.3 %collective-permute-start.2 = (f32[8,8,128]{2,1,0:T(8,128)S(1)}, f32[8,8,128]{2,1,0:T(8,128)S(1)}, u32[]{:S(2)}, u32[]{:S(2)}) collective-permute-start(f32[8,8,128]{2,1,0:T(8,128)S(1)} %get-tuple-element.26), channel_id=1, source_target_pairs={{1,0},{2,1},{3,2},{4,3},{5,4},{6,5},{7,6},{8,7},{9,8},{10,9},{11,1... | collective-permute-start | bytes 98312 | tf_op jit(solution)/shard_map/ppermute | solution.py:394
  32.0 5.0 %collective-permute-start.3 = (f32[8,8,128]{2,1,0:T(8,128)S(1)}, f32[8,8,128]{2,1,0:T(8,128)S(1)}, u32[]{:S(2)}, u32[]{:S(2)}) collective-permute-start(f32[8,8,128]{2,1,0:T(8,128)S(1)} %get-tuple-element.25), channel_id=1, source_target_pairs={{0,1},{1,2},{2,3},{3,4},{4,5},{5,6},{6,7},{7,8},{8,9},{9,10},{10,1... | collective-permute-start | bytes 98312 | tf_op jit(solution)/shard_map/ppermute | solution.py:395
  37.1 0.0 copy-start.3
  37.1 0.0 copy-start.4
  37.1 0.0 copy-start.5
  37.1 4.6 %inner.1 = f32[8,8,128]{2,1,0:T(8,128)S(1)} custom-call(s32[8,128]{1,0:T(8,128)S(1)} %get-tuple-element.15.near, f32[6,8,128,128]{3,2,1,0:T(8,128)S(1)} %get-tuple-element.18.coef, f32[8320,128]{1,0:T(8,128)S(1)} %get-tuple-element.19.u1, f32[8320,128]{1,0:T(8,128)S(1)} %get-tuple-element.20.u2), custom_call_target="tpu_custom_call" | custom-call | tf_op jit(solution)/shard_map/inner/pallas_call | solution.py:396
  41.7 0.0 collective-permute-done.2
  41.8 0.0 collective-permute-done.3
  41.8 0.0 all-to-all-done
  41.8 10.7 %all_to_all.20 = f32[8,8,8,128]{3,2,1,0:T(8,128)S(1)} all-to-all(f32[8,8,8,128]{3,2,1,0:T(8,128)S(1)} %broadcast_in_dim.9), channel_id=1, replica_groups=mesh['mode_0'=4,'mode_1'=2,'slab_0'=8,'slab_1'=8] {'mode_0','mode_1'}, dimensions={0} | all-to-all | bytes 524288 | tf_op jit(solution)/shard_map/all_to_all | solution.py:413
  52.5 0.0 copy-done.3
  52.5 0.0 copy-done.4
  52.5 0.9 %gram.1 = f32[8,32,128]{2,1,0:T(8,128)S(1)} custom-call(f32[64,1024]{1,0:T(8,128)S(1)} %bitcast.14, f32[1,1024]{1,0:T(1,128)S(1)} %bitcast.16, f32[16,1024]{1,0:T(8,128)S(1)} %bitcast.15), custom_call_target="tpu_custom_call" | custom-call | tf_op jit(solution)/shard_map/gram/pallas_call | solution.py:417
  53.4 13.3 %all_to_all.21.parts = f32[8,32,128]{2,1,0:T(8,128)S(1)} all-to-all(f32[8,32,128]{2,1,0:T(8,128)S(1)} %gram.1), channel_id=1, replica_groups=mesh['mode_0'=4,'mode_1'=2,'slab_0'=8,'slab_1'=8] {'slab_1'}, dimensions={0} | all-to-all | bytes 262144 | tf_op jit(solution)/shard_map/all_to_all | solution.py:420
  66.8 19.2 %all_to_all.22.parts = f32[8,32,128]{2,1,0:T(8,128)S(1)} all-to-all(f32[8,32,128]{2,1,0:T(8,128)S(1)} %total.1), channel_id=1, replica_groups=mesh['mode_0'=4,'mode_1'=2,'slab_0'=8,'slab_1'=8] {'slab_0'}, dimensions={0} | all-to-all | bytes 262144 | tf_op jit(solution)/shard_map/all_to_all | solution.py:422
  85.9 1.8 %solve.1 = f32[64,128]{1,0:T(8,128)S(1)} custom-call(f32[8,32,128]{2,1,0:T(8,128)S(1)} %all_to_all.22.parts), custom_call_target="tpu_custom_call" | custom-call | tf_op jit(solution)/shard_map/solve/pallas_call | solution.py:423
  87.7 0.0 copy-done.5
  87.7 1.1 %convolution_add_fusion = f32[16,4,16,128]{3,0,2,1:T(8,128)S(1)} fusion(bf16[64,4,16,128]{3,2,1,0:T(8,128)(2,1)S(1)} %bitcast.17, bf16[16,4,16,128]{3,2,1,0:T(8,128)(2,1)S(1)} %copy-done.5, f32[64,128]{1,0:T(8,128)S(1)} %solve.1), kind=kOutput, calls=%fused_computation | convolution fusion | flops 100925440 | bytes 1867776 | tf_op jit(solution)/shard_map/dot_general | solution.py:434
  88.8 1.0 %copy.20 = f32[16,4,16,128]{3,2,1,0:T(8,128)} copy(f32[16,4,16,128]{3,0,2,1:T(8,128)S(1)} %convolution_add_fusion) | data formatting | bytes 1048576 | tf_op jit(solution)/shard_map/add | solution.py:435
  (7 shorter events, 0.1 us)
Async XLA Ops:
  0.0 23.4 %copy-start.1 = (f32[4,128,128]{2,1,0:T(8,128)S(1)}, f32[4,128,128]{2,1,0:T(8,128)}, u32[]{:S(2)}) copy-start(f32[4,128,128]{2,1,0:T(8,128)} %lc.3) | copy-start | bytes 786436
  0.0 23.4 %copy-start = (bf16[8,4,128,128]{3,2,1,0:T(8,128)(2,1)S(1)}, bf16[8,4,128,128]{3,2,1,0:T(8,128)(2,1)}, u32[]{:S(2)}) copy-start(bf16[8,4,128,128]{3,2,1,0:T(8,128)(2,1)} %modes.1) | copy-start | bytes 3145732
  0.0 23.5 %copy-start.2 = (f32[4,128,128]{2,1,0:T(8,128)S(1)}, f32[4,128,128]{2,1,0:T(8,128)}, u32[]{:S(2)}) copy-start(f32[4,128,128]{2,1,0:T(8,128)} %hs.1) | copy-start | bytes 786436
  1.2 17.7 %collective-permute-start.1 = (f32[392,128]{1,0:T(8,128)S(1)}, f32[392,128]{1,0:T(8,128)S(1)}, u32[]{:S(2)}, u32[]{:S(2)}) collective-permute-start(f32[392,128]{1,0:T(8,128)S(1)} %get-tuple-element.17), channel_id=1, source_target_pairs={{1,0},{2,1},{3,2},{4,3},{5,4},{6,5},{7,6},{8,7},{9,8},{10,9},{11,1... | collective-permute-start | bytes 602120 | tf_op jit(solution)/shard_map/ppermute | solution.py:362
  5.0 36.7 %all-to-all-start = ((bf16[8,8,4,16,128]{4,3,2,1,0:T(8,128)(2,1)}), bf16[8,8,4,16,128]{4,3,2,1,0:T(8,128)(2,1)S(1)}, u32[]{:S(2)}, u32[]{:S(2)}) async-start(bf16[8,8,4,16,128]{4,3,2,1,0:T(8,128)(2,1)} %copy.17), calls=%async_computation | async-start | bytes 2097152 | tf_op jit(solution)/shard_map/all_to_all | solution.py:365
  14.4 9.1 %collective-permute-start = (f32[392,128]{1,0:T(8,128)S(1)}, f32[392,128]{1,0:T(8,128)S(1)}, u32[]{:S(2)}, u32[]{:S(2)}) collective-permute-start(f32[392,128]{1,0:T(8,128)S(1)} %get-tuple-element.16), channel_id=1, source_target_pairs={{0,1},{1,2},{2,3},{3,4},{4,5},{5,6},{6,7},{7,8},{8,9},{9,10},{10,1... | collective-permute-start | bytes 602120 | tf_op jit(solution)/shard_map/ppermute | solution.py:361
  30.7 11.0 %collective-permute-start.2 = (f32[8,8,128]{2,1,0:T(8,128)S(1)}, f32[8,8,128]{2,1,0:T(8,128)S(1)}, u32[]{:S(2)}, u32[]{:S(2)}) collective-permute-start(f32[8,8,128]{2,1,0:T(8,128)S(1)} %get-tuple-element.26), channel_id=1, source_target_pairs={{1,0},{2,1},{3,2},{4,3},{5,4},{6,5},{7,6},{8,7},{9,8},{10,9},{11,1... | collective-permute-start | bytes 98312 | tf_op jit(solution)/shard_map/ppermute | solution.py:394
  32.0 9.7 %collective-permute-start.3 = (f32[8,8,128]{2,1,0:T(8,128)S(1)}, f32[8,8,128]{2,1,0:T(8,128)S(1)}, u32[]{:S(2)}, u32[]{:S(2)}) collective-permute-start(f32[8,8,128]{2,1,0:T(8,128)S(1)} %get-tuple-element.25), channel_id=1, source_target_pairs={{0,1},{1,2},{2,3},{3,4},{4,5},{5,6},{6,7},{7,8},{8,9},{9,10},{10,1... | collective-permute-start | bytes 98312 | tf_op jit(solution)/shard_map/ppermute | solution.py:395
  37.1 15.4 %copy-start.3 = (f32[1024,16]{0,1:T(8,128)S(1)}, f32[1024,16]{0,1:T(8,128)}, u32[]{:S(2)}) copy-start(f32[1024,16]{0,1:T(8,128)} %param.12) | copy-start | bytes 196612
  37.1 15.4 %copy-start.4 = (f32[1024]{0:T(1024)S(1)}, f32[1024]{0:T(1024)}, u32[]{:S(2)}) copy-start(f32[1024]{0:T(1024)} %param.11) | copy-start | bytes 12292
  37.1 50.6 %copy-start.5 = (bf16[16,4,16,128]{3,2,1,0:T(8,128)(2,1)S(1)}, bf16[16,4,16,128]{3,2,1,0:T(8,128)(2,1)}, u32[]{:S(2)}) copy-start(bf16[16,4,16,128]{3,2,1,0:T(8,128)(2,1)} %param.13) | copy-start | bytes 786436

commit v5 on v4

--- a/solution.py
+++ b/solution.py
@@ -8,6 +8,7 @@
 from jax.experimental.pallas import tpu as pltpu
 from jax.sharding import Mesh
 from jax.sharding import PartitionSpec as P
+
 
 ITERS = 3
 SLAB = ("slab_0", "slab_1")
@@ -82,14 +83,25 @@
     put(u2, e, x, OWN2 * u + total)
 
 
-def pick_block(pick, u3, b, out):
+def pick_block(buf, u3, b, out):
     lanes = lax.broadcasted_iota(jnp.int32, (LM, NY), 1)
     acc = jnp.zeros((LM, NY), jnp.float32)
     for j in range(NY):
-        p = pick[b, j]
+        p = buf[0, j]
         row = u3[pl.ds(pl.multiple_of(lax.shift_right_logical(p, 7), LM), LM), :]
         acc = jnp.where(lanes == j, pltpu.roll(row, p & 127, 1), acc)
     out[b] = acc
+
+
+def fetches(picks, bufs, sems):
+    return [pltpu.make_async_copy(picks.at[q], buf, sems.at[q]) for q, buf in enumerate(bufs)]
+
+
+def pick_all(picks, bufs, sems, u3, out):
+    for fetch in fetches(picks, bufs, sems):
+        fetch.wait()
+    for q, buf in enumerate(bufs):
+        pick_block(buf, u3, q, out)
 
 
 def put_row(ref, row, value):
@@ -121,14 +133,16 @@
     upward[3 * NX :] = where.astype(jnp.float32)
     downward[3 * NX :] = where.astype(jnp.float32)
     place = lax.broadcasted_iota(jnp.int32, (8, NY), 1)
-    near[...] = address(where, place, 0, 0, 3)
+    spot = address(where, place, 0, 0, 3)
+    for q in range(8):
+        near[q] = spot[q : q + 1]
     for copy in copies[1:]:
         copy.wait()
 
 
-def outer_kernel(far, lc, hs, before, after, modes, share, coef, u1, u2, u3, pick, sem):
-    fetch = pltpu.make_async_copy(far, pick, sem)
-    fetch.start()
+def outer_kernel(far, lc, hs, before, after, modes, share, coef, u1, u2, u3, sems, *bufs):
+    for fetch in fetches(far, bufs, sems):
+        fetch.start()
     slab = lax.axis_index("slab_0") * 8 + lax.axis_index("slab_1")
     first = slab == 0
     last = slab == 63
@@ -208,18 +222,12 @@
         put_row(u3, e * NX + x - 1, (1.0 - W3) * u + (W3 / W2) * total)
 
     over_rows((1, 5, 2), 64, third)
-    fetch.wait()
-
-    def block(b, _):
-        pick_block(pick, u3, b, share)
-        return 0
-
-    lax.fori_loop(0, 16, block, 0)
-
-
-def inner_kernel(near, coef, u1, u2, out, w2, u3, pick, sem):
-    fetch = pltpu.make_async_copy(near, pick, sem)
-    fetch.start()
+    pick_all(far, bufs, sems, u3, share)
+
+
+def inner_kernel(near, coef, u1, u2, out, w2, u3, sems, *bufs):
+    for fetch in fetches(near, bufs, sems):
+        fetch.start()
 
     def second(e, x):
         u, total = sweep(coef, u1, e, x)
@@ -252,13 +260,7 @@
             lambda e, x, q=q: third(q + 2, x, lines[q + 2], lines[q + 1], lines[q + 3]),
         )
 
-    fetch.wait()
-
-    def block(b, _):
-        pick_block(pick, u3, b, out)
-        return 0
-
-    lax.fori_loop(0, 8, block, 0)
+    pick_all(near, bufs, sems, u3, out)
 
 
 def gram_kernel(resp, var, misfit, out):
@@ -331,10 +333,6 @@
     return [pl.BlockSpec(memory_space=pltpu.VMEM)] * n
 
 
-def smem(n):
-    return [pl.BlockSpec(memory_space=pltpu.SMEM)] * n
-
-
 def stay(x):
     return pltpu.with_memory_space_constraint(x, pltpu.HBM)
 
@@ -351,7 +349,7 @@
     message = jax.ShapeDtypeStruct((3 * NX + 8, NY), jnp.float32)
     upward, downward, near_pick = pl.pallas_call(
         pack_kernel,
-        out_shape=(message, message, jax.ShapeDtypeStruct((8, NY), jnp.int32)),
+        out_shape=(message, message, jax.ShapeDtypeStruct((8, 1, NY), jnp.int32)),
         in_specs=[pl.BlockSpec(memory_space=pltpu.HBM)] * 2,
         out_specs=vmem(3),
         scratch_shapes=[pltpu.VMEM((8, NY), jnp.int32), pltpu.SemaphoreType.DMA((7,))],
@@ -371,7 +369,7 @@
 
     far_pick = jnp.concatenate(
         [address(arrived(before), place, -2, 2, 3), address(arrived(after), place, 6, 0, 1)]
-    )
+    ).reshape(16, 1, NY)
     plane_rows = jax.ShapeDtypeStruct((8 * ROWS * LM, NY), jnp.float32)
     share, coefs, u1, u2 = pl.pallas_call(
         outer_kernel,
@@ -385,8 +383,8 @@
         out_specs=vmem(4),
         scratch_shapes=[
             pltpu.VMEM(((8 * NX + 8) * LM, NY), jnp.float32),
-            pltpu.SMEM((16, NY), jnp.int32),
-            pltpu.SemaphoreType.DMA,
+            pltpu.SemaphoreType.DMA((16,)),
+            *[pltpu.SMEM((1, NY), jnp.int32)] * 16,
         ],
         compiler_params=limit(24),
         name="outer",
@@ -401,8 +399,8 @@
         scratch_shapes=[
             pltpu.VMEM((4 * ROWS * LM, NY), jnp.float32),
             pltpu.VMEM((4 * NX * LM, NY), jnp.float32),
-            pltpu.SMEM((8, NY), jnp.int32),
-            pltpu.SemaphoreType.DMA,
+            pltpu.SemaphoreType.DMA((8,)),
+            *[pltpu.SMEM((1, NY), jnp.int32)] * 8,
         ],
         compiler_params=limit(24),
         name="inner",

time: 90.1 us -> 88.8 us (0.986)
  Pallas kernels: 15.8 us -> 14 us
    pallas_call x1, Pallas kernels: 7.25 us -> 5.98 us  [on_device(): pl.pallas_call(outer_kernel, out_shape=(jax.ShapeDtypeStruct((16, LM, NY)...]
  transfers between devices with their start and end apart: 5 -> 5, of which waited for: 1 -> 1; matrix products, arithmetic and copies ran while one was open for 3% -> 3% of each run, Pallas kernels for 13% -> 11%
where the time goes in v5:
time: 88.8 us; the launch traced here: 88.4 us
  blocking collectives  43.6 us (49%)
  starting transfers between devices  21.5 us (24%)
  Pallas kernels  14 us (16%)
  waiting for transfers between devices  4.49 us (5%)
  local copies, waits for them, and re-layouts  3.53 us (4%)
  matrix products  1.06 us (1%)
    all_to_all x1, blocking collectives, on_device(): part = lax.all_to_all(part, 'slab_0', 0, 0, tiled=True)  19.7 us
    all_to_all x1, blocking collectives, on_device(): part = lax.all_to_all(part, 'slab_1', 0, 0, tiled=True)  13.3 us
    all_to_all x1, blocking collectives, on_device(): whole = lax.all_to_all(copies, MODE, 0, 0, tiled=True)  10.7 us
    all_to_all x1, starting transfers between devices, on_device(): block = lax.all_to_all(pieces, MODE, 0, 0, tiled=True)  9.34 us
    pallas_call x1, Pallas kernels, on_device(): pl.pallas_call(outer_kernel, out_shape=(jax.ShapeDtypeStruct((16, LM, NY)...  5.98 us
    ppermute x1, starting transfers between devices, on_device(): from_below = lax.ppermute(share[8:], SLAB, ahead)  5.02 us
    ppermute x1, starting transfers between devices, on_device(): before = lax.ppermute(upward, SLAB, ahead)  4.55 us
    ppermute x1, waiting for transfers between devices, on_device(): before = lax.ppermute(upward, SLAB, ahead)  4.48 us
  transfers between devices with their start and end apart: 5, of which 1 were waited for; matrix products, arithmetic and copies ran while one was open for 3% of the time, Pallas kernels for 11%

profile of v5, /device:TPU:2, one launch (start us, length us, event | category | flops | bytes accessed | tf_op | source)
XLA Modules:
  0.0 88.4 jit_solution(3412909057194186379)
XLA Ops:
  0.0 0.0 copy-start.1
  0.0 0.0 copy-start
  0.0 0.0 copy-start.2
  0.0 1.2 %pack.1 = (f32[392,128]{1,0:T(8,128)S(1)}, f32[392,128]{1,0:T(8,128)S(1)}, s32[8,1,128]{2,1,0:T(1,128)S(1)}) custom-call(f32[4,128,128]{2,1,0:T(8,128)} %lc.3, s32[8,128]{1,0:T(8,128)} %bitcast.22), custom_call_target="tpu_custom_call" | custom-call | tf_op jit(solution)/shard_map/pack/pallas_call | solution.py:350
  1.2 1.3 %collective-permute-start.1 = (f32[392,128]{1,0:T(8,128)S(1)}, f32[392,128]{1,0:T(8,128)S(1)}, u32[]{:S(2)}, u32[]{:S(2)}) collective-permute-start(f32[392,128]{1,0:T(8,128)S(1)} %get-tuple-element.17), channel_id=1, source_target_pairs={{1,0},{2,1},{3,2},{4,3},{5,4},{6,5},{7,6},{8,7},{9,8},{10,9},{11,1... | collective-permute-start | bytes 602120 | tf_op jit(solution)/shard_map/ppermute | solution.py:360
  2.5 2.5 %copy.20 = bf16[8,8,4,16,128]{4,3,2,1,0:T(8,128)(2,1)} copy(bf16[8,8,4,16,128]{4,3,0,2,1:T(8,128)(2,1)} %bitcast.16) | data formatting | bytes 2097152 | tf_op jit(solution)/shard_map/transpose | solution.py:362
  5.0 9.3 %all-to-all-start = ((bf16[8,8,4,16,128]{4,3,2,1,0:T(8,128)(2,1)}), bf16[8,8,4,16,128]{4,3,2,1,0:T(8,128)(2,1)S(1)}, u32[]{:S(2)}, u32[]{:S(2)}) async-start(bf16[8,8,4,16,128]{4,3,2,1,0:T(8,128)(2,1)} %copy.20), calls=%async_computation | async-start | bytes 2097152 | tf_op jit(solution)/shard_map/all_to_all | solution.py:363
  14.4 4.5 %collective-permute-start = (f32[392,128]{1,0:T(8,128)S(1)}, f32[392,128]{1,0:T(8,128)S(1)}, u32[]{:S(2)}, u32[]{:S(2)}) collective-permute-start(f32[392,128]{1,0:T(8,128)S(1)} %get-tuple-element.16), channel_id=1, source_target_pairs={{0,1},{1,2},{2,3},{3,4},{4,5},{5,6},{6,7},{7,8},{8,9},{9,10},{10,1... | collective-permute-start | bytes 602120 | tf_op jit(solution)/shard_map/ppermute | solution.py:359
  18.9 0.0 collective-permute-done.1.after
  18.9 4.5 %collective-permute-done.before = f32[392,128]{1,0:T(8,128)S(1)} collective-permute-done((f32[392,128]{1,0:T(8,128)S(1)}, f32[392,128]{1,0:T(8,128)S(1)}, u32[]{:S(2)}, u32[]{:S(2)}) %collective-permute-start) | collective-permute-done | bytes 200736 | tf_op jit(solution)/shard_map/ppermute | solution.py:359
  23.4 0.0 copy-done.1
  23.4 0.0 copy-done
  23.5 0.0 copy-done.2
  23.5 6.0 %outer.1 = (f32[16,8,128]{2,1,0:T(8,128)S(1)}, f32[6,8,128,128]{3,2,1,0:T(8,128)S(1)}, f32[8320,128]{1,0:T(8,128)S(1)}, f32[8320,128]{1,0:T(8,128)S(1)}) custom-call(s32[16,1,128]{2,1,0:T(1,128)S(1)} %bitcast.19, f32[4,128,128]{2,1,0:T(8,128)S(1)} %copy-done.1, f32[4,128,128]{2,1,0:T(8,128)S(1)} %copy-done.2, f32[392,128]{1,0:T(8,128)S(1)} %collective-permute-done.before, ...), custom_call_target="tpu_custom_call" | custom-call | tf_op jit(solution)/shard_map/outer/pallas_call | solution.py:374
  29.5 1.3 %collective-permute-start.2 = (f32[8,8,128]{2,1,0:T(8,128)S(1)}, f32[8,8,128]{2,1,0:T(8,128)S(1)}, u32[]{:S(2)}, u32[]{:S(2)}) collective-permute-start(f32[8,8,128]{2,1,0:T(8,128)S(1)} %get-tuple-element.26), channel_id=1, source_target_pairs={{1,0},{2,1},{3,2},{4,3},{5,4},{6,5},{7,6},{8,7},{9,8},{10,9},{11,1... | collective-permute-start | bytes 98312 | tf_op jit(solution)/shard_map/ppermute | solution.py:392
  30.8 5.0 %collective-permute-start.3 = (f32[8,8,128]{2,1,0:T(8,128)S(1)}, f32[8,8,128]{2,1,0:T(8,128)S(1)}, u32[]{:S(2)}, u32[]{:S(2)}) collective-permute-start(f32[8,8,128]{2,1,0:T(8,128)S(1)} %get-tuple-element.25), channel_id=1, source_target_pairs={{0,1},{1,2},{2,3},{3,4},{4,5},{5,6},{6,7},{7,8},{8,9},{9,10},{10,1... | collective-permute-start | bytes 98312 | tf_op jit(solution)/shard_map/ppermute | solution.py:393
  35.8 0.0 copy-start.3
  35.8 0.0 copy-start.4
  35.8 0.0 copy-start.5
  35.8 4.1 %inner.1 = f32[8,8,128]{2,1,0:T(8,128)S(1)} custom-call(s32[8,1,128]{2,1,0:T(1,128)S(1)} %get-tuple-element.15.near, f32[6,8,128,128]{3,2,1,0:T(8,128)S(1)} %get-tuple-element.18.coef, f32[8320,128]{1,0:T(8,128)S(1)} %get-tuple-element.19.u1, f32[8320,128]{1,0:T(8,128)S(1)} %get-tuple-element.20.u2), custom_call_target="tpu_custom_call" | custom-call | tf_op jit(solution)/shard_map/inner/pallas_call | solution.py:394
  40.0 0.0 collective-permute-done.2
  40.0 0.0 collective-permute-done.3
  40.0 0.0 all-to-all-done
  40.0 10.7 %all_to_all.20 = f32[8,8,8,128]{3,2,1,0:T(8,128)S(1)} all-to-all(f32[8,8,8,128]{3,2,1,0:T(8,128)S(1)} %broadcast_in_dim.9), channel_id=1, replica_groups=mesh['mode_0'=4,'mode_1'=2,'slab_0'=8,'slab_1'=8] {'mode_0','mode_1'}, dimensions={0} | all-to-all | bytes 524288 | tf_op jit(solution)/shard_map/all_to_all | solution.py:411
  50.7 0.0 copy-done.3
  50.7 0.0 copy-done.4
  50.7 0.9 %gram.1 = f32[8,32,128]{2,1,0:T(8,128)S(1)} custom-call(f32[64,1024]{1,0:T(8,128)S(1)} %bitcast.17, f32[1,1024]{1,0:T(1,128)S(1)} %bitcast.20, f32[16,1024]{1,0:T(8,128)S(1)} %bitcast.18), custom_call_target="tpu_custom_call" | custom-call | tf_op jit(solution)/shard_map/gram/pallas_call | solution.py:415
  51.6 13.3 %all_to_all.21.parts = f32[8,32,128]{2,1,0:T(8,128)S(1)} all-to-all(f32[8,32,128]{2,1,0:T(8,128)S(1)} %gram.1), channel_id=1, replica_groups=mesh['mode_0'=4,'mode_1'=2,'slab_0'=8,'slab_1'=8] {'slab_1'}, dimensions={0} | all-to-all | bytes 262144 | tf_op jit(solution)/shard_map/all_to_all | solution.py:418
  65.0 19.7 %all_to_all.22.parts = f32[8,32,128]{2,1,0:T(8,128)S(1)} all-to-all(f32[8,32,128]{2,1,0:T(8,128)S(1)} %total.1), channel_id=1, replica_groups=mesh['mode_0'=4,'mode_1'=2,'slab_0'=8,'slab_1'=8] {'slab_0'}, dimensions={0} | all-to-all | bytes 262144 | tf_op jit(solution)/shard_map/all_to_all | solution.py:420
  84.6 1.8 %solve.1 = f32[64,128]{1,0:T(8,128)S(1)} custom-call(f32[8,32,128]{2,1,0:T(8,128)S(1)} %all_to_all.22.parts), custom_call_target="tpu_custom_call" | custom-call | tf_op jit(solution)/shard_map/solve/pallas_call | solution.py:421
  86.4 0.0 copy-done.5
  86.4 1.1 %convolution_add_fusion = f32[16,4,16,128]{3,0,2,1:T(8,128)S(1)} fusion(bf16[64,4,16,128]{3,2,1,0:T(8,128)(2,1)S(1)} %bitcast.21, bf16[16,4,16,128]{3,2,1,0:T(8,128)(2,1)S(1)} %copy-done.5, f32[64,128]{1,0:T(8,128)S(1)} %solve.1), kind=kOutput, calls=%fused_computation | convolution fusion | flops 100925440 | bytes 1867776 | tf_op jit(solution)/shard_map/dot_general | solution.py:432
  87.5 1.0 %copy.23 = f32[16,4,16,128]{3,2,1,0:T(8,128)} copy(f32[16,4,16,128]{3,0,2,1:T(8,128)S(1)} %convolution_add_fusion) | data formatting | bytes 1048576 | tf_op jit(solution)/shard_map/add | solution.py:433
  (7 shorter events, 0.1 us)
Async XLA Ops:
  0.0 23.4 %copy-start.1 = (f32[4,128,128]{2,1,0:T(8,128)S(1)}, f32[4,128,128]{2,1,0:T(8,128)}, u32[]{:S(2)}) copy-start(f32[4,128,128]{2,1,0:T(8,128)} %lc.3) | copy-start | bytes 786436
  0.0 23.4 %copy-start = (bf16[8,4,128,128]{3,2,1,0:T(8,128)(2,1)S(1)}, bf16[8,4,128,128]{3,2,1,0:T(8,128)(2,1)}, u32[]{:S(2)}) copy-start(bf16[8,4,128,128]{3,2,1,0:T(8,128)(2,1)} %modes.1) | copy-start | bytes 3145732
  0.0 23.5 %copy-start.2 = (f32[4,128,128]{2,1,0:T(8,128)S(1)}, f32[4,128,128]{2,1,0:T(8,128)}, u32[]{:S(2)}) copy-start(f32[4,128,128]{2,1,0:T(8,128)} %hs.1) | copy-start | bytes 786436
  1.2 17.7 %collective-permute-start.1 = (f32[392,128]{1,0:T(8,128)S(1)}, f32[392,128]{1,0:T(8,128)S(1)}, u32[]{:S(2)}, u32[]{:S(2)}) collective-permute-start(f32[392,128]{1,0:T(8,128)S(1)} %get-tuple-element.17), channel_id=1, source_target_pairs={{1,0},{2,1},{3,2},{4,3},{5,4},{6,5},{7,6},{8,7},{9,8},{10,9},{11,1... | collective-permute-start | bytes 602120 | tf_op jit(solution)/shard_map/ppermute | solution.py:360
  5.0 35.0 %all-to-all-start = ((bf16[8,8,4,16,128]{4,3,2,1,0:T(8,128)(2,1)}), bf16[8,8,4,16,128]{4,3,2,1,0:T(8,128)(2,1)S(1)}, u32[]{:S(2)}, u32[]{:S(2)}) async-start(bf16[8,8,4,16,128]{4,3,2,1,0:T(8,128)(2,1)} %copy.20), calls=%async_computation | async-start | bytes 2097152 | tf_op jit(solution)/shard_map/all_to_all | solution.py:363
  14.4 9.1 %collective-permute-start = (f32[392,128]{1,0:T(8,128)S(1)}, f32[392,128]{1,0:T(8,128)S(1)}, u32[]{:S(2)}, u32[]{:S(2)}) collective-permute-start(f32[392,128]{1,0:T(8,128)S(1)} %get-tuple-element.16), channel_id=1, source_target_pairs={{0,1},{1,2},{2,3},{3,4},{4,5},{5,6},{6,7},{7,8},{8,9},{9,10},{10,1... | collective-permute-start | bytes 602120 | tf_op jit(solution)/shard_map/ppermute | solution.py:359
  29.5 10.5 %collective-permute-start.2 = (f32[8,8,128]{2,1,0:T(8,128)S(1)}, f32[8,8,128]{2,1,0:T(8,128)S(1)}, u32[]{:S(2)}, u32[]{:S(2)}) collective-permute-start(f32[8,8,128]{2,1,0:T(8,128)S(1)} %get-tuple-element.26), channel_id=1, source_target_pairs={{1,0},{2,1},{3,2},{4,3},{5,4},{6,5},{7,6},{8,7},{9,8},{10,9},{11,1... | collective-permute-start | bytes 98312 | tf_op jit(solution)/shard_map/ppermute | solution.py:392
  30.8 9.2 %collective-permute-start.3 = (f32[8,8,128]{2,1,0:T(8,128)S(1)}, f32[8,8,128]{2,1,0:T(8,128)S(1)}, u32[]{:S(2)}, u32[]{:S(2)}) collective-permute-start(f32[8,8,128]{2,1,0:T(8,128)S(1)} %get-tuple-element.25), channel_id=1, source_target_pairs={{0,1},{1,2},{2,3},{3,4},{4,5},{5,6},{6,7},{7,8},{8,9},{9,10},{10,1... | collective-permute-start | bytes 98312 | tf_op jit(solution)/shard_map/ppermute | solution.py:393
  35.8 14.9 %copy-start.3 = (f32[1024,16]{0,1:T(8,128)S(1)}, f32[1024,16]{0,1:T(8,128)}, u32[]{:S(2)}) copy-start(f32[1024,16]{0,1:T(8,128)} %param.12) | copy-start | bytes 196612
  35.8 14.9 %copy-start.4 = (f32[1024]{0:T(1024)S(1)}, f32[1024]{0:T(1024)}, u32[]{:S(2)}) copy-start(f32[1024]{0:T(1024)} %param.11) | copy-start | bytes 12292
  35.8 50.6 %copy-start.5 = (bf16[16,4,16,128]{3,2,1,0:T(8,128)(2,1)S(1)}, bf16[16,4,16,128]{3,2,1,0:T(8,128)(2,1)}, u32[]{:S(2)}) copy-start(bf16[16,4,16,128]{3,2,1,0:T(8,128)(2,1)} %param.13) | copy-start | bytes 786436

commit v6 on v5

--- a/solution.py
+++ b/solution.py
@@ -120,12 +120,14 @@
     return (row << 10) | ((place - where) & 127)
 
 
-def pack_kernel(lc, cells, upward, downward, near, held, sems):
+def pack_kernel(lc, cells, modes, upward, downward, near, modes_near, held, sems):
     copies = [pltpu.make_async_copy(cells, held, sems.at[0])]
     for z in range(3):
         part = pl.ds(NX * z, NX)
         copies.append(pltpu.make_async_copy(lc.at[z + 1], upward.at[part], sems.at[1 + z]))
         copies.append(pltpu.make_async_copy(lc.at[z], downward.at[part], sems.at[4 + z]))
+    for k in range(LM):
+        copies.append(pltpu.make_async_copy(modes.at[k], modes_near.at[k], sems.at[7 + k]))
     for copy in copies:
         copy.start()
     copies[0].wait()
@@ -137,6 +139,15 @@
     for q in range(8):
         near[q] = spot[q : q + 1]
     for copy in copies[1:]:
+        copy.wait()
+
+
+def pieces_kernel(modes, out, held, sems):
+    copies = [pltpu.make_async_copy(held.at[d], out.at[d], sems.at[d]) for d in range(8)]
+    for d in range(8):
+        held[d] = modes[:, :, 16 * d : 16 * d + 16, :]
+        copies[d].start()
+    for copy in copies:
         copy.wait()
 
 
@@ -347,19 +358,33 @@
     back = [(i + 1, i) for i in range(slabs - 1)]
 
     message = jax.ShapeDtypeStruct((3 * NX + 8, NY), jnp.float32)
-    upward, downward, near_pick = pl.pallas_call(
+    upward, downward, near_pick, modes_near = pl.pallas_call(
         pack_kernel,
-        out_shape=(message, message, jax.ShapeDtypeStruct((8, 1, NY), jnp.int32)),
-        in_specs=[pl.BlockSpec(memory_space=pltpu.HBM)] * 2,
-        out_specs=vmem(3),
-        scratch_shapes=[pltpu.VMEM((8, NY), jnp.int32), pltpu.SemaphoreType.DMA((7,))],
-        compiler_params=limit(4),
+        out_shape=(
+            message,
+            message,
+            jax.ShapeDtypeStruct((8, 1, NY), jnp.int32),
+            jax.ShapeDtypeStruct(modes.shape, modes.dtype),
+        ),
+        in_specs=[pl.BlockSpec(memory_space=pltpu.HBM)] * 3,
+        out_specs=vmem(4),
+        scratch_shapes=[pltpu.VMEM((8, NY), jnp.int32), pltpu.SemaphoreType.DMA((7 + LM,))],
+        compiler_params=limit(6),
         name="pack",
-    )(stay(log_cond), stay(obs_cells.reshape(8, NY)))
+    )(stay(log_cond), stay(obs_cells.reshape(8, NY)), stay(modes))
     before = lax.ppermute(upward, SLAB, ahead)
     after = lax.ppermute(downward, SLAB, back)
 
-    pieces = jnp.moveaxis(modes.reshape(LM, CZ, 8, NX // 8, NY), 2, 0)
+    cut = (8, LM, CZ, NX // 8, NY)
+    pieces = pl.pallas_call(
+        pieces_kernel,
+        out_shape=jax.ShapeDtypeStruct(cut, jnp.bfloat16),
+        in_specs=vmem(1),
+        out_specs=pl.BlockSpec(memory_space=pltpu.HBM),
+        scratch_shapes=[pltpu.VMEM(cut, jnp.bfloat16), pltpu.SemaphoreType.DMA((8,))],
+        compiler_params=limit(4),
+        name="pieces",
+    )(modes_near)
     block = lax.all_to_all(pieces, MODE, 0, 0, tiled=True)
 
     place = lax.broadcasted_iota(jnp.int32, (8, NY), 1)
@@ -388,7 +413,7 @@
         ],
         compiler_params=limit(24),
         name="outer",
-    )(far_pick, log_cond, head_slope, before, after, modes)
+    )(far_pick, log_cond, head_slope, before, after, modes_near)
     from_above = lax.ppermute(share[:8], SLAB, back)
     from_below = lax.ppermute(share[8:], SLAB, ahead)
     picked = pl.pallas_call(

time: 88.8 us -> 87.7 us (0.988)
  local copies, waits for them, and re-layouts: 3.53 us -> 1.01 us
  Pallas kernels: 14 us -> 15.3 us
    transpose x1 -> x0, local copies, waits for them, and re-layouts: 2.52 us -> none  [on_device(): pieces = jnp.moveaxis(modes.reshape(LM, CZ, 8, NX // 8, NY), 2, 0)]
    pallas_call x0 -> x1, Pallas kernels: none -> 1.06 us  [on_device(): pl.pallas_call(pieces_kernel, out_shape=jax.ShapeDtypeStruct(cut, jnp.bfl...]
  transfers between devices with their start and end apart: 5 -> 5, of which waited for: 1 -> 1; matrix products, arithmetic and copies ran while one was open for 3% -> 0% of each run, Pallas kernels for 11% -> 13%
where the time goes in v6:
time: 87.7 us; the launch traced here: 87.3 us
  blocking collectives  43.7 us (50%)
  starting transfers between devices  21.5 us (25%)
  Pallas kernels  15.3 us (17%)
  waiting for transfers between devices  4.49 us (5%)
  matrix products  1.07 us (1%)
  local copies, waits for them, and re-layouts  1.01 us (1%)
    all_to_all x1, blocking collectives, on_device(): part = lax.all_to_all(part, 'slab_0', 0, 0, tiled=True)  19.8 us
    all_to_all x1, blocking collectives, on_device(): part = lax.all_to_all(part, 'slab_1', 0, 0, tiled=True)  13.3 us
    all_to_all x1, blocking collectives, on_device(): whole = lax.all_to_all(copies, MODE, 0, 0, tiled=True)  10.7 us
    all_to_all x1, starting transfers between devices, on_device(): block = lax.all_to_all(pieces, MODE, 0, 0, tiled=True)  9.36 us
    pallas_call x1, Pallas kernels, on_device(): pl.pallas_call(outer_kernel, out_shape=(jax.ShapeDtypeStruct((16, LM, NY)...  5.94 us
    ppermute x1, starting transfers between devices, on_device(): from_below = lax.ppermute(share[8:], SLAB, ahead)  5.02 us
    ppermute x1, starting transfers between devices, on_device(): before = lax.ppermute(upward, SLAB, ahead)  4.55 us
    ppermute x1, waiting for transfers between devices, on_device(): before = lax.ppermute(upward, SLAB, ahead)  4.48 us
  transfers between devices with their start and end apart: 5, of which 1 were waited for; matrix products, arithmetic and copies ran while one was open for 0% of the time, Pallas kernels for 13%

profile of v6, /device:TPU:2, one launch (start us, length us, event | category | flops | bytes accessed | tf_op | source)
XLA Modules:
  0.0 87.3 jit_solution(9120870890713520351)
XLA Ops:
  0.0 0.0 copy-start
  0.0 0.0 copy-start.1
  0.0 1.6 %pack.1 = (f32[392,128]{1,0:T(8,128)S(1)}, f32[392,128]{1,0:T(8,128)S(1)}, s32[8,1,128]{2,1,0:T(1,128)S(1)}, bf16[8,4,128,128]{3,2,1,0:T(8,128)(2,1)S(1)}) custom-call(f32[4,128,128]{2,1,0:T(8,128)} %lc.3, s32[8,128]{1,0:T(8,128)} %bitcast.18, bf16[8,4,128,128]{3,2,1,0:T(8,128)(2,1)} %modes.1), custom_call_target="tpu_custom_call" | custom-call | tf_op jit(solution)/shard_map/pack/pallas_call | solution.py:361
  1.6 1.3 %collective-permute-start.1 = (f32[392,128]{1,0:T(8,128)S(1)}, f32[392,128]{1,0:T(8,128)S(1)}, u32[]{:S(2)}, u32[]{:S(2)}) collective-permute-start(f32[392,128]{1,0:T(8,128)S(1)} %get-tuple-element.18), channel_id=1, source_target_pairs={{1,0},{2,1},{3,2},{4,3},{5,4},{6,5},{7,6},{8,7},{9,8},{10,9},{11,1... | collective-permute-start | bytes 602120 | tf_op jit(solution)/shard_map/ppermute | solution.py:376
  2.9 1.1 %pieces.1 = bf16[8,8,4,16,128]{4,3,2,1,0:T(8,128)(2,1)} custom-call(bf16[8,4,128,128]{3,2,1,0:T(8,128)(2,1)S(1)} %get-tuple-element.19.modes), custom_call_target="tpu_custom_call" | custom-call | tf_op jit(solution)/shard_map/pieces/pallas_call | solution.py:379
  4.0 9.4 %all-to-all-start = ((bf16[8,8,4,16,128]{4,3,2,1,0:T(8,128)(2,1)}), bf16[8,8,4,16,128]{4,3,2,1,0:T(8,128)(2,1)S(1)}, u32[]{:S(2)}, u32[]{:S(2)}) async-start(bf16[8,8,4,16,128]{4,3,2,1,0:T(8,128)(2,1)} %pieces.1), calls=%async_computation | async-start | bytes 2097152 | tf_op jit(solution)/shard_map/all_to_all | solution.py:388
  13.3 4.5 %collective-permute-start = (f32[392,128]{1,0:T(8,128)S(1)}, f32[392,128]{1,0:T(8,128)S(1)}, u32[]{:S(2)}, u32[]{:S(2)}) collective-permute-start(f32[392,128]{1,0:T(8,128)S(1)} %get-tuple-element.17), channel_id=1, source_target_pairs={{0,1},{1,2},{2,3},{3,4},{4,5},{5,6},{6,7},{7,8},{8,9},{9,10},{10,1... | collective-permute-start | bytes 602120 | tf_op jit(solution)/shard_map/ppermute | solution.py:375
  17.9 0.0 collective-permute-done.1.after
  17.9 4.5 %collective-permute-done.before = f32[392,128]{1,0:T(8,128)S(1)} collective-permute-done((f32[392,128]{1,0:T(8,128)S(1)}, f32[392,128]{1,0:T(8,128)S(1)}, u32[]{:S(2)}, u32[]{:S(2)}) %collective-permute-start) | collective-permute-done | bytes 200736 | tf_op jit(solution)/shard_map/ppermute | solution.py:375
  22.4 0.0 copy-done
  22.4 0.0 copy-done.1
  22.4 5.9 %outer.1 = (f32[16,8,128]{2,1,0:T(8,128)S(1)}, f32[6,8,128,128]{3,2,1,0:T(8,128)S(1)}, f32[8320,128]{1,0:T(8,128)S(1)}, f32[8320,128]{1,0:T(8,128)S(1)}) custom-call(s32[16,1,128]{2,1,0:T(1,128)S(1)} %bitcast.15, f32[4,128,128]{2,1,0:T(8,128)S(1)} %copy-done, f32[4,128,128]{2,1,0:T(8,128)S(1)} %copy-done.1, f32[392,128]{1,0:T(8,128)S(1)} %collective-permute-done.before, ...), custom_call_target="tpu_custom_call" | custom-call | tf_op jit(solution)/shard_map/outer/pallas_call | solution.py:399
  28.4 1.3 %collective-permute-start.2 = (f32[8,8,128]{2,1,0:T(8,128)S(1)}, f32[8,8,128]{2,1,0:T(8,128)S(1)}, u32[]{:S(2)}, u32[]{:S(2)}) collective-permute-start(f32[8,8,128]{2,1,0:T(8,128)S(1)} %get-tuple-element.28), channel_id=1, source_target_pairs={{1,0},{2,1},{3,2},{4,3},{5,4},{6,5},{7,6},{8,7},{9,8},{10,9},{11,1... | collective-permute-start | bytes 98312 | tf_op jit(solution)/shard_map/ppermute | solution.py:417
  29.7 5.0 %collective-permute-start.3 = (f32[8,8,128]{2,1,0:T(8,128)S(1)}, f32[8,8,128]{2,1,0:T(8,128)S(1)}, u32[]{:S(2)}, u32[]{:S(2)}) collective-permute-start(f32[8,8,128]{2,1,0:T(8,128)S(1)} %get-tuple-element.27), channel_id=1, source_target_pairs={{0,1},{1,2},{2,3},{3,4},{4,5},{5,6},{6,7},{7,8},{8,9},{9,10},{10,1... | collective-permute-start | bytes 98312 | tf_op jit(solution)/shard_map/ppermute | solution.py:418
  34.7 0.0 copy-start.2
  34.7 0.0 copy-start.3
  34.7 0.0 copy-start.4
  34.7 4.0 %inner.1 = f32[8,8,128]{2,1,0:T(8,128)S(1)} custom-call(s32[8,1,128]{2,1,0:T(1,128)S(1)} %get-tuple-element.16.near, f32[6,8,128,128]{3,2,1,0:T(8,128)S(1)} %get-tuple-element.20.coef, f32[8320,128]{1,0:T(8,128)S(1)} %get-tuple-element.21.u1, f32[8320,128]{1,0:T(8,128)S(1)} %get-tuple-element.22.u2), custom_call_target="tpu_custom_call" | custom-call | tf_op jit(solution)/shard_map/inner/pallas_call | solution.py:419
  38.8 0.0 collective-permute-done.2
  38.8 0.0 collective-permute-done.3
  38.8 0.0 all-to-all-done
  38.8 10.7 %all_to_all.20 = f32[8,8,8,128]{3,2,1,0:T(8,128)S(1)} all-to-all(f32[8,8,8,128]{3,2,1,0:T(8,128)S(1)} %broadcast_in_dim.9), channel_id=1, replica_groups=mesh['mode_0'=4,'mode_1'=2,'slab_0'=8,'slab_1'=8] {'mode_0','mode_1'}, dimensions={0} | all-to-all | bytes 524288 | tf_op jit(solution)/shard_map/all_to_all | solution.py:436
  49.5 0.0 copy-done.2
  49.5 0.0 copy-done.3
  49.5 0.9 %gram.1 = f32[8,32,128]{2,1,0:T(8,128)S(1)} custom-call(f32[64,1024]{1,0:T(8,128)S(1)} %bitcast.13, f32[1,1024]{1,0:T(1,128)S(1)} %bitcast.16, f32[16,1024]{1,0:T(8,128)S(1)} %bitcast.14), custom_call_target="tpu_custom_call" | custom-call | tf_op jit(solution)/shard_map/gram/pallas_call | solution.py:440
  50.4 13.3 %all_to_all.21.parts = f32[8,32,128]{2,1,0:T(8,128)S(1)} all-to-all(f32[8,32,128]{2,1,0:T(8,128)S(1)} %gram.1), channel_id=1, replica_groups=mesh['mode_0'=4,'mode_1'=2,'slab_0'=8,'slab_1'=8] {'slab_1'}, dimensions={0} | all-to-all | bytes 262144 | tf_op jit(solution)/shard_map/all_to_all | solution.py:443
  63.8 19.8 %all_to_all.22.parts = f32[8,32,128]{2,1,0:T(8,128)S(1)} all-to-all(f32[8,32,128]{2,1,0:T(8,128)S(1)} %total.1), channel_id=1, replica_groups=mesh['mode_0'=4,'mode_1'=2,'slab_0'=8,'slab_1'=8] {'slab_0'}, dimensions={0} | all-to-all | bytes 262144 | tf_op jit(solution)/shard_map/all_to_all | solution.py:445
  83.5 1.8 %solve.1 = f32[64,128]{1,0:T(8,128)S(1)} custom-call(f32[8,32,128]{2,1,0:T(8,128)S(1)} %all_to_all.22.parts), custom_call_target="tpu_custom_call" | custom-call | tf_op jit(solution)/shard_map/solve/pallas_call | solution.py:446
  85.3 0.0 copy-done.4
  85.3 1.1 %convolution_add_fusion = f32[16,4,16,128]{3,0,2,1:T(8,128)S(1)} fusion(bf16[64,4,16,128]{3,2,1,0:T(8,128)(2,1)S(1)} %bitcast.17, bf16[16,4,16,128]{3,2,1,0:T(8,128)(2,1)S(1)} %copy-done.4, f32[64,128]{1,0:T(8,128)S(1)} %solve.1), kind=kOutput, calls=%fused_computation | convolution fusion | flops 100925440 | bytes 1867776 | tf_op jit(solution)/shard_map/dot_general | solution.py:457
  86.4 1.0 %copy.12 = f32[16,4,16,128]{3,2,1,0:T(8,128)} copy(f32[16,4,16,128]{3,0,2,1:T(8,128)S(1)} %convolution_add_fusion) | data formatting | bytes 1048576 | tf_op jit(solution)/shard_map/add | solution.py:458
  (7 shorter events, 0.1 us)
Async XLA Ops:
  0.0 22.4 %copy-start = (f32[4,128,128]{2,1,0:T(8,128)S(1)}, f32[4,128,128]{2,1,0:T(8,128)}, u32[]{:S(2)}) copy-start(f32[4,128,128]{2,1,0:T(8,128)} %lc.3) | copy-start | bytes 786436
  0.0 22.4 %copy-start.1 = (f32[4,128,128]{2,1,0:T(8,128)S(1)}, f32[4,128,128]{2,1,0:T(8,128)}, u32[]{:S(2)}) copy-start(f32[4,128,128]{2,1,0:T(8,128)} %hs.1) | copy-start | bytes 786436
  1.6 16.3 %collective-permute-start.1 = (f32[392,128]{1,0:T(8,128)S(1)}, f32[392,128]{1,0:T(8,128)S(1)}, u32[]{:S(2)}, u32[]{:S(2)}) collective-permute-start(f32[392,128]{1,0:T(8,128)S(1)} %get-tuple-element.18), channel_id=1, source_target_pairs={{1,0},{2,1},{3,2},{4,3},{5,4},{6,5},{7,6},{8,7},{9,8},{10,9},{11,1... | collective-permute-start | bytes 602120 | tf_op jit(solution)/shard_map/ppermute | solution.py:376
  4.0 34.8 %all-to-all-start = ((bf16[8,8,4,16,128]{4,3,2,1,0:T(8,128)(2,1)}), bf16[8,8,4,16,128]{4,3,2,1,0:T(8,128)(2,1)S(1)}, u32[]{:S(2)}, u32[]{:S(2)}) async-start(bf16[8,8,4,16,128]{4,3,2,1,0:T(8,128)(2,1)} %pieces.1), calls=%async_computation | async-start | bytes 2097152 | tf_op jit(solution)/shard_map/all_to_all | solution.py:388
  13.3 9.1 %collective-permute-start = (f32[392,128]{1,0:T(8,128)S(1)}, f32[392,128]{1,0:T(8,128)S(1)}, u32[]{:S(2)}, u32[]{:S(2)}) collective-permute-start(f32[392,128]{1,0:T(8,128)S(1)} %get-tuple-element.17), channel_id=1, source_target_pairs={{0,1},{1,2},{2,3},{3,4},{4,5},{5,6},{6,7},{7,8},{8,9},{9,10},{10,1... | collective-permute-start | bytes 602120 | tf_op jit(solution)/shard_map/ppermute | solution.py:375
  28.4 10.4 %collective-permute-start.2 = (f32[8,8,128]{2,1,0:T(8,128)S(1)}, f32[8,8,128]{2,1,0:T(8,128)S(1)}, u32[]{:S(2)}, u32[]{:S(2)}) collective-permute-start(f32[8,8,128]{2,1,0:T(8,128)S(1)} %get-tuple-element.28), channel_id=1, source_target_pairs={{1,0},{2,1},{3,2},{4,3},{5,4},{6,5},{7,6},{8,7},{9,8},{10,9},{11,1... | collective-permute-start | bytes 98312 | tf_op jit(solution)/shard_map/ppermute | solution.py:417
  29.7 9.1 %collective-permute-start.3 = (f32[8,8,128]{2,1,0:T(8,128)S(1)}, f32[8,8,128]{2,1,0:T(8,128)S(1)}, u32[]{:S(2)}, u32[]{:S(2)}) collective-permute-start(f32[8,8,128]{2,1,0:T(8,128)S(1)} %get-tuple-element.27), channel_id=1, source_target_pairs={{0,1},{1,2},{2,3},{3,4},{4,5},{5,6},{6,7},{7,8},{8,9},{9,10},{10,1... | collective-permute-start | bytes 98312 | tf_op jit(solution)/shard_map/ppermute | solution.py:418
  34.7 14.8 %copy-start.2 = (f32[1024,16]{0,1:T(8,128)S(1)}, f32[1024,16]{0,1:T(8,128)}, u32[]{:S(2)}) copy-start(f32[1024,16]{0,1:T(8,128)} %param.12) | copy-start | bytes 196612
  34.7 14.8 %copy-start.3 = (f32[1024]{0:T(1024)S(1)}, f32[1024]{0:T(1024)}, u32[]{:S(2)}) copy-start(f32[1024]{0:T(1024)} %param.11) | copy-start | bytes 12292
  34.7 50.6 %copy-start.4 = (bf16[16,4,16,128]{3,2,1,0:T(8,128)(2,1)S(1)}, bf16[16,4,16,128]{3,2,1,0:T(8,128)(2,1)}, u32[]{:S(2)}) copy-start(bf16[16,4,16,128]{3,2,1,0:T(8,128)(2,1)} %param.13) | copy-start | bytes 786436

commit v7 on v6

--- a/solution.py
+++ b/solution.py
@@ -279,15 +279,16 @@
     scaled = r / var[...]
     mis = misfit[...]
     half = MODES // 2
-    none = jnp.zeros((half, OBS), jnp.float32)
-    none_f = jnp.zeros((FIELDS, OBS), jnp.float32)
-    right_a = jnp.concatenate([r, none, mis, none_f], axis=0)
-    right_b = jnp.concatenate([none, none, r[half:], none_f, mis], axis=0)
+    rest = jnp.zeros((128 - MODES - FIELDS, OBS), jnp.float32)
+    right = jnp.concatenate([r, mis, rest], axis=0)
     dims = (((1,), (1,)), ((), ()))
-    got = lax.dot_general(scaled[:half], right_a, dims, precision=HI, preferred_element_type=jnp.float32)
-    got = got + lax.dot_general(
-        scaled[half:], right_b, dims, precision=HI, preferred_element_type=jnp.float32
-    )
+    both = lax.dot_general(scaled, right, dims, precision=HI, preferred_element_type=jnp.float32)
+    top = both[:half]
+    low = both[half:]
+    lane = lax.broadcasted_iota(jnp.int32, (half, 128), 1)
+    got = jnp.where(lane < 112, pltpu.roll(top, 32, 1), pltpu.roll(low, 48, 1))
+    got = jnp.where(lane < 96, pltpu.roll(low, 32, 1), got)
+    got = jnp.where(lane < 64, top, got)
     for d in range(8):
         out[d] = got
 

time: 87.7 us -> 87.3 us (level)
  no operation moved by 1% of the time
where the time goes in v7:
time: 87.3 us; the launch traced here: 86.9 us
  blocking collectives  43.7 us (50%)
  starting transfers between devices  21.5 us (25%)
  Pallas kernels  14.9 us (17%)
  waiting for transfers between devices  4.49 us (5%)
  matrix products  1.07 us (1%)
  local copies, waits for them, and re-layouts  1.01 us (1%)
    all_to_all x1, blocking collectives, on_device(): part = lax.all_to_all(part, 'slab_0', 0, 0, tiled=True)  19.8 us
    all_to_all x1, blocking collectives, on_device(): part = lax.all_to_all(part, 'slab_1', 0, 0, tiled=True)  13.3 us
    all_to_all x1, blocking collectives, on_device(): whole = lax.all_to_all(copies, MODE, 0, 0, tiled=True)  10.7 us
    all_to_all x1, starting transfers between devices, on_device(): block = lax.all_to_all(pieces, MODE, 0, 0, tiled=True)  9.36 us
    pallas_call x1, Pallas kernels, on_device(): pl.pallas_call(outer_kernel, out_shape=(jax.ShapeDtypeStruct((16, LM, NY)...  5.94 us
    ppermute x1, starting transfers between devices, on_device(): from_below = lax.ppermute(share[8:], SLAB, ahead)  5.02 us
    ppermute x1, starting transfers between devices, on_device(): before = lax.ppermute(upward, SLAB, ahead)  4.55 us
    ppermute x1, waiting for transfers between devices, on_device(): before = lax.ppermute(upward, SLAB, ahead)  4.48 us
  transfers between devices with their start and end apart: 5, of which 1 were waited for; matrix products, arithmetic and copies ran while one was open for 0% of the time, Pallas kernels for 13%

profile of v7, /device:TPU:2, one launch (start us, length us, event | category | flops | bytes accessed | tf_op | source)
XLA Modules:
  0.0 86.9 jit_solution(2148725454441717508)
XLA Ops:
  0.0 0.0 copy-start
  0.0 0.0 copy-start.1
  0.0 1.6 %pack.1 = (f32[392,128]{1,0:T(8,128)S(1)}, f32[392,128]{1,0:T(8,128)S(1)}, s32[8,1,128]{2,1,0:T(1,128)S(1)}, bf16[8,4,128,128]{3,2,1,0:T(8,128)(2,1)S(1)}) custom-call(f32[4,128,128]{2,1,0:T(8,128)} %lc.3, s32[8,128]{1,0:T(8,128)} %bitcast.18, bf16[8,4,128,128]{3,2,1,0:T(8,128)(2,1)} %modes.1), custom_call_target="tpu_custom_call" | custom-call | tf_op jit(solution)/shard_map/pack/pallas_call | solution.py:362
  1.6 1.3 %collective-permute-start.1 = (f32[392,128]{1,0:T(8,128)S(1)}, f32[392,128]{1,0:T(8,128)S(1)}, u32[]{:S(2)}, u32[]{:S(2)}) collective-permute-start(f32[392,128]{1,0:T(8,128)S(1)} %get-tuple-element.18), channel_id=1, source_target_pairs={{1,0},{2,1},{3,2},{4,3},{5,4},{6,5},{7,6},{8,7},{9,8},{10,9},{11,1... | collective-permute-start | bytes 602120 | tf_op jit(solution)/shard_map/ppermute | solution.py:377
  2.9 1.1 %pieces.1 = bf16[8,8,4,16,128]{4,3,2,1,0:T(8,128)(2,1)} custom-call(bf16[8,4,128,128]{3,2,1,0:T(8,128)(2,1)S(1)} %get-tuple-element.19.modes), custom_call_target="tpu_custom_call" | custom-call | tf_op jit(solution)/shard_map/pieces/pallas_call | solution.py:380
  4.0 9.4 %all-to-all-start = ((bf16[8,8,4,16,128]{4,3,2,1,0:T(8,128)(2,1)}), bf16[8,8,4,16,128]{4,3,2,1,0:T(8,128)(2,1)S(1)}, u32[]{:S(2)}, u32[]{:S(2)}) async-start(bf16[8,8,4,16,128]{4,3,2,1,0:T(8,128)(2,1)} %pieces.1), calls=%async_computation | async-start | bytes 2097152 | tf_op jit(solution)/shard_map/all_to_all | solution.py:389
  13.3 4.5 %collective-permute-start = (f32[392,128]{1,0:T(8,128)S(1)}, f32[392,128]{1,0:T(8,128)S(1)}, u32[]{:S(2)}, u32[]{:S(2)}) collective-permute-start(f32[392,128]{1,0:T(8,128)S(1)} %get-tuple-element.17), channel_id=1, source_target_pairs={{0,1},{1,2},{2,3},{3,4},{4,5},{5,6},{6,7},{7,8},{8,9},{9,10},{10,1... | collective-permute-start | bytes 602120 | tf_op jit(solution)/shard_map/ppermute | solution.py:376
  17.9 0.0 collective-permute-done.1.after
  17.9 4.5 %collective-permute-done.before = f32[392,128]{1,0:T(8,128)S(1)} collective-permute-done((f32[392,128]{1,0:T(8,128)S(1)}, f32[392,128]{1,0:T(8,128)S(1)}, u32[]{:S(2)}, u32[]{:S(2)}) %collective-permute-start) | collective-permute-done | bytes 200736 | tf_op jit(solution)/shard_map/ppermute | solution.py:376
  22.4 0.0 copy-done
  22.4 0.0 copy-done.1
  22.4 5.9 %outer.1 = (f32[16,8,128]{2,1,0:T(8,128)S(1)}, f32[6,8,128,128]{3,2,1,0:T(8,128)S(1)}, f32[8320,128]{1,0:T(8,128)S(1)}, f32[8320,128]{1,0:T(8,128)S(1)}) custom-call(s32[16,1,128]{2,1,0:T(1,128)S(1)} %bitcast.15, f32[4,128,128]{2,1,0:T(8,128)S(1)} %copy-done, f32[4,128,128]{2,1,0:T(8,128)S(1)} %copy-done.1, f32[392,128]{1,0:T(8,128)S(1)} %collective-permute-done.before, ...), custom_call_target="tpu_custom_call" | custom-call | tf_op jit(solution)/shard_map/outer/pallas_call | solution.py:400
  28.4 1.3 %collective-permute-start.2 = (f32[8,8,128]{2,1,0:T(8,128)S(1)}, f32[8,8,128]{2,1,0:T(8,128)S(1)}, u32[]{:S(2)}, u32[]{:S(2)}) collective-permute-start(f32[8,8,128]{2,1,0:T(8,128)S(1)} %get-tuple-element.28), channel_id=1, source_target_pairs={{1,0},{2,1},{3,2},{4,3},{5,4},{6,5},{7,6},{8,7},{9,8},{10,9},{11,1... | collective-permute-start | bytes 98312 | tf_op jit(solution)/shard_map/ppermute | solution.py:418
  29.7 5.0 %collective-permute-start.3 = (f32[8,8,128]{2,1,0:T(8,128)S(1)}, f32[8,8,128]{2,1,0:T(8,128)S(1)}, u32[]{:S(2)}, u32[]{:S(2)}) collective-permute-start(f32[8,8,128]{2,1,0:T(8,128)S(1)} %get-tuple-element.27), channel_id=1, source_target_pairs={{0,1},{1,2},{2,3},{3,4},{4,5},{5,6},{6,7},{7,8},{8,9},{9,10},{10,1... | collective-permute-start | bytes 98312 | tf_op jit(solution)/shard_map/ppermute | solution.py:419
  34.7 0.0 copy-start.2
  34.7 0.0 copy-start.3
  34.7 0.0 copy-start.4
  34.7 4.0 %inner.1 = f32[8,8,128]{2,1,0:T(8,128)S(1)} custom-call(s32[8,1,128]{2,1,0:T(1,128)S(1)} %get-tuple-element.16.near, f32[6,8,128,128]{3,2,1,0:T(8,128)S(1)} %get-tuple-element.20.coef, f32[8320,128]{1,0:T(8,128)S(1)} %get-tuple-element.21.u1, f32[8320,128]{1,0:T(8,128)S(1)} %get-tuple-element.22.u2), custom_call_target="tpu_custom_call" | custom-call | tf_op jit(solution)/shard_map/inner/pallas_call | solution.py:420
  38.8 0.0 collective-permute-done.2
  38.8 0.0 collective-permute-done.3
  38.8 0.0 all-to-all-done
  38.8 10.7 %all_to_all.20 = f32[8,8,8,128]{3,2,1,0:T(8,128)S(1)} all-to-all(f32[8,8,8,128]{3,2,1,0:T(8,128)S(1)} %broadcast_in_dim.9), channel_id=1, replica_groups=mesh['mode_0'=4,'mode_1'=2,'slab_0'=8,'slab_1'=8] {'mode_0','mode_1'}, dimensions={0} | all-to-all | bytes 524288 | tf_op jit(solution)/shard_map/all_to_all | solution.py:437
  49.5 0.0 copy-done.2
  49.5 0.0 copy-done.3
  49.5 0.5 gram.1
  50.0 13.3 %all_to_all.21.parts = f32[8,32,128]{2,1,0:T(8,128)S(1)} all-to-all(f32[8,32,128]{2,1,0:T(8,128)S(1)} %gram.1), channel_id=1, replica_groups=mesh['mode_0'=4,'mode_1'=2,'slab_0'=8,'slab_1'=8] {'slab_1'}, dimensions={0} | all-to-all | bytes 262144 | tf_op jit(solution)/shard_map/all_to_all | solution.py:444
  63.3 19.8 %all_to_all.22.parts = f32[8,32,128]{2,1,0:T(8,128)S(1)} all-to-all(f32[8,32,128]{2,1,0:T(8,128)S(1)} %total.1), channel_id=1, replica_groups=mesh['mode_0'=4,'mode_1'=2,'slab_0'=8,'slab_1'=8] {'slab_0'}, dimensions={0} | all-to-all | bytes 262144 | tf_op jit(solution)/shard_map/all_to_all | solution.py:446
  83.1 1.8 %solve.1 = f32[64,128]{1,0:T(8,128)S(1)} custom-call(f32[8,32,128]{2,1,0:T(8,128)S(1)} %all_to_all.22.parts), custom_call_target="tpu_custom_call" | custom-call | tf_op jit(solution)/shard_map/solve/pallas_call | solution.py:447
  84.9 0.0 copy-done.4
  84.9 1.1 %convolution_add_fusion = f32[16,4,16,128]{3,0,2,1:T(8,128)S(1)} fusion(bf16[64,4,16,128]{3,2,1,0:T(8,128)(2,1)S(1)} %bitcast.17, bf16[16,4,16,128]{3,2,1,0:T(8,128)(2,1)S(1)} %copy-done.4, f32[64,128]{1,0:T(8,128)S(1)} %solve.1), kind=kOutput, calls=%fused_computation | convolution fusion | flops 100925440 | bytes 1867776 | tf_op jit(solution)/shard_map/dot_general | solution.py:458
  85.9 1.0 %copy.12 = f32[16,4,16,128]{3,2,1,0:T(8,128)} copy(f32[16,4,16,128]{3,0,2,1:T(8,128)S(1)} %convolution_add_fusion) | data formatting | bytes 1048576 | tf_op jit(solution)/shard_map/add | solution.py:459
  (7 shorter events, 0.1 us)
Async XLA Ops:
  0.0 22.4 %copy-start = (f32[4,128,128]{2,1,0:T(8,128)S(1)}, f32[4,128,128]{2,1,0:T(8,128)}, u32[]{:S(2)}) copy-start(f32[4,128,128]{2,1,0:T(8,128)} %lc.3) | copy-start | bytes 786436
  0.0 22.4 %copy-start.1 = (f32[4,128,128]{2,1,0:T(8,128)S(1)}, f32[4,128,128]{2,1,0:T(8,128)}, u32[]{:S(2)}) copy-start(f32[4,128,128]{2,1,0:T(8,128)} %hs.1) | copy-start | bytes 786436
  1.6 16.3 %collective-permute-start.1 = (f32[392,128]{1,0:T(8,128)S(1)}, f32[392,128]{1,0:T(8,128)S(1)}, u32[]{:S(2)}, u32[]{:S(2)}) collective-permute-start(f32[392,128]{1,0:T(8,128)S(1)} %get-tuple-element.18), channel_id=1, source_target_pairs={{1,0},{2,1},{3,2},{4,3},{5,4},{6,5},{7,6},{8,7},{9,8},{10,9},{11,1... | collective-permute-start | bytes 602120 | tf_op jit(solution)/shard_map/ppermute | solution.py:377
  4.0 34.8 %all-to-all-start = ((bf16[8,8,4,16,128]{4,3,2,1,0:T(8,128)(2,1)}), bf16[8,8,4,16,128]{4,3,2,1,0:T(8,128)(2,1)S(1)}, u32[]{:S(2)}, u32[]{:S(2)}) async-start(bf16[8,8,4,16,128]{4,3,2,1,0:T(8,128)(2,1)} %pieces.1), calls=%async_computation | async-start | bytes 2097152 | tf_op jit(solution)/shard_map/all_to_all | solution.py:389
  13.3 9.1 %collective-permute-start = (f32[392,128]{1,0:T(8,128)S(1)}, f32[392,128]{1,0:T(8,128)S(1)}, u32[]{:S(2)}, u32[]{:S(2)}) collective-permute-start(f32[392,128]{1,0:T(8,128)S(1)} %get-tuple-element.17), channel_id=1, source_target_pairs={{0,1},{1,2},{2,3},{3,4},{4,5},{5,6},{6,7},{7,8},{8,9},{9,10},{10,1... | collective-permute-start | bytes 602120 | tf_op jit(solution)/shard_map/ppermute | solution.py:376
  28.4 10.4 %collective-permute-start.2 = (f32[8,8,128]{2,1,0:T(8,128)S(1)}, f32[8,8,128]{2,1,0:T(8,128)S(1)}, u32[]{:S(2)}, u32[]{:S(2)}) collective-permute-start(f32[8,8,128]{2,1,0:T(8,128)S(1)} %get-tuple-element.28), channel_id=1, source_target_pairs={{1,0},{2,1},{3,2},{4,3},{5,4},{6,5},{7,6},{8,7},{9,8},{10,9},{11,1... | collective-permute-start | bytes 98312 | tf_op jit(solution)/shard_map/ppermute | solution.py:418
  29.7 9.1 %collective-permute-start.3 = (f32[8,8,128]{2,1,0:T(8,128)S(1)}, f32[8,8,128]{2,1,0:T(8,128)S(1)}, u32[]{:S(2)}, u32[]{:S(2)}) collective-permute-start(f32[8,8,128]{2,1,0:T(8,128)S(1)} %get-tuple-element.27), channel_id=1, source_target_pairs={{0,1},{1,2},{2,3},{3,4},{4,5},{5,6},{6,7},{7,8},{8,9},{9,10},{10,1... | collective-permute-start | bytes 98312 | tf_op jit(solution)/shard_map/ppermute | solution.py:419
  34.7 14.8 %copy-start.2 = (f32[1024,16]{0,1:T(8,128)S(1)}, f32[1024,16]{0,1:T(8,128)}, u32[]{:S(2)}) copy-start(f32[1024,16]{0,1:T(8,128)} %param.12) | copy-start | bytes 196612
  34.7 14.8 %copy-start.3 = (f32[1024]{0:T(1024)S(1)}, f32[1024]{0:T(1024)}, u32[]{:S(2)}) copy-start(f32[1024]{0:T(1024)} %param.11) | copy-start | bytes 12292
  34.7 50.1 %copy-start.4 = (bf16[16,4,16,128]{3,2,1,0:T(8,128)(2,1)S(1)}, bf16[16,4,16,128]{3,2,1,0:T(8,128)(2,1)}, u32[]{:S(2)}) copy-start(bf16[16,4,16,128]{3,2,1,0:T(8,128)(2,1)} %param.13) | copy-start | bytes 786436
